TPU v7x, 256 devices: a whole 4x4x8 slice. The times are simulated.
256 devices in a mesh: scen: 64 (over z, y, core), cell: 2 (over x_hi), site: 2 (over x_lo).
Axes of the slice: x: 4 (x_hi: 2, x_lo: 2; x = x_hi * 2 + x_lo), y: 4, z: 8, core: 2. Of those that a mesh axis runs over, the one named last changes fastest.
Arguments:
- demand: float32 [64, 2048], P('scen', 'cell'), may hold values from 0.1 to 10
- start_potential: float32 [64, 16384], P('scen', 'site'), may hold values from -60 to 60
- cell_feat: bfloat16 [32, 2048], P(None, ('cell', 'scen', 'site')), may hold values from -8 to 8
- site_feat: bfloat16 [32, 16384], P(None, 'site'), may hold values from -8 to 8
- weights: float32 [64], replicated, may hold values from 0.5 to 4
Outputs:
- cell_potential: float32 [64, 2048], P('scen', 'cell')
- site_potential: float32 [64, 16384], P('scen', 'site')
- log_barycenter: float32 [16384], P('site')
All inputs are finite; a program needn't handle non-finite values.
Results may differ from a plain program's by a relative error of at most 0.0003.
Values may be sent and summed in bfloat16 or wider, within the bound.
No kernel may reach another device: no remote copies, remote signals or barrier semaphores. Data moves between devices by JAX's collectives and lax.ppermute only.
A program may use at most 128 MiB of HBM per device.

v0:
```python
import math

import jax
import jax.numpy as jnp
from jax import lax
from jax.sharding import Mesh
from jax.sharding import PartitionSpec as P

ITERS = 2
SCEN = ("scen_0", "scen_1", "scen_2")
CELL_SCEN_SITE = ("cell", "scen_0", "scen_1", "scen_2", "site")


entropic_eps = 0.25


def sent_to_all(value, axis):
    copies = jnp.broadcast_to(value, (lax.axis_size(axis), *value.shape))
    return lax.all_to_all(copies, axis, split_axis=0, concat_axis=0, tiled=True)


def over_copies(value, axis):
    return sent_to_all(value, axis).sum(axis=0)


def in_order(pieces, dim):
    shape = list(pieces.shape[1:])
    shape[dim] *= pieces.shape[0]
    return jnp.moveaxis(pieces, 0, dim).reshape(shape)


def whole_of(value, axes, dim):
    far, near = axes
    leading = sent_to_all(value, far)
    pieces = jnp.swapaxes(sent_to_all(leading, near), 0, 1)
    return in_order(pieces.reshape(-1, *value.shape), dim)


def gathered_once(value, axis):
    leaves = jax.tree.leaves(value)
    order = sorted(range(len(leaves)), key=lambda k: -leaves[k].size)
    width = (1, *leaves[order[0]].shape)[-1]
    lines = [
        jnp.pad(leaves[k].reshape(-1), (0, -leaves[k].size % width)).reshape(-1, width)
        for k in order
    ]
    both, at, found = (sent_to_all(jnp.concatenate(lines), axis), 0, {})
    for k, line in zip(order, lines):
        share = both[:, at : at + len(line)].reshape(len(both), -1)
        found[k] = share[:, : leaves[k].size].reshape(-1, *leaves[k].shape)
        at += len(line)
    numbers = iter(range(len(leaves)))
    return jax.tree.map(lambda _: found[next(numbers)], value)


def collected_alike(value, axis):
    leaves, found = (jax.tree.leaves(value), {})
    for leading, a in enumerate(leaves):
        if leading not in found:
            alike = [k for k, b in enumerate(leaves) if b.dtype == a.dtype]
            got = (
                gathered_once([leaves[k] for k in alike], axis)
                if len(alike) > 1
                else [sent_to_all(a, axis)]
            )
            for k, b in zip(alike, got):
                found[k] = b
    numbers = iter(range(len(leaves)))
    return jax.tree.map(lambda _: found[next(numbers)], value)


def folded_in_pairs(pieces, combine):
    while len(jax.tree.leaves(pieces)[0]) > 1:
        pieces = jax.vmap(combine)(
            *(jax.tree.map(lambda part: part[side::2], pieces) for side in (0, 1))
        )
    return jax.tree.map(lambda part: part[0], pieces)


def combined_all(value, axis, combine):
    pieces = collected_alike(value, axis)
    return folded_in_pairs(pieces, combine)


def filled_up(lines, length):
    spare = -len(lines) % length
    return jnp.pad(lines, [(0, spare)] + [(0, 0)] * (lines.ndim - 1))


def collect(value, axis, dim):
    return in_order(sent_to_all(value, axis), dim)


def cut_along(value, dim, length):
    before, after = (value.shape[:dim], value.shape[dim + 1 :])
    return jnp.moveaxis(value.reshape(*before, length, -1, *after), dim, 0)


def sent_and_summed(value, axis, dim):
    pieces = cut_along(value, dim, lax.axis_size(axis))
    arrived = lax.all_to_all(pieces, axis, split_axis=0, concat_axis=0, tiled=True)
    return arrived.sum(axis=0)


def total_of(value, axes):
    lines = value.reshape(-1)
    padded = filled_up(lines, lax.axis_size(axes))
    whole = collect(sent_and_summed(padded, axes, 0), axes, 0)
    return lax.slice_in_dim(whole, 0, len(lines)).reshape(value.shape)


def pair_merge(earlier, later):
    new_max = jnp.maximum(earlier[0], later[0])
    new_sum = earlier[1] * jnp.exp(earlier[0] - new_max) + later[1] * jnp.exp(later[0] - new_max)
    return (new_max, new_sum)


def tile_costs(cell_cols, cell_norm, site_cols, site_norm):
    inner_prod = lax.dot_general(
        cell_cols, site_cols, (((0,), (0,)), ((), ())), preferred_element_type=jnp.float32
    )
    feature_count = cell_cols.shape[0]
    return (cell_norm[:, None] + site_norm[None, :] - 2.0 * inner_prod) / feature_count


def squares(features):
    widened = features.astype(jnp.float32)
    return jnp.sum(widened * widened, axis=0)


def fold_columns(block_max, block_sum):
    col_max = jnp.max(block_max, axis=0)
    col_sum = jnp.sum(block_sum * jnp.exp(block_max - col_max[None, :]), axis=0)
    return (col_max, col_sum)


def row_pass(cell_cols, cell_norm, site_cols, site_norm, potential):
    blk_rows = math.gcd(cell_cols.shape[1], 512)

    def row_per_block(block_idx):
        offset = block_idx * blk_rows
        cell_part = lax.dynamic_slice_in_dim(cell_cols, offset, blk_rows, 1)
        norm_part = lax.dynamic_slice_in_dim(cell_norm, offset, blk_rows, 0)
        scores = (
            potential[None, :] - tile_costs(cell_part, norm_part, site_cols, site_norm)
        ) / entropic_eps
        row_max = jnp.max(scores, axis=1)
        row_sum = jnp.sum(jnp.exp(scores - row_max[:, None]), axis=1)
        return (row_max, row_sum)

    maxima, sums_exp = lax.map(row_per_block, jnp.arange(cell_cols.shape[1] // blk_rows))
    return (maxima.reshape(-1), sums_exp.reshape(-1))


def column_pass(cell_cols, cell_norm, site_cols, site_norm, row_pot):
    blk_rows = math.gcd(cell_cols.shape[1], 512)

    def column_per_block(block_idx):
        offset = block_idx * blk_rows
        cell_part = lax.dynamic_slice_in_dim(cell_cols, offset, blk_rows, 1)
        norm_part = lax.dynamic_slice_in_dim(cell_norm, offset, blk_rows, 0)
        pot_part = lax.dynamic_slice_in_dim(row_pot, offset, blk_rows, 0)
        back_scores = (
            pot_part[:, None] - tile_costs(cell_part, norm_part, site_cols, site_norm)
        ) / entropic_eps
        block_max = jnp.max(back_scores, axis=0)
        block_sum = jnp.sum(jnp.exp(back_scores - block_max[None, :]), axis=0)
        return (block_max, block_sum)

    maxima, sums_exp = lax.map(column_per_block, jnp.arange(cell_cols.shape[1] // blk_rows))
    return fold_columns(maxima, sums_exp)


def on_device(demand, start_potential, cell_feat, site_feat, weights):
    scen_index = lax.axis_index(SCEN)
    mix_weights = weights / jnp.sum(weights)
    own_mix = lax.dynamic_slice_in_dim(mix_weights, scen_index, 1, 0)[0]
    demand_sum = over_copies(jnp.sum(demand), "cell")
    log_share = jnp.log(demand[0]) - jnp.log(demand_sum)
    cell_cols = whole_of(cell_feat, (("scen_0", "scen_1"), ("scen_2", "site")), 1)
    cell_norm = squares(cell_cols)
    site_norm = squares(site_feat)
    potential = start_potential[0]
    row_pot = log_share
    log_bary = potential
    for repeat in range(ITERS):
        maxima, sums_exp = row_pass(cell_cols, cell_norm, site_feat, site_norm, potential)
        maxima, sums_exp = combined_all((maxima, sums_exp), "site", pair_merge)
        row_pot = entropic_eps * (log_share - maxima - jnp.log(sums_exp))
        col_max, col_sum = column_pass(cell_cols, cell_norm, site_feat, site_norm, row_pot)
        col_max, col_sum = combined_all((col_max, col_sum), "cell", pair_merge)
        column_lse = col_max + jnp.log(col_sum)
        log_bary = total_of(own_mix * (potential / entropic_eps + column_lse), SCEN)
        potential = entropic_eps * (log_bary - column_lse)
    return (row_pot[None, :], potential[None, :], log_bary)


def solution(mesh):
    torus = Mesh(
        mesh.devices.reshape(8, 4, 2, mesh.shape["cell"], mesh.shape["site"]),
        ("scen_0", "scen_1", "scen_2", "cell", "site"),
    )
    placed = (P(SCEN, "cell"), P(SCEN, "site"), P(None, CELL_SCEN_SITE), P(None, "site"), P())
    return jax.shard_map(
        on_device,
        mesh=torus,
        in_specs=placed,
        out_specs=(P(SCEN, "cell"), P(SCEN, "site"), P("site")),
        check_vma=False,
    )
```

profile of v0, /device:TPU:1, one launch (start us, length us, event | category | flops | bytes accessed | tf_op | source)
XLA Modules:
  0.0 292.2 jit_solution(3732955529728155952)
XLA Ops:
  0.6 0.7 copy-done
  1.3 0.7 reshape.620
  2.0 12.0 %all-to-all-start.1 = ((bf16[32,2,128]{2,1,0:T(2,128)(2,1)}), bf16[32,2,128]{2,1,0:T(2,128)(2,1)S(1)}, u32[]{:S(2)}, u32[]{:S(2)}) async-start(bf16[32,2,128]{2,1,0:T(2,128)(2,1)} %reshape.620), calls=%async_computation.1 | async-start | bytes 32768 | tf_op jit(solution)/shard_map/all_to_all | solution.py:19
  14.1 1.3 reduce_sum.119
  15.4 7.2 %all-to-all-done.1 = bf16[32,2,128]{2,1,0:T(2,128)(2,1)S(1)} async-done(((bf16[32,2,128]{2,1,0:T(2,128)(2,1)}), bf16[32,2,128]{2,1,0:T(2,128)(2,1)S(1)}, u32[]{:S(2)}, u32[]{:S(2)}) %all-to-all-start.1) | async-done | bytes 16416 | tf_op jit(solution)/shard_map/all_to_all | solution.py:19
  22.6 1.2 broadcast_in_dim.72
  23.8 4.0 %all-to-all-start = ((f32[2,1,1]{2,1,0:T(1,128)}), f32[2,1,1]{2,1,0:T(1,128)S(1)}, u32[]{:S(2)}, u32[]{:S(2)}) async-start(f32[2,1,1]{2,1,0:T(1,128)} %broadcast_in_dim.72), calls=%async_computation | async-start | bytes 2048 | tf_op jit(solution)/shard_map/all_to_all | solution.py:19
  28.0 0.9 reshape.622
  28.9 3.0 %all-to-all-done = f32[2,1,1]{2,1,0:T(1,128)S(1)} async-done(((f32[2,1,1]{2,1,0:T(1,128)}), f32[2,1,1]{2,1,0:T(1,128)S(1)}, u32[]{:S(2)}, u32[]{:S(2)}) %all-to-all-start) | async-done | bytes 40 | tf_op jit(solution)/shard_map/all_to_all | solution.py:19
  31.9 6.8 %all-to-all-start.2 = ((bf16[4,2,4096]{2,1,0:T(2,128)(2,1)}), bf16[4,2,4096]{2,1,0:T(2,128)(2,1)S(1)}, u32[]{:S(2)}, u32[]{:S(2)}) async-start(bf16[4,2,4096]{2,1,0:T(2,128)(2,1)} %reshape.622), calls=%async_computation.2 | async-start | bytes 131072 | tf_op jit(solution)/shard_map/all_to_all | solution.py:19
  38.7 1.2 multiply_reduce_fusion
  39.9 1.3 reduce_sum.121
  41.1 0.6 reduce_sum.120
  43.2 37.5 %while.48 = (s32[]{:T(128)}, f32[2,512]{1,0:T(2,128)S(1)}, f32[2,512]{1,0:T(2,128)S(1)}, f32[1,8192]{1,0:T(1,128)}, s32[2]{0:T(128)S(1)}, /*index=5*/f32[1024]{0...) while((s32[]{:T(128)}, f32[2,512]{1,0:T(2,128)S(1)}, ...), condition=%wide.region_8.9_spmd, body=%wide.region_5.8_spmd.sunk | while | flops 306183168 | bytes 34197700 | solution.py:151
  43.2 0.6 dynamic_slice.78
  44.5 9.2 %fusion.58 = (f32[512]{0:T(512)S(1)}, f32[512,8192]{1,0:T(8,128)}) fusion(bf16[32,8192]{1,0:T(8,128)(2,1)} %get-tuple-element.747, bf16[32,1024]{1,0:T(8,128)(2,1)S(1)} %get-tuple-element.746, s32[]{:T(128)S(6)} %select_n.26, f32[8192]{0:T(1024)S(1)} %get-tuple-element.745, f32[512]{0:T(512)S(1)} %dynamic_slice.79, f32[8192]{0:T(1024)} %bitcast.281), kind=kOutput, calls=%fused_computation.81.clone.1 | convolution fusion | flops 297795072 | bytes 17403908 | tf_op jit(solution)/shard_map/while/body/eval_jaxpr/dot_general | solution.py:119
  53.7 8.1 %exponential_reduce_fusion.8 = f32[512]{0:T(512)S(1)} fusion(f32[512,8192]{1,0:T(8,128)} %get-tuple-element.679, f32[512]{0:T(512)S(1)} %get-tuple-element.678), kind=kLoop, calls=%fused_computation.clone.1 | loop fusion | flops 8388096 | bytes 16781312 | tf_op jit(solution)/shard_map/while/body/eval_jaxpr/reduce_sum | solution.py:148
  61.9 0.6 dynamic_slice.78
  63.3 9.2 %fusion.58 = (f32[512]{0:T(512)S(1)}, f32[512,8192]{1,0:T(8,128)}) fusion(bf16[32,8192]{1,0:T(8,128)(2,1)} %get-tuple-element.747, bf16[32,1024]{1,0:T(8,128)(2,1)S(1)} %get-tuple-element.746, s32[]{:T(128)S(6)} %select_n.26, f32[8192]{0:T(1024)S(1)} %get-tuple-element.745, f32[512]{0:T(512)S(1)} %dynamic_slice.79, f32[8192]{0:T(1024)} %bitcast.281), kind=kOutput, calls=%fused_computation.81.clone.1 | convolution fusion | flops 297795072 | bytes 17403908 | tf_op jit(solution)/shard_map/while/body/eval_jaxpr/dot_general | solution.py:119
  72.5 8.1 %exponential_reduce_fusion.8 = f32[512]{0:T(512)S(1)} fusion(f32[512,8192]{1,0:T(8,128)} %get-tuple-element.679, f32[512]{0:T(512)S(1)} %get-tuple-element.678), kind=kLoop, calls=%fused_computation.clone.1 | loop fusion | flops 8388096 | bytes 16781312 | tf_op jit(solution)/shard_map/while/body/eval_jaxpr/reduce_sum | solution.py:148
  80.7 0.6 broadcast_in_dim.75
  81.3 3.4 %all-to-all-start.3 = ((f32[2,2,1024]{2,1,0:T(2,128)}), f32[2,2,1024]{2,1,0:T(2,128)S(1)}, u32[]{:S(2)}, u32[]{:S(2)}) async-start(f32[2,2,1024]{2,1,0:T(2,128)} %broadcast_in_dim.75), calls=%async_computation.3 | async-start | bytes 32768 | tf_op jit(solution)/shard_map/all_to_all | solution.py:19
  84.8 2.6 all-to-all-done.3
  87.5 39.3 %while.49 = (s32[]{:T(128)}, f32[2,8192]{1,0:T(2,128)S(1)}, f32[2,8192]{1,0:T(2,128)S(1)}, s32[2]{0:T(128)S(1)}, f32[1024]{0:T(1024)S(1)}, /*index=5*/f32[1024]{...) while((s32[]{:T(128)}, f32[2,8192]{1,0:T(2,128)S(1)}, ...), condition=%wide.region_12.13_spmd, body=%wide.region_9.12_spmd.sunk | while | flops 306167808 | bytes 34386124 | solution.py:170
  87.5 0.6 dynamic_slice.81
  88.9 9.2 %fusion.60 = (f32[8192]{0:T(1024)S(1)}, f32[512,8192]{1,0:T(8,128)}) fusion(bf16[32,8192]{1,0:T(8,128)(2,1)} %get-tuple-element.786, bf16[32,1024]{1,0:T(8,128)(2,1)S(1)} %get-tuple-element.785, s32[]{:T(128)S(6)} %select_n.27, f32[8192]{0:T(1024)S(1)} %get-tuple-element.784, f32[512]{0:T(512)S(1)} %dynamic_slice.82, f32[512]{0:T(512)S(1)} %dynamic_slice.83), kind=kOutput, calls=%fused_computation.82.clone.1 | convolution fusion | flops 297787392 | bytes 17403908 | tf_op jit(solution)/shard_map/while/body/eval_jaxpr/dot_general | solution.py:119
  98.1 8.3 %exponential_reduce_fusion.9 = f32[8192]{0:T(1024)S(1)} fusion(f32[512,8192]{1,0:T(8,128)} %get-tuple-element.690, f32[8192]{0:T(1024)S(1)} %get-tuple-element.689), kind=kLoop, calls=%fused_computation.4.clone.1 | loop fusion | flops 8380416 | bytes 16842752 | tf_op jit(solution)/shard_map/while/body/eval_jaxpr/reduce_sum | solution.py:167
  107.1 0.6 dynamic_slice.81
  108.5 9.2 %fusion.60 = (f32[8192]{0:T(1024)S(1)}, f32[512,8192]{1,0:T(8,128)}) fusion(bf16[32,8192]{1,0:T(8,128)(2,1)} %get-tuple-element.786, bf16[32,1024]{1,0:T(8,128)(2,1)S(1)} %get-tuple-element.785, s32[]{:T(128)S(6)} %select_n.27, f32[8192]{0:T(1024)S(1)} %get-tuple-element.784, f32[512]{0:T(512)S(1)} %dynamic_slice.82, f32[512]{0:T(512)S(1)} %dynamic_slice.83), kind=kOutput, calls=%fused_computation.82.clone.1 | convolution fusion | flops 297787392 | bytes 17403908 | tf_op jit(solution)/shard_map/while/body/eval_jaxpr/dot_general | solution.py:119
  117.8 8.3 %exponential_reduce_fusion.9 = f32[8192]{0:T(1024)S(1)} fusion(f32[512,8192]{1,0:T(8,128)} %get-tuple-element.690, f32[8192]{0:T(1024)S(1)} %get-tuple-element.689), kind=kLoop, calls=%fused_computation.4.clone.1 | loop fusion | flops 8380416 | bytes 16842752 | tf_op jit(solution)/shard_map/while/body/eval_jaxpr/reduce_sum | solution.py:167
  127.0 0.7 broadcast_in_dim.76
  127.7 3.4 %all-to-all-start.4 = ((f32[2,2,8192]{2,1,0:T(2,128)}), f32[2,2,8192]{2,1,0:T(2,128)S(1)}, u32[]{:S(2)}, u32[]{:S(2)}) async-start(f32[2,2,8192]{2,1,0:T(2,128)} %broadcast_in_dim.76), calls=%async_computation.4 | async-start | bytes 262144 | tf_op jit(solution)/shard_map/all_to_all | solution.py:19
  131.1 0.7 broadcast_divide_fusion
  131.8 0.6 dynamic_slice.46
  132.4 3.5 %all-to-all-done.4 = f32[2,2,8192]{2,1,0:T(2,128)S(1)} async-done(((f32[2,2,8192]{2,1,0:T(2,128)}), f32[2,2,8192]{2,1,0:T(2,128)S(1)}, u32[]{:S(2)}, u32[]{:S(2)}) %all-to-all-start.4) | async-done | bytes 131104 | tf_op jit(solution)/shard_map/all_to_all | solution.py:19
  135.9 1.4 fusion.27
  137.4 6.6 %all-to-all-start.5 = ((f32[64,1,128]{2,1,0:T(1,128)}), f32[64,1,128]{2,1,0:T(1,128)S(1)}, u32[]{:S(2)}, u32[]{:S(2)}) async-start(f32[64,1,128]{2,1,0:T(1,128)} %get-tuple-element.455), calls=%async_computation.5 | async-start | bytes 65536 | tf_op jit(solution)/shard_map/all_to_all | solution.py:101
  144.0 9.4 %all-to-all-done.5 = f32[64,1,128]{2,1,0:T(1,128)S(1)} async-done(((f32[64,1,128]{2,1,0:T(1,128)}), f32[64,1,128]{2,1,0:T(1,128)S(1)}, u32[]{:S(2)}, u32[]{:S(2)}) %all-to-all-start.5) | async-done | bytes 32800 | tf_op jit(solution)/shard_map/all_to_all | solution.py:101
  153.5 0.6 broadcast_in_dim.77
  154.1 4.7 %all-to-all-start.6 = ((f32[64,1,128]{2,1,0:T(1,128)}), f32[64,1,128]{2,1,0:T(1,128)S(1)}, u32[]{:S(2)}, u32[]{:S(2)}) async-start(f32[64,1,128]{2,1,0:T(1,128)} %broadcast_in_dim.77), calls=%async_computation.6 | async-start | bytes 65536 | tf_op jit(solution)/shard_map/all_to_all | solution.py:19
  158.9 9.3 %all-to-all-done.6 = f32[64,1,128]{2,1,0:T(1,128)S(1)} async-done(((f32[64,1,128]{2,1,0:T(1,128)}), f32[64,1,128]{2,1,0:T(1,128)S(1)}, u32[]{:S(2)}, u32[]{:S(2)}) %all-to-all-start.6) | async-done | bytes 32800 | tf_op jit(solution)/shard_map/all_to_all | solution.py:19
  168.3 37.5 %while.50 = (s32[]{:T(128)}, f32[2,512]{1,0:T(2,128)S(1)}, f32[2,512]{1,0:T(2,128)S(1)}, f32[8192]{0:T(1024)S(1)}, s32[2]{0:T(128)S(1)}, /*index=5*/f32[1024]{0:...) while((s32[]{:T(128)}, f32[2,512]{1,0:T(2,128)S(1)}, ...), condition=%wide.region_19.20_spmd, body=%wide.region_16.19_spmd.sunk | while | flops 306183168 | bytes 34197700 | solution.py:151
  168.4 0.6 dynamic_slice.85
  169.7 9.2 %fusion.62 = (f32[512]{0:T(512)S(1)}, f32[512,8192]{1,0:T(8,128)}) fusion(bf16[32,8192]{1,0:T(8,128)(2,1)} %get-tuple-element.825, bf16[32,1024]{1,0:T(8,128)(2,1)S(1)} %get-tuple-element.824, s32[]{:T(128)S(6)} %select_n.28, f32[8192]{0:T(1024)S(1)} %get-tuple-element.823, f32[512]{0:T(512)S(1)} %dynamic_slice.86, f32[8192]{0:T(1024)S(1)} %get-tuple-element.820), kind=kOutput, calls=%fused_computation.83.clone.1 | convolution fusion | flops 297795072 | bytes 17403908 | tf_op jit(solution)/shard_map/while/body/eval_jaxpr/dot_general | solution.py:119
  178.9 8.1 %exponential_reduce_fusion.10 = f32[512]{0:T(512)S(1)} fusion(f32[512,8192]{1,0:T(8,128)} %get-tuple-element.701, f32[512]{0:T(512)S(1)} %get-tuple-element.700), kind=kLoop, calls=%fused_computation.8.clone.1 | loop fusion | flops 8388096 | bytes 16781312 | tf_op jit(solution)/shard_map/while/body/eval_jaxpr/reduce_sum | solution.py:148
  188.4 9.2 %fusion.62 = (f32[512]{0:T(512)S(1)}, f32[512,8192]{1,0:T(8,128)}) fusion(bf16[32,8192]{1,0:T(8,128)(2,1)} %get-tuple-element.825, bf16[32,1024]{1,0:T(8,128)(2,1)S(1)} %get-tuple-element.824, s32[]{:T(128)S(6)} %select_n.28, f32[8192]{0:T(1024)S(1)} %get-tuple-element.823, f32[512]{0:T(512)S(1)} %dynamic_slice.86, f32[8192]{0:T(1024)S(1)} %get-tuple-element.820), kind=kOutput, calls=%fused_computation.83.clone.1 | convolution fusion | flops 297795072 | bytes 17403908 | tf_op jit(solution)/shard_map/while/body/eval_jaxpr/dot_general | solution.py:119
  197.7 8.1 %exponential_reduce_fusion.10 = f32[512]{0:T(512)S(1)} fusion(f32[512,8192]{1,0:T(8,128)} %get-tuple-element.701, f32[512]{0:T(512)S(1)} %get-tuple-element.700), kind=kLoop, calls=%fused_computation.8.clone.1 | loop fusion | flops 8388096 | bytes 16781312 | tf_op jit(solution)/shard_map/while/body/eval_jaxpr/reduce_sum | solution.py:148
  205.9 0.6 broadcast_in_dim.78
  206.5 3.2 %all-to-all-start.7 = ((f32[2,2,1024]{2,1,0:T(2,128)}), f32[2,2,1024]{2,1,0:T(2,128)S(1)}, u32[]{:S(2)}, u32[]{:S(2)}) async-start(f32[2,2,1024]{2,1,0:T(2,128)} %broadcast_in_dim.78), calls=%async_computation.7 | async-start | bytes 32768 | tf_op jit(solution)/shard_map/all_to_all | solution.py:19
  209.8 2.7 all-to-all-done.7
  212.6 39.3 %while.51 = (s32[]{:T(128)}, f32[2,8192]{1,0:T(2,128)S(1)}, f32[2,8192]{1,0:T(2,128)S(1)}, s32[2]{0:T(128)S(1)}, f32[1024]{0:T(1024)S(1)}, /*index=5*/f32[1024]{...) while((s32[]{:T(128)}, f32[2,8192]{1,0:T(2,128)S(1)}, ...), condition=%wide.region_23.24_spmd, body=%wide.region_20.23_spmd.sunk | while | flops 306167808 | bytes 34386124 | solution.py:170
  214.0 9.2 %fusion.64 = (f32[8192]{0:T(1024)S(1)}, f32[512,8192]{1,0:T(8,128)}) fusion(bf16[32,8192]{1,0:T(8,128)(2,1)} %get-tuple-element.864, bf16[32,1024]{1,0:T(8,128)(2,1)S(1)} %get-tuple-element.863, s32[]{:T(128)S(6)} %select_n.29, f32[8192]{0:T(1024)S(1)} %get-tuple-element.862, f32[512]{0:T(512)S(1)} %dynamic_slice.89, f32[512]{0:T(512)S(1)} %dynamic_slice.90), kind=kOutput, calls=%fused_computation.84.clone.1 | convolution fusion | flops 297787392 | bytes 17403908 | tf_op jit(solution)/shard_map/while/body/eval_jaxpr/dot_general | solution.py:119
  223.2 8.3 %exponential_reduce_fusion.11 = f32[8192]{0:T(1024)S(1)} fusion(f32[512,8192]{1,0:T(8,128)} %get-tuple-element.712, f32[8192]{0:T(1024)S(1)} %get-tuple-element.711), kind=kLoop, calls=%fused_computation.12.clone.1 | loop fusion | flops 8380416 | bytes 16842752 | tf_op jit(solution)/shard_map/while/body/eval_jaxpr/reduce_sum | solution.py:167
  233.6 9.2 %fusion.64 = (f32[8192]{0:T(1024)S(1)}, f32[512,8192]{1,0:T(8,128)}) fusion(bf16[32,8192]{1,0:T(8,128)(2,1)} %get-tuple-element.864, bf16[32,1024]{1,0:T(8,128)(2,1)S(1)} %get-tuple-element.863, s32[]{:T(128)S(6)} %select_n.29, f32[8192]{0:T(1024)S(1)} %get-tuple-element.862, f32[512]{0:T(512)S(1)} %dynamic_slice.89, f32[512]{0:T(512)S(1)} %dynamic_slice.90), kind=kOutput, calls=%fused_computation.84.clone.1 | convolution fusion | flops 297787392 | bytes 17403908 | tf_op jit(solution)/shard_map/while/body/eval_jaxpr/dot_general | solution.py:119
  242.8 8.3 %exponential_reduce_fusion.11 = f32[8192]{0:T(1024)S(1)} fusion(f32[512,8192]{1,0:T(8,128)} %get-tuple-element.712, f32[8192]{0:T(1024)S(1)} %get-tuple-element.711), kind=kLoop, calls=%fused_computation.12.clone.1 | loop fusion | flops 8380416 | bytes 16842752 | tf_op jit(solution)/shard_map/while/body/eval_jaxpr/reduce_sum | solution.py:167
  252.2 7.2 %all_to_all.60 = f32[2,2,8192]{2,1,0:T(2,128)S(1)} all-to-all(f32[2,2,8192]{2,1,0:T(2,128)S(1)} %broadcast_in_dim.79), channel_id=1, replica_groups=mesh['scen_0'=8,'scen_1'=4,'scen_2'=2,'cell'=2,'site'=2] {'cell'}, dimensions={0} | all-to-all | bytes 262144 | tf_op jit(solution)/shard_map/all_to_all | solution.py:19
  259.4 0.8 add_multiply_fusion
  260.2 15.7 %all_to_all.61 = f32[64,1,128]{2,1,0:T(1,128)S(1)} all-to-all(f32[64,1,128]{2,1,0:T(1,128)S(1)} %add_multiply_fusion), channel_id=1, replica_groups=mesh['scen_0'=8,'scen_1'=4,'scen_2'=2,'cell'=2,'site'=2] {'scen_0','scen..., dimensions={0} | all-to-all | bytes 65536 | tf_op jit(solution)/shard_map/all_to_all | solution.py:101
  276.0 0.6 broadcast_in_dim.80
  276.6 4.7 %all-to-all-start.10 = ((f32[64,1,128]{2,1,0:T(1,128)}), f32[64,1,128]{2,1,0:T(1,128)S(1)}, u32[]{:S(2)}, u32[]{:S(2)}) async-start(f32[64,1,128]{2,1,0:T(1,128)} %broadcast_in_dim.80), calls=%async_computation.10 | async-start | bytes 65536 | tf_op jit(solution)/shard_map/all_to_all | solution.py:19
  281.3 0.6 fusion.36
  282.0 8.8 %all-to-all-done.10 = f32[64,1,128]{2,1,0:T(1,128)S(1)} async-done(((f32[64,1,128]{2,1,0:T(1,128)}), f32[64,1,128]{2,1,0:T(1,128)S(1)}, u32[]{:S(2)}, u32[]{:S(2)}) %all-to-all-start.10) | async-done | bytes 32800 | tf_op jit(solution)/shard_map/all_to_all | solution.py:19
  290.8 0.8 fusion.14
  291.6 0.6 copy.88
  (86 shorter events, 7.6 us)
Async XLA Ops:
  0.6 0.7 copy-start
  2.0 20.6 %all-to-all-start.1 = ((bf16[32,2,128]{2,1,0:T(2,128)(2,1)}), bf16[32,2,128]{2,1,0:T(2,128)(2,1)S(1)}, u32[]{:S(2)}, u32[]{:S(2)}) async-start(bf16[32,2,128]{2,1,0:T(2,128)(2,1)} %reshape.620), calls=%async_computation.1 | async-start | bytes 32768 | tf_op jit(solution)/shard_map/all_to_all | solution.py:19
  23.8 8.1 %all-to-all-start = ((f32[2,1,1]{2,1,0:T(1,128)}), f32[2,1,1]{2,1,0:T(1,128)S(1)}, u32[]{:S(2)}, u32[]{:S(2)}) async-start(f32[2,1,1]{2,1,0:T(1,128)} %broadcast_in_dim.72), calls=%async_computation | async-start | bytes 2048 | tf_op jit(solution)/shard_map/all_to_all | solution.py:19
  31.9 10.5 %all-to-all-start.2 = ((bf16[4,2,4096]{2,1,0:T(2,128)(2,1)}), bf16[4,2,4096]{2,1,0:T(2,128)(2,1)S(1)}, u32[]{:S(2)}, u32[]{:S(2)}) async-start(bf16[4,2,4096]{2,1,0:T(2,128)(2,1)} %reshape.622), calls=%async_computation.2 | async-start | bytes 131072 | tf_op jit(solution)/shard_map/all_to_all | solution.py:19
  43.2 41.6 %copy-start.2 = (f32[1,1024]{1,0:T(1,128)S(1)}, f32[1,1024]{1,0:T(1,128)}, u32[]{:S(2)}) copy-start(f32[1,1024]{1,0:T(1,128)} %param.13) | copy-start | bytes 12292
  81.3 6.0 %all-to-all-start.3 = ((f32[2,2,1024]{2,1,0:T(2,128)}), f32[2,2,1024]{2,1,0:T(2,128)S(1)}, u32[]{:S(2)}, u32[]{:S(2)}) async-start(f32[2,2,1024]{2,1,0:T(2,128)} %broadcast_in_dim.75), calls=%async_computation.3 | async-start | bytes 32768 | tf_op jit(solution)/shard_map/all_to_all | solution.py:19
  87.5 43.6 %copy-start.5 = (f32[64]{0:T(128)S(1)}, f32[64]{0:T(128)}, u32[]{:S(2)}) copy-start(f32[64]{0:T(128)} %param.17) | copy-start | bytes 772
  87.5 48.4 %copy-start.4 = (f32[1,8192]{1,0:T(1,128)S(1)}, f32[1,8192]{1,0:T(1,128)}, u32[]{:S(2)}) copy-start(f32[1,8192]{1,0:T(1,128)} %get-tuple-element.892) | copy-start | bytes 98308
  127.7 8.2 %all-to-all-start.4 = ((f32[2,2,8192]{2,1,0:T(2,128)}), f32[2,2,8192]{2,1,0:T(2,128)S(1)}, u32[]{:S(2)}, u32[]{:S(2)}) async-start(f32[2,2,8192]{2,1,0:T(2,128)} %broadcast_in_dim.76), calls=%async_computation.4 | async-start | bytes 262144 | tf_op jit(solution)/shard_map/all_to_all | solution.py:19
  137.4 16.1 %all-to-all-start.5 = ((f32[64,1,128]{2,1,0:T(1,128)}), f32[64,1,128]{2,1,0:T(1,128)S(1)}, u32[]{:S(2)}, u32[]{:S(2)}) async-start(f32[64,1,128]{2,1,0:T(1,128)} %get-tuple-element.455), calls=%async_computation.5 | async-start | bytes 65536 | tf_op jit(solution)/shard_map/all_to_all | solution.py:101
  154.1 14.2 %all-to-all-start.6 = ((f32[64,1,128]{2,1,0:T(1,128)}), f32[64,1,128]{2,1,0:T(1,128)S(1)}, u32[]{:S(2)}, u32[]{:S(2)}) async-start(f32[64,1,128]{2,1,0:T(1,128)} %broadcast_in_dim.77), calls=%async_computation.6 | async-start | bytes 65536 | tf_op jit(solution)/shard_map/all_to_all | solution.py:19
  206.5 5.9 %all-to-all-start.7 = ((f32[2,2,1024]{2,1,0:T(2,128)}), f32[2,2,1024]{2,1,0:T(2,128)S(1)}, u32[]{:S(2)}, u32[]{:S(2)}) async-start(f32[2,2,1024]{2,1,0:T(2,128)} %broadcast_in_dim.78), calls=%async_computation.7 | async-start | bytes 32768 | tf_op jit(solution)/shard_map/all_to_all | solution.py:19
  212.5 68.8 %copy-start.3 = (f32[1,1024]{1,0:T(1,128)S(1)}, f32[1,1024]{1,0:T(1,128)}, u32[]{:S(2)}) copy-start(f32[1,1024]{1,0:T(1,128)} %param.13) | copy-start | bytes 12292
  251.8 40.4 %copy-start.1 = (bf16[32,8]{0,1:T(8,128)(2,1)S(1)}, bf16[32,8]{0,1:T(8,128)(2,1)}, u32[]{:S(2)}) copy-start(bf16[32,8]{0,1:T(8,128)(2,1)} %param.15) | copy-start | bytes 1540
  276.6 14.1 %all-to-all-start.10 = ((f32[64,1,128]{2,1,0:T(1,128)}), f32[64,1,128]{2,1,0:T(1,128)S(1)}, u32[]{:S(2)}, u32[]{:S(2)}) async-start(f32[64,1,128]{2,1,0:T(1,128)} %broadcast_in_dim.80), calls=%async_computation.10 | async-start | bytes 65536 | tf_op jit(solution)/shard_map/all_to_all | solution.py:19
where the time goes:
time: 294 us; the launch traced here: 292 us
  other arithmetic  75.4 us (26%)
  matrix products  73.8 us (25%)
  starting transfers between devices  48.9 us (17%)
  waiting for transfers between devices  46.6 us (16%)
  blocking collectives  22.9 us (8%)
  local copies, waits for them, and re-layouts  17.4 us (6%)
  loops' own time  5.46 us (2%)
    dot_general x8, matrix products, tile_costs(): lax.dot_general(cell_cols, site_cols, (((0,), (0,)), ((), ())), preferred...  73.8 us
    all_to_all x8, starting transfers between devices, sent_to_all(): return lax.all_to_all(copies, axis, split_axis=0, concat_axis=0, tiled=True)  42.3 us
    all_to_all x8, waiting for transfers between devices, sent_to_all(): return lax.all_to_all(copies, axis, split_axis=0, concat_axis=0, tiled=True)  37.2 us
    reduce_sum x4, other arithmetic, column_per_block(): block_sum = jnp.sum(jnp.exp(back_scores - block_max[None, :]), axis=0)  33.2 us
    reduce_sum x4, other arithmetic, row_per_block(): row_sum = jnp.sum(jnp.exp(scores - row_max[:, None]), axis=1)  32.4 us
    all_to_all x1, blocking collectives, sent_and_summed(): lax.all_to_all(pieces, axis, split_axis=0, concat_axis=0, tiled=True)  15.7 us
    all_to_all x1, waiting for transfers between devices, sent_and_summed(): lax.all_to_all(pieces, axis, split_axis=0, concat_axis=0, tiled=True)  9.44 us
    all_to_all x1, blocking collectives, sent_to_all(): return lax.all_to_all(copies, axis, split_axis=0, concat_axis=0, tiled=True)  7.2 us
  transfers between devices with their start and end apart: 9, of which 8 were waited for; matrix products, arithmetic and copies ran while one was open for 3% of the time, Pallas kernels for 0%

commit v1 on v0

v1 whole, which is shorter than its diff:
```python
import jax
import jax.numpy as jnp
from jax import lax
from jax.experimental import pallas as pl
from jax.experimental.pallas import tpu as pltpu
from jax.sharding import Mesh
from jax.sharding import PartitionSpec as P

ITERS = 2
EPS = 0.25
SCEN = ("z", "y", "core")
CELL_ORDER = ("xh", "z", "y", "core", "xl")
ROW_GROUP = ("xh", "xl", "core")
BARY_GROUP = ("z", "y")
HOME_GROUP = ("xh", "core")
F32 = jnp.float32
BF16 = jnp.bfloat16
SAFE_NORMS = 14400.0
BLK = 256
VMEM = pl.BlockSpec(memory_space=pltpu.VMEM)
SMEM = pl.BlockSpec(memory_space=pltpu.SMEM)


def nt_dot(a, b):
    return lax.dot_general(a, b, (((1,), (1,)), ((), ())), preferred_element_type=F32)


def to_lanes(column):
    n = column.shape[0]
    on = lax.broadcasted_iota(jnp.int32, (n, n), 0) == lax.broadcasted_iota(jnp.int32, (n, n), 1)
    return jnp.sum(jnp.where(on, column, 0.0), axis=0, keepdims=True)


def build_kernel(feat_ref, site_ref, gibbs_ref, rest_ref, cells_ref, sites_ref, site_norm_ref, cell_norm_ref, safe_ref):
    n_cells, width = cells_ref.shape
    n_sites = sites_ref.shape[1]
    depth = site_ref.shape[0]
    per_row = width // depth
    scale = 2.0 / (depth * EPS)
    site = site_ref[...]
    wide = site.astype(F32)
    site_norm = jnp.sum(wide * wide, axis=0, keepdims=True)
    site_norm_ref[...] = site_norm / (depth * EPS)
    spread = (
        lax.broadcasted_iota(jnp.int32, (width, depth), 0) // per_row
        == lax.broadcasted_iota(jnp.int32, (width, depth), 1)
    )
    sites_ref[...] = jnp.dot(
        jnp.where(spread, 1.0, 0.0).astype(BF16), site, preferred_element_type=F32
    ).astype(BF16)
    feat = feat_ref[...]
    rows = lax.broadcasted_iota(jnp.int32, (BLK, width), 0)
    lanes = lax.broadcasted_iota(jnp.int32, (BLK, width), 1)
    own = rows % per_row == lanes % per_row
    ones = jnp.ones((8, width), BF16)

    def cell_block(i, largest):
        at = pl.multiple_of(i * BLK, BLK)
        pick = jnp.where(rows // per_row + i * (BLK // per_row) == lanes, 1.0, 0.0).astype(BF16)
        block = jnp.where(own, jnp.dot(pick, feat, preferred_element_type=F32), 0.0)
        cells_ref[pl.ds(at, BLK), :] = block.astype(BF16)
        square = block * block
        high = square.astype(BF16)
        low = (square - high.astype(F32)).astype(BF16)
        norm = (nt_dot(ones, high) + nt_dot(ones, low))[0:1]
        cell_norm_ref[:, pl.ds(at, BLK)] = norm / (depth * EPS)
        return jnp.maximum(largest, jnp.max(norm))

    largest = lax.fori_loop(0, n_cells // BLK, cell_block, jnp.float32(0.0))
    safe = largest * jnp.max(site_norm) <= SAFE_NORMS
    safe_ref[0, 0] = jnp.where(safe, 1, 0)

    @pl.when(safe)
    def _():
        def tile(t, _):
            i, j = t // (n_sites // 512), t % (n_sites // 512)
            at, to = pl.multiple_of(i * BLK, BLK), pl.multiple_of(j * 512, 512)
            inner = jnp.dot(
                cells_ref[pl.ds(at, BLK), :], sites_ref[:, pl.ds(to, 512)], preferred_element_type=F32
            )
            value = jnp.exp(inner * scale)
            high = value.astype(BF16)
            gibbs_ref[pl.ds(at, BLK), pl.ds(to, 512)] = high
            rest_ref[pl.ds(at, BLK), pl.ds(to, 512)] = (value - high.astype(F32)).astype(BF16)
            return 0

        lax.fori_loop(0, (n_cells // BLK) * (n_sites // 512), tile, 0)


def build(feat, site_feat, quarter, n_sites):
    width = feat.shape[1]
    depth = site_feat.shape[0]
    n_cells = feat.shape[0] * (width // depth)
    return pl.pallas_call(
        build_kernel,
        out_shape=(
            jax.ShapeDtypeStruct((n_cells, n_sites), BF16),
            jax.ShapeDtypeStruct((n_cells, n_sites), BF16),
            jax.ShapeDtypeStruct((n_cells, width), BF16),
            jax.ShapeDtypeStruct((width, n_sites), BF16),
            jax.ShapeDtypeStruct((1, n_sites), F32),
            jax.ShapeDtypeStruct((1, n_cells), F32),
            jax.ShapeDtypeStruct((1, 1), jnp.int32),
        ),
        in_specs=[VMEM, VMEM],
        out_specs=(VMEM, VMEM, VMEM, VMEM, VMEM, VMEM, SMEM),
        compiler_params=pltpu.CompilerParams(vmem_limit_bytes=40 << 20),
        name="build",
    )(feat, lax.dynamic_slice_in_dim(site_feat, quarter * n_sites, n_sites, 1))


def two_parts(factor):
    high = factor.astype(BF16).astype(F32)
    rest = jnp.zeros((4, factor.shape[1]), F32)
    return jnp.concatenate([high, factor - high, rest], axis=0).astype(BF16)


def log_sums(safe, level, gibbs_ref, rest_ref, cells_ref, sites_ref, out_ref, over_sites):
    n_out = out_ref.shape[1]
    scale = 2.0 / ((cells_ref.shape[1] // 8) * EPS)

    @pl.when(safe)
    def _():
        top = jnp.max(level, axis=1, keepdims=True)
        parts = two_parts(jnp.exp(level - top))

        def block(i, _):
            at = pl.multiple_of(i * BLK, BLK)
            if over_sites:
                total = nt_dot(parts, gibbs_ref[pl.ds(at, BLK), :])
                more = nt_dot(parts, rest_ref[pl.ds(at, BLK), :])
            else:
                total = jnp.dot(parts, gibbs_ref[:, pl.ds(at, BLK)], preferred_element_type=F32)
                more = jnp.dot(parts, rest_ref[:, pl.ds(at, BLK)], preferred_element_type=F32)
            out_ref[:, pl.ds(at, BLK)] = top + jnp.log(total[0:2] + (total[2:4] + more[0:2]))
            return 0

        lax.fori_loop(0, n_out // BLK, block, 0)

    @pl.when(jnp.logical_not(safe))
    def _():
        def block(i, _):
            at = pl.multiple_of(i * 128, 128)
            if over_sites:
                inner = jnp.dot(cells_ref[pl.ds(at, 128), :], sites_ref[...], preferred_element_type=F32)
            else:
                inner = lax.dot_general(
                    sites_ref[:, pl.ds(at, 128)],
                    cells_ref[...],
                    (((0,), (1,)), ((), ())),
                    preferred_element_type=F32,
                )
            for s in range(2):
                score = inner * scale + level[s : s + 1]
                top = jnp.max(score, axis=1, keepdims=True)
                total = jnp.sum(jnp.exp(score - top), axis=1, keepdims=True)
                out_ref[s : s + 1, pl.ds(at, 128)] = to_lanes(top + jnp.log(total))
            return 0

        lax.fori_loop(0, n_out // 128, block, 0)


def send_rows(sums_ref, out_ref):
    half = sums_ref.shape[1]
    for s in range(2):
        out_ref[:, s * half : (s + 1) * half] = jnp.broadcast_to(sums_ref[s : s + 1], (out_ref.shape[0], half))


def first_row_kernel(safe_ref, home_ref, site_norm_ref, gibbs_ref, rest_ref, cells_ref, sites_ref, send_ref, level_ref, sums_ref):
    n_demand = home_ref.shape[1] - site_norm_ref.shape[1]
    level = home_ref[0:2, n_demand:] * (1.0 / EPS) - site_norm_ref[...]
    level_ref[...] = level
    log_sums(safe_ref[0, 0] == 1, level, gibbs_ref, rest_ref, cells_ref, sites_ref, sums_ref, True)
    send_rows(sums_ref, send_ref)


def next_row_kernel(safe_ref, terms_ref, column_ref, gibbs_ref, rest_ref, cells_ref, sites_ref, send_ref, level_ref, sums_ref):
    level = jnp.sum(terms_ref[...], axis=0, keepdims=True) - column_ref[...]
    level_ref[...] = level
    log_sums(safe_ref[0, 0] == 1, level, gibbs_ref, rest_ref, cells_ref, sites_ref, sums_ref, True)
    send_rows(sums_ref, send_ref)


def column_kernel(
    safe_ref, pair_ref, weight_ref, home_ref, got_ref, cell_norm_ref, level_ref, gibbs_ref, rest_ref, cells_ref, sites_ref,
    send_ref, column_ref, row_pot_ref,
):
    n_cells = cell_norm_ref.shape[1]
    half = n_cells // 2
    home = home_ref[...]
    demand = jnp.concatenate([home[0:2, :half], home[2:4, :half]], axis=1)
    log_share = jnp.log(demand) - jnp.log(jnp.sum(demand, axis=1, keepdims=True))
    got = got_ref[...]
    top = jnp.max(got, axis=0, keepdims=True)
    row = top + jnp.log(jnp.sum(jnp.exp(got - top), axis=0, keepdims=True))
    down = log_share - jnp.concatenate([row[:, :n_cells], row[:, n_cells:]], axis=0)
    row_pot_ref[...] = EPS * (down + cell_norm_ref[...])
    log_sums(safe_ref[0, 0] == 1, down, gibbs_ref, rest_ref, cells_ref, sites_ref, column_ref, False)
    weight = weight_ref[...]
    which = lax.broadcasted_iota(jnp.int32, weight.shape, 1)
    term = jnp.zeros((1, level_ref.shape[1]), F32)
    for s in range(2):
        own = jnp.sum(jnp.where(which == 2 * pair_ref[0] + s, weight, 0.0), axis=1, keepdims=True)
        term += own / jnp.sum(weight, axis=1, keepdims=True) * (level_ref[s : s + 1] + column_ref[s : s + 1])
    send_ref[...] = jnp.broadcast_to(term, send_ref.shape)


def last_kernel(terms_ref, column_ref, site_norm_ref, send_ref):
    n_sites = site_norm_ref.shape[1]
    log_bary = jnp.sum(terms_ref[...], axis=0, keepdims=True)
    potential = EPS * (log_bary - column_ref[...] + site_norm_ref[...])
    send_ref[:, :n_sites] = jnp.concatenate([potential, potential], axis=0)
    send_ref[:, n_sites:] = jnp.broadcast_to(log_bary, (4, n_sites))


def call(kernel, outs, *args, scratch=()):
    return pl.pallas_call(
        kernel,
        out_shape=tuple(jax.ShapeDtypeStruct(s, F32) for s in outs),
        in_specs=[SMEM if a.dtype == jnp.int32 else VMEM for a in args],
        out_specs=(VMEM,) * len(outs),
        scratch_shapes=[pltpu.VMEM(s, F32) for s in scratch],
        compiler_params=pltpu.CompilerParams(vmem_limit_bytes=40 << 20),
        name=kernel.__name__,
    )(*args)


def exchange(value, axes):
    return lax.all_to_all(value, axes, split_axis=0, concat_axis=0, tiled=True)


def on_device(demand, start_potential, cell_feat, site_feat, weights):
    n_home = lax.axis_size(HOME_GROUP)
    n_row = lax.axis_size(ROW_GROUP)
    n_bary = lax.axis_size(BARY_GROUP)
    n_sites = start_potential.shape[1] // n_home
    n_cells = demand.shape[1] * 2
    quarter = lax.axis_index(HOME_GROUP)
    pair = lax.axis_index(BARY_GROUP).astype(jnp.int32).reshape(1)
    core, xh = lax.axis_index("core"), lax.axis_index("xh")

    packed = cell_feat.reshape(1, -1)
    feat = exchange(jnp.broadcast_to(packed, (lax.axis_size(CELL_ORDER), packed.shape[1])), CELL_ORDER)
    home = exchange(
        jnp.concatenate(
            [jnp.broadcast_to(demand, (n_home, demand.shape[1])), start_potential.reshape(n_home, n_sites)], axis=1
        ),
        HOME_GROUP,
    )
    gibbs, rest, cells, sites, site_norm, cell_norm, safe = build(feat, site_feat, quarter, n_sites)
    weight = weights.reshape(1, -1)
    sums = [(2, n_cells)]
    send, level = call(
        first_row_kernel, [(n_row, 2 * n_cells), (2, n_sites)], safe, home, site_norm, gibbs, rest, cells, sites, scratch=sums
    )
    for repeat in range(ITERS):
        got = exchange(send, ROW_GROUP)
        send, column, row_pot = call(
            column_kernel, [(n_bary, n_sites), (2, n_sites), (2, n_cells)],
            safe, pair, weight, home, got, cell_norm, level, gibbs, rest, cells, sites,
        )
        terms = exchange(send, BARY_GROUP)
        if repeat < ITERS - 1:
            send, level = call(
                next_row_kernel, [(n_row, 2 * n_cells), (2, n_sites)], safe, terms, column, gibbs, rest, cells, sites, scratch=sums
            )
    (send,) = call(last_kernel, [(n_home, 2 * n_sites)], terms, column, site_norm)
    both = exchange(send, HOME_GROUP)
    own_pot = lax.dynamic_slice(row_pot, (core, xh * demand.shape[1]), demand.shape)
    return own_pot, both[:, :n_sites].reshape(1, -1), both[:, n_sites:].reshape(-1)


def solution(mesh):
    torus = Mesh(
        mesh.devices.reshape(8, 4, 2, mesh.shape["cell"], mesh.shape["site"]), ("z", "y", "core", "xh", "xl")
    )
    return jax.shard_map(
        on_device,
        mesh=torus,
        in_specs=(P(SCEN, "xh"), P(SCEN, "xl"), P(None, CELL_ORDER), P(None, "xl"), P()),
        out_specs=(P(SCEN, "xh"), P(SCEN, "xl"), P("xl")),
        check_vma=False,
    )
```

time: 294 us -> 190 us (0.65)
  Pallas kernels: 0 us -> 81.3 us
  matrix products: 73.8 us -> 0 us
  other arithmetic: 75.4 us -> 2.9 us
  waiting for transfers between devices: 46.6 us -> 23.3 us
  starting transfers between devices: 48.9 us -> 28.8 us
  blocking collectives: 22.9 us -> 39.6 us
  loops' own time: 5.46 us -> 0 us
  local copies, waits for them, and re-layouts: 17.4 us -> 12 us
    pallas_call x0 -> x6, Pallas kernels: none -> 81.3 us  [the longest x5 73.9 us: call(): pl.pallas_call(kernel, out_shape=tuple((jax.ShapeDtypeStruct(s, F32) for...]
    dot_general x8 -> x0, matrix products: 73.8 us -> none  [tile_costs(): lax.dot_general(cell_cols, site_cols, (((0,), (0,)), ((), ())), preferred...]
    reduce_sum x17 -> x0, other arithmetic: 70.6 us -> none  [the longest x4 33.2 us: column_per_block(): block_sum = jnp.sum(jnp.exp(back_scores - block_max[None, :]), axis=0)]
    all_to_all x9 -> x4, waiting for transfers between devices: 46.6 us -> 23.3 us  [exchange(): return lax.all_to_all(value, axes, split_axis=0, concat_axis=0, tiled=True)]
    all_to_all x9 -> x4, starting transfers between devices: 48.9 us -> 28.8 us  [exchange(): return lax.all_to_all(value, axes, split_axis=0, concat_axis=0, tiled=True)]
    all_to_all x2 -> x3, blocking collectives: 22.9 us -> 39.6 us  [exchange(): return lax.all_to_all(value, axes, split_axis=0, concat_axis=0, tiled=True)]
    dynamic_slice x21 -> x2, local copies, waits for them, and re-layouts: 6.19 us -> 0.69 us  [the longest x1 0.67 us: on_device(): lax.dynamic_slice(row_pot, (core, xh * demand.shape[1]), demand.shape)]
    another operation x4 -> x0, loops' own time: 5.46 us -> none  [the longest x2 2.78 us: column_pass(): lax.map(column_per_block, jnp.arange(cell_cols.shape[1] // blk_rows))]
  transfers between devices with their start and end apart: 9 -> 4, of which waited for: 8 -> 4; matrix products, arithmetic and copies ran while one was open for 3% -> 2% of each run, Pallas kernels for 0% -> 0%
where the time goes in v1:
time: 190 us; the launch traced here: 189 us
  Pallas kernels  81.3 us (43%)
  blocking collectives  39.6 us (21%)
  starting transfers between devices  28.8 us (15%)
  waiting for transfers between devices  23.3 us (12%)
  local copies, waits for them, and re-layouts  12 us (6%)
  other arithmetic  2.9 us (2%)
    pallas_call x5, Pallas kernels, call(): pl.pallas_call(kernel, out_shape=tuple((jax.ShapeDtypeStruct(s, F32) for...  73.9 us
    all_to_all x3, blocking collectives, exchange(): return lax.all_to_all(value, axes, split_axis=0, concat_axis=0, tiled=True)  39.6 us
    all_to_all x4, starting transfers between devices, exchange(): return lax.all_to_all(value, axes, split_axis=0, concat_axis=0, tiled=True)  28.8 us
    all_to_all x4, waiting for transfers between devices, exchange(): return lax.all_to_all(value, axes, split_axis=0, concat_axis=0, tiled=True)  23.3 us
    pallas_call x1, Pallas kernels, build(): pl.pallas_call(build_kernel, out_shape=(jax.ShapeDtypeStruct((n_cells, n_...  7.39 us
    unnamed x22, local copies, waits for them, and re-layouts  7.08 us
  transfers between devices with their start and end apart: 4, of which 4 were waited for; matrix products, arithmetic and copies ran while one was open for 2% of the time, Pallas kernels for 0%

profile of v1, /device:TPU:1, one launch (start us, length us, event | category | flops | bytes accessed | tf_op | source)
XLA Modules:
  0.0 188.8 jit_solution(14253913359313983221)
XLA Ops:
  0.6 0.0 copy-start
  0.6 0.5 broadcast.8
  1.2 1.5 reduce.3
  2.7 0.7 pad.clone
  3.4 0.6 all_to_all.50
  4.0 6.4 %all-to-all-start.1 = ((f32[4,1,3072]{2,1,0:T(1,128)}), f32[4,1,3072]{2,1,0:T(1,128)S(1)}, u32[]{:S(2)}, u32[]{:S(2)}) async-start(f32[4,1,3072]{2,1,0:T(1,128)} %all_to_all.50), calls=%async_computation.1 | async-start | bytes 98304 | tf_op jit(solution)/shard_map/all_to_all | solution.py:229
  10.5 0.8 copy.15
  11.2 0.1 broadcast_in_dim.14
  11.3 0.1 broadcast_in_dim.15
  11.5 0.5 broadcast.9
  12.0 1.4 reduce.4
  13.4 0.7 reshape.57
  14.1 1.1 all-to-all-done.1
  15.2 12.9 %all-to-all-start = ((bf16[256,2,128]{2,1,0:T(2,128)(2,1)}), bf16[256,2,128]{2,1,0:T(2,128)(2,1)S(1)}, u32[]{:S(2)}, u32[]{:S(2)}) async-start(bf16[256,2,128]{2,1,0:T(2,128)(2,1)} %reshape.57), calls=%async_computation | async-start | bytes 262144 | tf_op jit(solution)/shard_map/all_to_all | solution.py:229
  28.1 0.0 copy-done
  28.2 12.8 %all-to-all-done = bf16[256,2,128]{2,1,0:T(2,128)(2,1)S(1)} async-done(((bf16[256,2,128]{2,1,0:T(2,128)(2,1)}), bf16[256,2,128]{2,1,0:T(2,128)(2,1)S(1)}, u32[]{:S(2)}, u32[]{:S(2)}) %all-to-all-start) | async-done | bytes 131104 | tf_op jit(solution)/shard_map/all_to_all | solution.py:229
  41.1 7.4 %build.1 = (bf16[2048,2048]{1,0:T(8,128)(2,1)S(1)}, bf16[2048,2048]{1,0:T(8,128)(2,1)}, bf16[2048,256]{1,0:T(8,128)(2,1)S(1)}, bf16[256,2048]{1,0:T(8,128)(2,1)S...) custom-call(bf16[256,256]{1,0:T(8,128)(2,1)S(1)} %bitcast.43, ...), custom_call_target="tpu_custom_call" | custom-call | tf_op jit(solution)/shard_map/build/pallas_call | solution.py:94
  48.5 0.0 copy-start.1
  48.5 0.0 copy-start.3
  48.5 18.8 %first_row_kernel.1 = (f32[8,4096]{1,0:T(8,128)S(1)}, f32[2,2048]{1,0:T(2,128)S(1)}) custom-call(s32[1,1]{1,0:T(1,128)} %get-tuple-element.19.safe_ref, f32[4,3072]{1,0:T(4,128)S(1)} %bitcast.38, f32[1,2048]{1,0:T(1,128)S(1)} %get-tuple-element.20.site_norm_ref, bf16[2048,2048]{1,0:T(8,128)(2,1)S(1)} %get-tuple-element.21.gibbs_ref, ...), custom_call_target="tpu_custom_call" | custom-call | tf_op jit(solution)/shard_map/first_row_kernel/pallas_call | solution.py:217
  67.3 0.0 copy-done.1
  67.3 0.8 copy.16
  68.1 3.8 %all-to-all-start.2 = ((f32[8,1,4096]{2,1,0:T(1,128)}), f32[8,1,4096]{2,1,0:T(1,128)S(1)}, u32[]{:S(2)}, u32[]{:S(2)}) async-start(f32[8,1,4096]{2,1,0:T(1,128)} %copy.16), calls=%async_computation.2 | async-start | bytes 262144 | tf_op jit(solution)/shard_map/all_to_all | solution.py:229
  71.8 5.3 %all-to-all-done.2 = f32[8,1,4096]{2,1,0:T(1,128)S(1)} async-done(((f32[8,1,4096]{2,1,0:T(1,128)}), f32[8,1,4096]{2,1,0:T(1,128)S(1)}, u32[]{:S(2)}, u32[]{:S(2)}) %all-to-all-start.2) | async-done | bytes 131104 | tf_op jit(solution)/shard_map/all_to_all | solution.py:229
  77.1 0.1 copy.40
  77.2 0.0 copy-done.3
  77.2 0.0 copy-start.2
  77.2 3.4 %copy-done.2 = bf16[2048,2048]{1,0:T(8,128)(2,1)S(1)} copy-done((bf16[2048,2048]{1,0:T(8,128)(2,1)S(1)}, bf16[2048,2048]{1,0:T(8,128)(2,1)}, u32[]{:S(2)}) %copy-start.2) | copy-done | bytes 8388632
  80.6 19.6 %column_kernel.2 = (f32[32,2048]{1,0:T(8,128)S(1)}, f32[2,2048]{1,0:T(2,128)S(1)}, f32[2,2048]{1,0:T(2,128)}) custom-call(s32[1,1]{1,0:T(1,128)} %get-tuple-element.19.safe_ref, s32[1]{0:T(128)} %bitcast.pair_ref, f32[1,64]{1,0:T(1,128)S(1)} %bitcast.49, f32[4,3072]{1,0:T(4,128)S(1)} %bitcast.39, f32[8,4096]{1,0:T(8,128)S(1)} %bitcast.42, ...), custom_call_target="tpu_custom_call" | custom-call | tf_op jit(solution)/shard_map/column_kernel/pallas_call | solution.py:217
  100.2 0.3 copy.17
  100.5 14.6 %all_to_all.75 = f32[32,1,2048]{2,1,0:T(1,128)S(1)} all-to-all(f32[32,1,2048]{2,1,0:T(1,128)S(1)} %copy.17), channel_id=1, replica_groups=mesh['z'=8,'y'=4,'core'=2,'xh'=2,'xl'=2] {'z','y'}, dimensions={0} | all-to-all | bytes 524288 | tf_op jit(solution)/shard_map/all_to_all | solution.py:229
  115.1 0.1 copy.38
  115.2 16.4 %next_row_kernel.1 = (f32[8,4096]{1,0:T(8,128)S(1)}, f32[2,2048]{1,0:T(2,128)S(1)}) custom-call(s32[1,1]{1,0:T(1,128)} %get-tuple-element.19.safe_ref, f32[32,2048]{1,0:T(8,128)S(1)} %bitcast.36, f32[2,2048]{1,0:T(2,128)S(1)} %get-tuple-element.29.column_ref, bf16[2048,2048]{1,0:T(8,128)(2,1)S(1)} %copy-done.2, ...), custom_call_target="tpu_custom_call" | custom-call | tf_op jit(solution)/shard_map/next_row_kernel/pallas_call | solution.py:217
  131.6 0.1 copy.18
  131.7 10.1 %all_to_all.76 = f32[8,1,4096]{2,1,0:T(1,128)S(1)} all-to-all(f32[8,1,4096]{2,1,0:T(1,128)S(1)} %copy.18), channel_id=1, replica_groups=mesh['z'=8,'y'=4,'core'=2,'xh'=2,'xl'=2] {'xh','xl','core'}, dimensions={0} | all-to-all | bytes 262144 | tf_op jit(solution)/shard_map/all_to_all | solution.py:229
  141.8 0.1 copy.39
  141.9 19.1 %column_kernel.3 = (f32[32,2048]{1,0:T(8,128)S(1)}, f32[2,2048]{1,0:T(2,128)S(1)}, f32[2,2048]{1,0:T(2,128)S(1)}) custom-call(s32[1,1]{1,0:T(1,128)} %get-tuple-element.19.safe_ref, s32[1]{0:T(128)} %bitcast.pair_ref, f32[1,64]{1,0:T(1,128)S(1)} %bitcast.50, f32[4,3072]{1,0:T(4,128)S(1)} %bitcast.40, f32[8,4096]{1,0:T(8,128)S(1)} %bitcast.41, ...), custom_call_target="tpu_custom_call" | custom-call | tf_op jit(solution)/shard_map/column_kernel/pallas_call | solution.py:217
  161.0 0.3 copy.19
  161.3 14.8 %all_to_all.77 = f32[32,1,2048]{2,1,0:T(1,128)S(1)} all-to-all(f32[32,1,2048]{2,1,0:T(1,128)S(1)} %copy.19), channel_id=1, replica_groups=mesh['z'=8,'y'=4,'core'=2,'xh'=2,'xl'=2] {'z','y'}, dimensions={0} | all-to-all | bytes 524288 | tf_op jit(solution)/shard_map/all_to_all | solution.py:229
  176.1 0.1 copy.37
  176.3 0.7 copy.20
  177.0 5.7 %all-to-all-start.6 = ((f32[4,1,4096]{2,1,0:T(1,128)}), f32[4,1,4096]{2,1,0:T(1,128)S(1)}, u32[]{:S(2)}, u32[]{:S(2)}) async-start(f32[4,1,4096]{2,1,0:T(1,128)} %copy.20), calls=%async_computation.6 | async-start | bytes 131072 | tf_op jit(solution)/shard_map/all_to_all | solution.py:229
  182.7 0.7 dynamic_slice.7
  183.3 4.1 %all-to-all-done.6 = f32[4,1,4096]{2,1,0:T(1,128)S(1)} async-done(((f32[4,1,4096]{2,1,0:T(1,128)}), f32[4,1,4096]{2,1,0:T(1,128)S(1)}, u32[]{:S(2)}, u32[]{:S(2)}) %all-to-all-start.6) | async-done | bytes 65568 | tf_op jit(solution)/shard_map/all_to_all | solution.py:229
  187.5 0.6 copy.29
  188.1 0.6 copy.28
  (9 shorter events, 0.2 us)
Async XLA Ops:
  0.6 27.5 %copy-start = (bf16[32,8192]{1,0:T(8,128)(2,1)S(1)}, bf16[32,8192]{1,0:T(8,128)(2,1)}, u32[]{:S(2)}) copy-start(bf16[32,8192]{1,0:T(8,128)(2,1)} %param.8) | copy-start | bytes 1572868
  4.0 11.2 %all-to-all-start.1 = ((f32[4,1,3072]{2,1,0:T(1,128)}), f32[4,1,3072]{2,1,0:T(1,128)S(1)}, u32[]{:S(2)}, u32[]{:S(2)}) async-start(f32[4,1,3072]{2,1,0:T(1,128)} %all_to_all.50), calls=%async_computation.1 | async-start | bytes 98304 | tf_op jit(solution)/shard_map/all_to_all | solution.py:229
  15.2 25.8 %all-to-all-start = ((bf16[256,2,128]{2,1,0:T(2,128)(2,1)}), bf16[256,2,128]{2,1,0:T(2,128)(2,1)S(1)}, u32[]{:S(2)}, u32[]{:S(2)}) async-start(bf16[256,2,128]{2,1,0:T(2,128)(2,1)} %reshape.57), calls=%async_computation | async-start | bytes 262144 | tf_op jit(solution)/shard_map/all_to_all | solution.py:229
  48.5 18.8 %copy-start.1 = (bf16[2048,2048]{1,0:T(8,128)(2,1)}, bf16[2048,2048]{1,0:T(8,128)(2,1)S(1)}, u32[]{:S(2)}) copy-start(bf16[2048,2048]{1,0:T(8,128)(2,1)S(1)} %get-tuple-element.21.gibbs_ref) | copy-start | bytes 25165828
  48.5 28.7 %copy-start.3 = (f32[64]{0:T(128)S(1)}, f32[64]{0:T(128)}, u32[]{:S(2)}) copy-start(f32[64]{0:T(128)} %param.9) | copy-start | bytes 772
  68.1 9.0 %all-to-all-start.2 = ((f32[8,1,4096]{2,1,0:T(1,128)}), f32[8,1,4096]{2,1,0:T(1,128)S(1)}, u32[]{:S(2)}, u32[]{:S(2)}) async-start(f32[8,1,4096]{2,1,0:T(1,128)} %copy.16), calls=%async_computation.2 | async-start | bytes 262144 | tf_op jit(solution)/shard_map/all_to_all | solution.py:229
  77.2 3.4 %copy-start.2 = (bf16[2048,2048]{1,0:T(8,128)(2,1)S(1)}, bf16[2048,2048]{1,0:T(8,128)(2,1)}, u32[]{:S(2)}) copy-start(bf16[2048,2048]{1,0:T(8,128)(2,1)} %copy-done.1) | copy-start | bytes 25165828
  177.0 10.5 %all-to-all-start.6 = ((f32[4,1,4096]{2,1,0:T(1,128)}), f32[4,1,4096]{2,1,0:T(1,128)S(1)}, u32[]{:S(2)}, u32[]{:S(2)}) async-start(f32[4,1,4096]{2,1,0:T(1,128)} %copy.20), calls=%async_computation.6 | async-start | bytes 131072 | tf_op jit(solution)/shard_map/all_to_all | solution.py:229

commit v2 on v1

v2 whole, which is shorter than its diff:
```python
import math

import jax
import jax.numpy as jnp
from jax import lax
from jax.experimental import pallas as pl
from jax.experimental.pallas import tpu as pltpu
from jax.sharding import Mesh
from jax.sharding import PartitionSpec as P

ITERS = 2
EPS = 0.25
SCEN = ("z", "y", "core")
CELL_ORDER = ("xh", "z", "y", "core", "xl")
ROW_GROUP = ("xh", "xl", "core")
BARY_GROUP = ("z", "y")
HOME_GROUP = ("xh", "core")
F32 = jnp.float32
BF16 = jnp.bfloat16
SAFE_NORMS = 14400.0
LANE = 128
VMEM = pl.BlockSpec(memory_space=pltpu.VMEM)
SMEM = pl.BlockSpec(memory_space=pltpu.SMEM)


def nt_dot(a, b):
    return lax.dot_general(a, b, (((1,), (1,)), ((), ())), preferred_element_type=F32)


def diagonal():
    shape = (LANE, LANE)
    return lax.broadcasted_iota(jnp.int32, shape, 0) == lax.broadcasted_iota(jnp.int32, shape, 1)


def to_row(column):
    return jnp.sum(jnp.where(diagonal(), column, 0.0), axis=0, keepdims=True)


def to_column(row):
    return jnp.sum(jnp.where(diagonal(), row, 0.0), axis=1, keepdims=True)


def block_at(i, size):
    return pl.ds(pl.multiple_of(i * size, size), size)


def call(kernel, outs, *args, scratch=(), limit=16):
    def spec(a):
        return SMEM if a.dtype == jnp.int32 else VMEM

    outs = tuple(jax.ShapeDtypeStruct(*o) for o in outs)
    return pl.pallas_call(
        kernel,
        out_shape=outs,
        in_specs=[spec(a) for a in args],
        out_specs=tuple(spec(o) for o in outs),
        scratch_shapes=[pltpu.VMEM(s, F32) for s in scratch],
        compiler_params=pltpu.CompilerParams(vmem_limit_bytes=limit << 20),
        name=kernel.__name__,
    )(*args)


def pack_kernel(feat_ref, out_ref):
    depth, per_row = feat_ref.shape
    width = depth * per_row
    spread = lax.broadcasted_iota(jnp.int32, (per_row, width), 1) % per_row == lax.broadcasted_iota(
        jnp.int32, (per_row, width), 0
    )
    wide = jnp.dot(feat_ref[...], jnp.where(spread, 1.0, 0.0).astype(BF16), preferred_element_type=F32)
    own = lax.broadcasted_iota(jnp.int32, (depth, width), 1) // per_row == lax.broadcasted_iota(
        jnp.int32, (depth, width), 0
    )
    line = jnp.sum(jnp.where(own, wide, 0.0), axis=0, keepdims=True)
    lines = jnp.concatenate([line[:, h * LANE : (h + 1) * LANE] for h in range(width // LANE)], axis=0)
    out_ref[...] = jnp.broadcast_to(lines.astype(BF16)[None], out_ref.shape)


def build_kernel(feat_ref, site_ref, gibbs_ref, cells_ref, sites_ref, site_norm_ref, cell_norm_ref, safe_ref):
    n_cells, width = cells_ref.shape
    n_sites = sites_ref.shape[1]
    depth = site_ref.shape[0]
    per_row = width // depth
    rows_blk, cols_blk = 256, 512
    site = site_ref[...]
    wide = site.astype(F32)
    site_norm = jnp.sum(wide * wide, axis=0, keepdims=True)
    for b in range(n_sites // LANE):
        site_norm_ref[b : b + 1, :] = site_norm[:, b * LANE : (b + 1) * LANE] / (depth * EPS)
    spread = (
        lax.broadcasted_iota(jnp.int32, (width, depth), 0) // per_row
        == lax.broadcasted_iota(jnp.int32, (width, depth), 1)
    )
    sites_ref[...] = jnp.dot(
        jnp.where(spread, 1.0, 0.0).astype(BF16), site, preferred_element_type=F32
    ).astype(BF16)
    feat = feat_ref[...]
    rows = lax.broadcasted_iota(jnp.int32, (rows_blk, width), 0)
    lanes = lax.broadcasted_iota(jnp.int32, (rows_blk, width), 1)
    own = rows % per_row == lanes % per_row
    ones = jnp.ones((8, width), BF16)
    largest = jnp.float32(0.0)
    for i in range(n_cells // rows_blk):
        pick = jnp.where(rows // per_row + i * (rows_blk // per_row) == lanes, 1.0, 0.0).astype(BF16)
        block = jnp.where(own, jnp.dot(pick, feat, preferred_element_type=F32), 0.0)
        cells_ref[i * rows_blk : (i + 1) * rows_blk, :] = block.astype(BF16)
        square = block * block
        high = square.astype(BF16)
        low = (square - high.astype(F32)).astype(BF16)
        norm = (nt_dot(ones, high) + nt_dot(ones, low))[0:1]
        for b in range(rows_blk // LANE):
            at = i * (rows_blk // LANE) + b
            cell_norm_ref[at : at + 1, :] = norm[:, b * LANE : (b + 1) * LANE] / (depth * EPS)
        largest = jnp.maximum(largest, jnp.max(norm))
    safe = largest * jnp.max(site_norm) <= SAFE_NORMS
    safe_ref[0, 0] = jnp.where(safe, 1, 0)

    @pl.when(safe)
    def _():
        scale = 2.0 / (depth * EPS) * math.log2(math.e)

        def tile(t, _):
            at = block_at(t // (n_sites // cols_blk), rows_blk)
            to = block_at(t % (n_sites // cols_blk), cols_blk)
            inner = jnp.dot(cells_ref[at, :], sites_ref[:, to], preferred_element_type=F32)
            gibbs_ref[at, to] = jnp.exp2(inner * scale)
            return 0

        lax.fori_loop(0, (n_cells // rows_blk) * (n_sites // cols_blk), tile, 0)


def log_sums(safe, level, gibbs_ref, cells_ref, sites_ref, out_ref, part_ref, sum_ref, over_sites):
    n_scen, blocks_in, _ = level.shape
    blocks_out = out_ref.shape[1]
    scale = 2.0 / ((cells_ref.shape[1] // 8) * EPS)

    @pl.when(safe)
    def _():
        top = jnp.max(jnp.max(level, axis=2, keepdims=True), axis=1, keepdims=True)
        part_ref[...] = jnp.exp(level - top)
        if over_sites:

            def cell_block(i, _):
                at = block_at(i, LANE)
                sums = [jnp.zeros((LANE, LANE), F32) for _ in range(n_scen)]
                for b in range(blocks_in):
                    tile = gibbs_ref[at, b * LANE : (b + 1) * LANE]
                    for s in range(n_scen):
                        sums[s] += tile * part_ref[s, b : b + 1, :]
                for s in range(n_scen):
                    out_ref[s, pl.ds(i, 1), :] = to_row(jnp.sum(sums[s], axis=1, keepdims=True))
                return 0

            lax.fori_loop(0, blocks_out, cell_block, 0)
        else:
            sum_ref[...] = jnp.zeros_like(sum_ref)

            def cell_block(i, _):
                at = block_at(i, LANE)
                columns = [
                    jnp.broadcast_to(to_column(part_ref[s, pl.ds(i, 1), :]), (LANE, LANE)) for s in range(n_scen)
                ]
                for b in range(blocks_out):
                    tile = gibbs_ref[at, b * LANE : (b + 1) * LANE]
                    for s in range(n_scen):
                        sum_ref[s, b] += jnp.sum((tile * columns[s]).reshape(LANE // 8, 8, LANE), axis=0)
                return 0

            lax.fori_loop(0, blocks_in, cell_block, 0)
            out_ref[...] = jnp.sum(sum_ref[...], axis=2)
        out_ref[...] = top + jnp.log(out_ref[...])

    @pl.when(jnp.logical_not(safe))
    def _():
        def block(i, _):
            at = block_at(i, LANE)
            if over_sites:
                inner = jnp.dot(cells_ref[at, :], sites_ref[...], preferred_element_type=F32)
            else:
                inner = lax.dot_general(
                    sites_ref[:, at], cells_ref[...], (((0,), (1,)), ((), ())), preferred_element_type=F32
                )
            for s in range(n_scen):
                score = inner * scale + jnp.concatenate([level[s, b : b + 1, :] for b in range(blocks_in)], axis=1)
                top = jnp.max(score, axis=1, keepdims=True)
                total = jnp.sum(jnp.exp(score - top), axis=1, keepdims=True)
                out_ref[s, pl.ds(i, 1), :] = to_row(top + jnp.log(total))
            return 0

        lax.fori_loop(0, blocks_out, block, 0)


def first_row_kernel(
    safe_ref, home_ref, site_norm_ref, gibbs_ref, cells_ref, sites_ref, send_ref, level_ref, out_ref, part_ref
):
    n_blocks = site_norm_ref.shape[0]
    level = home_ref[0:2, home_ref.shape[1] - n_blocks :, :] * (1.0 / EPS) - site_norm_ref[...][None]
    level_ref[...] = level
    log_sums(safe_ref[0, 0] == 1, level, gibbs_ref, cells_ref, sites_ref, out_ref, part_ref, None, True)
    send_ref[...] = jnp.broadcast_to(out_ref[...][None], send_ref.shape)


def next_row_kernel(
    safe_ref, terms_ref, column_ref, gibbs_ref, cells_ref, sites_ref, send_ref, level_ref, out_ref, part_ref
):
    level = jnp.sum(terms_ref[...], axis=0)[None] - column_ref[...]
    level_ref[...] = level
    log_sums(safe_ref[0, 0] == 1, level, gibbs_ref, cells_ref, sites_ref, out_ref, part_ref, None, True)
    send_ref[...] = jnp.broadcast_to(out_ref[...][None], send_ref.shape)


def column_kernel(
    safe_ref, place_ref, weight_ref, home_ref, got_ref, cell_norm_ref, level_ref, gibbs_ref, cells_ref, sites_ref,
    send_ref, column_ref, row_pot_ref, part_ref, sum_ref,
):
    half = row_pot_ref.shape[0]
    home = home_ref[...]
    demand = jnp.concatenate([home[0:2, :half], home[2:4, :half]], axis=1)
    total = jnp.sum(jnp.sum(demand, axis=2, keepdims=True), axis=1, keepdims=True)
    got = got_ref[...]
    top = jnp.max(got, axis=0)
    row = top + jnp.log(jnp.sum(jnp.exp(got - top[None]), axis=0))
    down = jnp.log(demand) - jnp.log(total) - row
    own = jnp.where(place_ref[1] == 0, down[0], down[1])
    norm = cell_norm_ref[...]
    first = place_ref[2] == 0
    row_pot_ref[...] = EPS * (jnp.where(first, own[:half], own[half:]) + jnp.where(first, norm[:half], norm[half:]))
    log_sums(safe_ref[0, 0] == 1, down, gibbs_ref, cells_ref, sites_ref, column_ref, part_ref, sum_ref, False)
    weight = weight_ref[...]
    which = lax.broadcasted_iota(jnp.int32, weight.shape, 1)
    term = jnp.zeros(level_ref.shape[1:], F32)
    for s in range(2):
        own_weight = jnp.sum(jnp.where(which == 2 * place_ref[0] + s, weight, 0.0), axis=1, keepdims=True)
        term += own_weight / jnp.sum(weight, axis=1, keepdims=True) * (level_ref[s] + column_ref[s])
    send_ref[...] = jnp.broadcast_to(term[None], send_ref.shape)


def last_kernel(terms_ref, column_ref, site_norm_ref, send_ref):
    n_blocks = site_norm_ref.shape[0]
    log_bary = jnp.sum(terms_ref[...], axis=0)
    potential = EPS * (log_bary[None] - column_ref[...] + site_norm_ref[...][None])
    send_ref[:, :n_blocks, :] = jnp.concatenate([potential, potential], axis=0)
    send_ref[:, n_blocks:, :] = jnp.broadcast_to(log_bary[None], (4, n_blocks, LANE))


def exchange(value, axes):
    return lax.all_to_all(value, axes, split_axis=0, concat_axis=0, tiled=True)


def on_device(demand, start_potential, cell_feat, site_feat, weights):
    n_home = lax.axis_size(HOME_GROUP)
    n_row = lax.axis_size(ROW_GROUP)
    n_bary = lax.axis_size(BARY_GROUP)
    n_sites = start_potential.shape[1] // n_home
    n_cells = demand.shape[1] * 2
    site_blocks, cell_blocks = n_sites // LANE, n_cells // LANE
    quarter = lax.axis_index(HOME_GROUP)
    place = jnp.stack([lax.axis_index(BARY_GROUP), lax.axis_index("core"), lax.axis_index("xh")]).astype(jnp.int32)

    width = cell_feat.size
    n_all = lax.axis_size(CELL_ORDER)
    (packed,) = call(pack_kernel, [((n_all, width // LANE, LANE), BF16)], cell_feat)
    packed, demand, start_potential = lax.optimization_barrier((packed, demand, start_potential))
    feat = exchange(packed, CELL_ORDER).reshape(n_all, width)
    shares = jnp.broadcast_to(demand.reshape(1, -1, LANE), (n_home, cell_blocks // 2, LANE))
    home = exchange(
        jnp.concatenate([shares, start_potential.reshape(n_home, site_blocks, LANE)], axis=1), HOME_GROUP
    )
    own_sites = lax.dynamic_slice_in_dim(site_feat, quarter * n_sites, n_sites, 1)
    weight = weights.reshape(1, -1)
    feat, home, own_sites, place, weight = lax.optimization_barrier((feat, home, own_sites, place, weight))
    gibbs, cells, sites, site_norm, cell_norm, safe = call(
        build_kernel,
        [
            ((n_cells, n_sites), F32),
            ((n_cells, width), BF16),
            ((width, n_sites), BF16),
            ((site_blocks, LANE), F32),
            ((cell_blocks, LANE), F32),
            ((1, 1), jnp.int32),
        ],
        feat, own_sites, limit=24,
    )
    on_cells, on_sites = (2, cell_blocks, LANE), (2, site_blocks, LANE)
    row_outs = [((n_row, *on_cells), F32), (on_sites, F32)]
    row_scratch = [on_cells, on_sites]
    send, level = call(
        first_row_kernel, row_outs, safe, home, site_norm, gibbs, cells, sites, scratch=row_scratch
    )
    for repeat in range(ITERS):
        got = exchange(send, ROW_GROUP)
        send, column, row_pot = call(
            column_kernel,
            [((n_bary, site_blocks, LANE), F32), (on_sites, F32), ((cell_blocks // 2, LANE), F32)],
            safe, place, weight, home, got, cell_norm, level, gibbs, cells, sites,
            scratch=[on_cells, (2, site_blocks, 8, LANE)],
        )
        terms = exchange(send, BARY_GROUP)
        if repeat < ITERS - 1:
            send, level = call(
                next_row_kernel, row_outs, safe, terms, column, gibbs, cells, sites, scratch=row_scratch
            )
    (send,) = call(last_kernel, [((n_home, 2 * site_blocks, LANE), F32)], terms, column, site_norm)
    both = exchange(send, HOME_GROUP)
    return row_pot.reshape(1, -1), both[:, :site_blocks].reshape(1, -1), both[:, site_blocks:].reshape(-1)


def solution(mesh):
    torus = Mesh(
        mesh.devices.reshape(8, 4, 2, mesh.shape["cell"], mesh.shape["site"]), ("z", "y", "core", "xh", "xl")
    )
    return jax.shard_map(
        on_device,
        mesh=torus,
        in_specs=(P(SCEN, "xh"), P(SCEN, "xl"), P(None, CELL_ORDER), P(None, "xl"), P()),
        out_specs=(P(SCEN, "xh"), P(SCEN, "xl"), P("xl")),
        check_vma=False,
    )
```

time: 190 us -> 160 us (0.84)
  Pallas kernels: 81.3 us -> 62.5 us
  blocking collectives: 39.6 us -> 57.6 us
  local copies, waits for them, and re-layouts: 12 us -> 2.18 us
  starting transfers between devices: 28.8 us -> 19.4 us
  waiting for transfers between devices: 23.3 us -> 15.4 us
    pallas_call x6 -> x7, Pallas kernels: 81.3 us -> 62.5 us  [call(): pl.pallas_call(kernel, out_shape=outs, in_specs=[spec(a) for a in args],...]
    all_to_all x3 -> x5, blocking collectives: 39.6 us -> 57.6 us  [exchange(): return lax.all_to_all(value, axes, split_axis=0, concat_axis=0, tiled=True)]
    all_to_all x4 -> x2, starting transfers between devices: 28.8 us -> 19.4 us  [exchange(): return lax.all_to_all(value, axes, split_axis=0, concat_axis=0, tiled=True)]
    all_to_all x4 -> x2, waiting for transfers between devices: 23.3 us -> 15.4 us  [exchange(): return lax.all_to_all(value, axes, split_axis=0, concat_axis=0, tiled=True)]
    unnamed x22 -> x6, local copies, waits for them, and re-layouts: 7.08 us -> 0.85 us
    all_to_all x6 -> x0, local copies, waits for them, and re-layouts: 2.82 us -> none  [exchange(): return lax.all_to_all(value, axes, split_axis=0, concat_axis=0, tiled=True)]
  transfers between devices with their start and end apart: 4 -> 2, of which waited for: 4 -> 2; matrix products, arithmetic and copies ran while one was open for 2% -> 1% of each run, Pallas kernels for 0% -> 0%
where the time goes in v2:
time: 160 us; the launch traced here: 159 us
  Pallas kernels  62.5 us (39%)
  blocking collectives  57.6 us (36%)
  starting transfers between devices  19.4 us (12%)
  waiting for transfers between devices  15.4 us (10%)
  local copies, waits for them, and re-layouts  2.18 us (1%)
    pallas_call x7, Pallas kernels, call(): pl.pallas_call(kernel, out_shape=outs, in_specs=[spec(a) for a in args],...  62.5 us
    all_to_all x5, blocking collectives, exchange(): return lax.all_to_all(value, axes, split_axis=0, concat_axis=0, tiled=True)  57.6 us
    all_to_all x2, starting transfers between devices, exchange(): return lax.all_to_all(value, axes, split_axis=0, concat_axis=0, tiled=True)  19.4 us
    all_to_all x2, waiting for transfers between devices, exchange(): return lax.all_to_all(value, axes, split_axis=0, concat_axis=0, tiled=True)  15.4 us
  transfers between devices with their start and end apart: 2, of which 2 were waited for; matrix products, arithmetic and copies ran while one was open for 1% of the time, Pallas kernels for 0%

profile of v2, /device:TPU:1, one launch (start us, length us, event | category | flops | bytes accessed | tf_op | source)
XLA Modules:
  0.0 159.2 jit_solution(733815173519010188)
XLA Ops:
  0.6 0.0 copy-start
  0.6 0.0 copy-start.1
  0.7 0.8 copy.8.feat_ref
  1.5 0.8 pack_kernel.1
  2.3 15.6 %all-to-all-start = ((bf16[256,2,128]{2,1,0:T(2,128)(2,1)}), bf16[256,2,128]{2,1,0:T(2,128)(2,1)S(1)}, u32[]{:S(2)}, u32[]{:S(2)}) async-start(bf16[256,2,128]{2,1,0:T(2,128)(2,1)} %pack_kernel.1), calls=%async_computation | async-start | bytes 262144 | tf_op jit(solution)/shard_map/all_to_all | solution.py:246
  18.0 0.7 broadcast_in_dim.8
  18.7 1.4 pad_maximum_fusion
  20.0 0.0 copy-done
  20.1 10.8 %all-to-all-done = bf16[256,2,128]{2,1,0:T(2,128)(2,1)S(1)} async-done(((bf16[256,2,128]{2,1,0:T(2,128)(2,1)}), bf16[256,2,128]{2,1,0:T(2,128)(2,1)S(1)}, u32[]{:S(2)}, u32[]{:S(2)}) %all-to-all-start) | async-done | bytes 131104 | tf_op jit(solution)/shard_map/all_to_all | solution.py:246
  30.9 3.8 %all-to-all-start.1 = ((f32[4,24,128]{2,1,0:T(8,128)}), f32[4,24,128]{2,1,0:T(8,128)S(1)}, u32[]{:S(2)}, u32[]{:S(2)}) async-start(f32[4,24,128]{2,1,0:T(8,128)} %pad_maximum_fusion), calls=%async_computation.1 | async-start | bytes 98304 | tf_op jit(solution)/shard_map/all_to_all | solution.py:246
  34.6 0.1 pad_add_fusion.place_ref
  34.7 4.6 %all-to-all-done.1.home_ref = f32[4,24,128]{2,1,0:T(8,128)S(1)} async-done(((f32[4,24,128]{2,1,0:T(8,128)}), f32[4,24,128]{2,1,0:T(8,128)S(1)}, u32[]{:S(2)}, u32[]{:S(2)}) %all-to-all-start.1) | async-done | bytes 49184 | tf_op jit(solution)/shard_map/all_to_all | solution.py:246
  39.3 2.2 %build_kernel.1 = (f32[2048,2048]{1,0:T(8,128)S(1)}, bf16[2048,256]{1,0:T(8,128)(2,1)S(1)}, bf16[256,2048]{1,0:T(8,128)(2,1)S(1)}, f32[16,128]{1,0:T(8,128)S(1)}, f32[16,128]{1,0:T(8,128)S(1)}, /*index=5*/s32[1,1]{1,0:T(1,128)}) custom-call(bf16[256,256]{1,0:T(8,128)(2,1)S(1)} %bitcast.13, bf16[32,2048]{1,0:T(8,128)(2,1)S(1)} %constant_dynamic-slice_fusion.site_ref), custom_call_target="tpu_custom_call" | custom-call | tf_op jit(solution)/shard_map/build_kernel/pallas_call | solution.py:52
  41.5 13.0 %first_row_kernel.1 = (f32[8,2,16,128]{3,2,1,0:T(8,128)S(1)}, f32[2,16,128]{2,1,0:T(8,128)S(1)}) custom-call(s32[1,1]{1,0:T(1,128)} %get-tuple-element.31.safe_ref, f32[4,24,128]{2,1,0:T(8,128)S(1)} %all-to-all-done.1.home_ref, f32[16,128]{1,0:T(8,128)S(1)} %get-tuple-element.35.site_norm_ref, f32[2048,2048]{1,0:T(8,128)S(1)} %get-tuple-element.36.gibbs_ref, ...), custom_call_target="tpu_custom_call" | custom-call | tf_op jit(solution)/shard_map/first_row_kernel/pallas_call | solution.py:52
  54.5 8.4 %all_to_all.35.got_ref = f32[8,2,16,128]{3,2,1,0:T(8,128)S(1)} all-to-all(f32[8,2,16,128]{3,2,1,0:T(8,128)S(1)} %get-tuple-element.39), channel_id=1, replica_groups=mesh['z'=8,'y'=4,'core'=2,'xh'=2,'xl'=2] {'xh','xl','core'}, dimensions={0} | all-to-all | bytes 262144 | tf_op jit(solution)/shard_map/all_to_all | solution.py:246
  63.0 0.0 copy-done.1
  63.0 16.7 %column_kernel.2 = (f32[32,16,128]{2,1,0:T(8,128)S(1)}, f32[2,16,128]{2,1,0:T(8,128)S(1)}, f32[8,128]{1,0:T(8,128)}) custom-call(s32[1,1]{1,0:T(1,128)} %get-tuple-element.31.safe_ref, s32[3]{0:T(128)S(1)} %pad_add_fusion.place_ref, f32[1,64]{1,0:T(1,128)S(1)} %bitcast.14, f32[4,24,128]{2,1,0:T(8,128)S(1)} %all-to-all-done.1.home_ref, ...), custom_call_target="tpu_custom_call" | custom-call | tf_op jit(solution)/shard_map/column_kernel/pallas_call | solution.py:52
  79.7 14.7 %all_to_all.36.terms_ref = f32[32,16,128]{2,1,0:T(8,128)S(1)} all-to-all(f32[32,16,128]{2,1,0:T(8,128)S(1)} %get-tuple-element.42), channel_id=1, replica_groups=mesh['z'=8,'y'=4,'core'=2,'xh'=2,'xl'=2] {'z','y'}, dimensions={0} | all-to-all | bytes 524288 | tf_op jit(solution)/shard_map/all_to_all | solution.py:246
  94.3 13.1 %next_row_kernel.1 = (f32[8,2,16,128]{3,2,1,0:T(8,128)S(1)}, f32[2,16,128]{2,1,0:T(8,128)S(1)}) custom-call(s32[1,1]{1,0:T(1,128)} %get-tuple-element.31.safe_ref, f32[32,16,128]{2,1,0:T(8,128)S(1)} %all_to_all.36.terms_ref, f32[2,16,128]{2,1,0:T(8,128)S(1)} %get-tuple-element.43.column_ref, f32[2048,2048]{1,0:T(8,128)S(1)} %get-tuple-element.36.gibbs_ref, ...), custom_call_target="tpu_custom_call" | custom-call | tf_op jit(solution)/shard_map/next_row_kernel/pallas_call | solution.py:52
  107.4 10.1 %all_to_all.37.got_ref = f32[8,2,16,128]{3,2,1,0:T(8,128)S(1)} all-to-all(f32[8,2,16,128]{3,2,1,0:T(8,128)S(1)} %get-tuple-element.44), channel_id=1, replica_groups=mesh['z'=8,'y'=4,'core'=2,'xh'=2,'xl'=2] {'xh','xl','core'}, dimensions={0} | all-to-all | bytes 262144 | tf_op jit(solution)/shard_map/all_to_all | solution.py:246
  117.5 16.7 %column_kernel.3 = (f32[32,16,128]{2,1,0:T(8,128)S(1)}, f32[2,16,128]{2,1,0:T(8,128)S(1)}, f32[8,128]{1,0:T(8,128)}) custom-call(s32[1,1]{1,0:T(1,128)} %get-tuple-element.31.safe_ref, s32[3]{0:T(128)S(1)} %pad_add_fusion.place_ref, f32[1,64]{1,0:T(1,128)S(1)} %bitcast.15, f32[4,24,128]{2,1,0:T(8,128)S(1)} %all-to-all-done.1.home_ref, ...), custom_call_target="tpu_custom_call" | custom-call | tf_op jit(solution)/shard_map/column_kernel/pallas_call | solution.py:52
  134.2 14.8 %all_to_all.38.terms_ref = f32[32,16,128]{2,1,0:T(8,128)S(1)} all-to-all(f32[32,16,128]{2,1,0:T(8,128)S(1)} %get-tuple-element.47), channel_id=1, replica_groups=mesh['z'=8,'y'=4,'core'=2,'xh'=2,'xl'=2] {'z','y'}, dimensions={0} | all-to-all | bytes 524288 | tf_op jit(solution)/shard_map/all_to_all | solution.py:246
  149.0 9.6 %all_to_all.39 = f32[4,32,128]{2,1,0:T(8,128)S(1)} all-to-all(f32[4,32,128]{2,1,0:T(8,128)S(1)} %last_kernel.1), channel_id=1, replica_groups=mesh['z'=8,'y'=4,'core'=2,'xh'=2,'xl'=2] {'xh','core'}, dimensions={0} | all-to-all | bytes 131072 | tf_op jit(solution)/shard_map/all_to_all | solution.py:246
  158.6 0.6 fusion
  (3 shorter events, 0.1 us)
Async XLA Ops:
  0.6 19.4 %copy-start = (bf16[32,8192]{1,0:T(8,128)(2,1)S(1)}, bf16[32,8192]{1,0:T(8,128)(2,1)}, u32[]{:S(2)}) copy-start(bf16[32,8192]{1,0:T(8,128)(2,1)} %param.8) | copy-start | bytes 1572868
  0.6 62.3 %copy-start.1 = (f32[64]{0:T(128)S(1)}, f32[64]{0:T(128)}, u32[]{:S(2)}) copy-start(f32[64]{0:T(128)} %param.9) | copy-start | bytes 772
  2.3 28.5 %all-to-all-start = ((bf16[256,2,128]{2,1,0:T(2,128)(2,1)}), bf16[256,2,128]{2,1,0:T(2,128)(2,1)S(1)}, u32[]{:S(2)}, u32[]{:S(2)}) async-start(bf16[256,2,128]{2,1,0:T(2,128)(2,1)} %pack_kernel.1), calls=%async_computation | async-start | bytes 262144 | tf_op jit(solution)/shard_map/all_to_all | solution.py:246
  30.9 8.5 %all-to-all-start.1 = ((f32[4,24,128]{2,1,0:T(8,128)}), f32[4,24,128]{2,1,0:T(8,128)S(1)}, u32[]{:S(2)}, u32[]{:S(2)}) async-start(f32[4,24,128]{2,1,0:T(8,128)} %pad_maximum_fusion), calls=%async_computation.1 | async-start | bytes 98304 | tf_op jit(solution)/shard_map/all_to_all | solution.py:246

commit v3 on v2

--- a/solution.py
+++ b/solution.py
@@ -42,6 +42,15 @@
 
 def block_at(i, size):
     return pl.ds(pl.multiple_of(i * size, size), size)
+
+
+def unrolled_loop(steps, by, body):
+    def several(i, _):
+        for u in range(by):
+            body(i * by + u)
+        return 0
+
+    lax.fori_loop(0, steps // by, several, 0)
 
 
 def call(kernel, outs, *args, scratch=(), limit=16):
@@ -118,14 +127,13 @@
     def _():
         scale = 2.0 / (depth * EPS) * math.log2(math.e)
 
-        def tile(t, _):
+        def tile(t):
             at = block_at(t // (n_sites // cols_blk), rows_blk)
             to = block_at(t % (n_sites // cols_blk), cols_blk)
             inner = jnp.dot(cells_ref[at, :], sites_ref[:, to], preferred_element_type=F32)
             gibbs_ref[at, to] = jnp.exp2(inner * scale)
-            return 0
-
-        lax.fori_loop(0, (n_cells // rows_blk) * (n_sites // cols_blk), tile, 0)
+
+        unrolled_loop((n_cells // rows_blk) * (n_sites // cols_blk), 4, tile)
 
 
 def log_sums(safe, level, gibbs_ref, cells_ref, sites_ref, out_ref, part_ref, sum_ref, over_sites):
@@ -139,7 +147,7 @@
         part_ref[...] = jnp.exp(level - top)
         if over_sites:
 
-            def cell_block(i, _):
+            def cell_block(i):
                 at = block_at(i, LANE)
                 sums = [jnp.zeros((LANE, LANE), F32) for _ in range(n_scen)]
                 for b in range(blocks_in):
@@ -148,13 +156,12 @@
                         sums[s] += tile * part_ref[s, b : b + 1, :]
                 for s in range(n_scen):
                     out_ref[s, pl.ds(i, 1), :] = to_row(jnp.sum(sums[s], axis=1, keepdims=True))
-                return 0
-
-            lax.fori_loop(0, blocks_out, cell_block, 0)
+
+            unrolled_loop(blocks_out, 4, cell_block)
         else:
             sum_ref[...] = jnp.zeros_like(sum_ref)
 
-            def cell_block(i, _):
+            def cell_block(i):
                 at = block_at(i, LANE)
                 columns = [
                     jnp.broadcast_to(to_column(part_ref[s, pl.ds(i, 1), :]), (LANE, LANE)) for s in range(n_scen)
@@ -163,9 +170,8 @@
                     tile = gibbs_ref[at, b * LANE : (b + 1) * LANE]
                     for s in range(n_scen):
                         sum_ref[s, b] += jnp.sum((tile * columns[s]).reshape(LANE // 8, 8, LANE), axis=0)
-                return 0
-
-            lax.fori_loop(0, blocks_in, cell_block, 0)
+
+            unrolled_loop(blocks_in, 4, cell_block)
             out_ref[...] = jnp.sum(sum_ref[...], axis=2)
         out_ref[...] = top + jnp.log(out_ref[...])
 
@@ -190,10 +196,9 @@
 
 
 def first_row_kernel(
-    safe_ref, home_ref, site_norm_ref, gibbs_ref, cells_ref, sites_ref, send_ref, level_ref, out_ref, part_ref
+    safe_ref, pots_ref, site_norm_ref, gibbs_ref, cells_ref, sites_ref, send_ref, level_ref, out_ref, part_ref
 ):
-    n_blocks = site_norm_ref.shape[0]
-    level = home_ref[0:2, home_ref.shape[1] - n_blocks :, :] * (1.0 / EPS) - site_norm_ref[...][None]
+    level = pots_ref[...] * (1.0 / EPS) - site_norm_ref[...][None]
     level_ref[...] = level
     log_sums(safe_ref[0, 0] == 1, level, gibbs_ref, cells_ref, sites_ref, out_ref, part_ref, None, True)
     send_ref[...] = jnp.broadcast_to(out_ref[...][None], send_ref.shape)
@@ -209,12 +214,11 @@
 
 
 def column_kernel(
-    safe_ref, place_ref, weight_ref, home_ref, got_ref, cell_norm_ref, level_ref, gibbs_ref, cells_ref, sites_ref,
+    safe_ref, place_ref, weight_ref, shares_ref, got_ref, cell_norm_ref, level_ref, gibbs_ref, cells_ref, sites_ref,
     send_ref, column_ref, row_pot_ref, part_ref, sum_ref,
 ):
     half = row_pot_ref.shape[0]
-    home = home_ref[...]
-    demand = jnp.concatenate([home[0:2, :half], home[2:4, :half]], axis=1)
+    demand = shares_ref[...]
     total = jnp.sum(jnp.sum(demand, axis=2, keepdims=True), axis=1, keepdims=True)
     got = got_ref[...]
     top = jnp.max(got, axis=0)
@@ -246,6 +250,10 @@
     return lax.all_to_all(value, axes, split_axis=0, concat_axis=0, tiled=True)
 
 
+def swapped(value, axis):
+    return lax.ppermute(value, axis, [(0, 1), (1, 0)])
+
+
 def on_device(demand, start_potential, cell_feat, site_feat, weights):
     n_home = lax.axis_size(HOME_GROUP)
     n_row = lax.axis_size(ROW_GROUP)
@@ -261,13 +269,22 @@
     (packed,) = call(pack_kernel, [((n_all, width // LANE, LANE), BF16)], cell_feat)
     packed, demand, start_potential = lax.optimization_barrier((packed, demand, start_potential))
     feat = exchange(packed, CELL_ORDER).reshape(n_all, width)
-    shares = jnp.broadcast_to(demand.reshape(1, -1, LANE), (n_home, cell_blocks // 2, LANE))
-    home = exchange(
-        jnp.concatenate([shares, start_potential.reshape(n_home, site_blocks, LANE)], axis=1), HOME_GROUP
+    core, far = lax.axis_index("core"), lax.axis_index("xh")
+    pots = start_potential.reshape(2, 2, site_blocks, LANE)
+    pots = jnp.where(far == 0, pots[0], pots[1])
+    share = demand.reshape(-1, LANE)
+    from_core = swapped(jnp.concatenate([share, jnp.where(core == 0, pots[1], pots[0])], axis=0), "core")
+    other_share, other_pot = from_core[: cell_blocks // 2], from_core[cell_blocks // 2 :]
+    own_pot = jnp.where(core == 0, pots[0], pots[1])
+    pots = jnp.where(core == 0, jnp.stack([own_pot, other_pot]), jnp.stack([other_pot, own_pot]))
+    shares = jnp.where(core == 0, jnp.stack([share, other_share]), jnp.stack([other_share, share]))
+    far_shares = swapped(shares, "xh")
+    shares = jnp.where(
+        far == 0, jnp.concatenate([shares, far_shares], axis=1), jnp.concatenate([far_shares, shares], axis=1)
     )
     own_sites = lax.dynamic_slice_in_dim(site_feat, quarter * n_sites, n_sites, 1)
     weight = weights.reshape(1, -1)
-    feat, home, own_sites, place, weight = lax.optimization_barrier((feat, home, own_sites, place, weight))
+    feat, pots, shares, own_sites, place, weight = lax.optimization_barrier((feat, pots, shares, own_sites, place, weight))
     gibbs, cells, sites, site_norm, cell_norm, safe = call(
         build_kernel,
         [
@@ -284,14 +301,14 @@
     row_outs = [((n_row, *on_cells), F32), (on_sites, F32)]
     row_scratch = [on_cells, on_sites]
     send, level = call(
-        first_row_kernel, row_outs, safe, home, site_norm, gibbs, cells, sites, scratch=row_scratch
+        first_row_kernel, row_outs, safe, pots, site_norm, gibbs, cells, sites, scratch=row_scratch
     )
     for repeat in range(ITERS):
         got = exchange(send, ROW_GROUP)
         send, column, row_pot = call(
             column_kernel,
             [((n_bary, site_blocks, LANE), F32), (on_sites, F32), ((cell_blocks // 2, LANE), F32)],
-            safe, place, weight, home, got, cell_norm, level, gibbs, cells, sites,
+            safe, place, weight, shares, got, cell_norm, level, gibbs, cells, sites,
             scratch=[on_cells, (2, site_blocks, 8, LANE)],
         )
         terms = exchange(send, BARY_GROUP)

time: 160 us -> 155 us (0.969)
  waiting for transfers between devices: 15.4 us -> 7.27 us
  blocking collectives: 57.6 us -> 61.2 us
    all_to_all x2 -> x1, waiting for transfers between devices: 15.4 us -> 3.34 us  [exchange(): return lax.all_to_all(value, axes, split_axis=0, concat_axis=0, tiled=True)]
    ppermute x0 -> x2, waiting for transfers between devices: none -> 3.93 us  [swapped(): return lax.ppermute(value, axis, [(0, 1), (1, 0)])]
    all_to_all x2 -> x1, starting transfers between devices: 19.4 us -> 15.6 us  [exchange(): return lax.all_to_all(value, axes, split_axis=0, concat_axis=0, tiled=True)]
    all_to_all x5, blocking collectives: 57.6 us -> 61.2 us  [exchange(): return lax.all_to_all(value, axes, split_axis=0, concat_axis=0, tiled=True)]
    ppermute x0 -> x2, starting transfers between devices: none -> 3.25 us  [swapped(): return lax.ppermute(value, axis, [(0, 1), (1, 0)])]
  transfers between devices with their start and end apart: 2 -> 3, of which waited for: 2 -> 3; matrix products, arithmetic and copies ran while one was open for 1% -> 2% of each run, Pallas kernels for 0% -> 0%
where the time goes in v3:
time: 155 us
  Pallas kernels  62.6 us (40%)
  blocking collectives  61.2 us (39%)
  starting transfers between devices  18.9 us (12%)
  waiting for transfers between devices  7.27 us (5%)
  other arithmetic  2.32 us (1%)
    pallas_call x7, Pallas kernels, call(): pl.pallas_call(kernel, out_shape=outs, in_specs=[spec(a) for a in args],...  62.6 us
    all_to_all x5, blocking collectives, exchange(): return lax.all_to_all(value, axes, split_axis=0, concat_axis=0, tiled=True)  61.2 us
    all_to_all x1, starting transfers between devices, exchange(): return lax.all_to_all(value, axes, split_axis=0, concat_axis=0, tiled=True)  15.6 us
    ppermute x2, waiting for transfers between devices, swapped(): return lax.ppermute(value, axis, [(0, 1), (1, 0)])  3.93 us
    all_to_all x1, waiting for transfers between devices, exchange(): return lax.all_to_all(value, axes, split_axis=0, concat_axis=0, tiled=True)  3.34 us
    ppermute x2, starting transfers between devices, swapped(): return lax.ppermute(value, axis, [(0, 1), (1, 0)])  3.25 us
  transfers between devices with their start and end apart: 3, of which 3 were waited for; matrix products, arithmetic and copies ran while one was open for 2% of the time, Pallas kernels for 0%

profile of v3, /device:TPU:1, one launch (start us, length us, event | category | flops | bytes accessed | tf_op | source)
XLA Modules:
  0.0 154.5 jit_solution(10516796362372652126)
XLA Ops:
  0.6 0.0 copy-start
  0.6 0.0 copy-start.1
  0.7 0.8 copy.8.feat_ref
  1.5 0.9 pack_kernel.1
  2.3 15.6 %all-to-all-start = ((bf16[256,2,128]{2,1,0:T(2,128)(2,1)}), bf16[256,2,128]{2,1,0:T(2,128)(2,1)S(1)}, u32[]{:S(2)}, u32[]{:S(2)}) async-start(bf16[256,2,128]{2,1,0:T(2,128)(2,1)} %pack_kernel.1), calls=%async_computation | async-start | bytes 262144 | tf_op jit(solution)/shard_map/all_to_all | solution.py:250
  18.0 0.8 broadcast_select_fusion
  18.8 0.7 pad_maximum_fusion
  19.5 2.1 %collective-permute-start = (f32[24,128]{1,0:T(8,128)S(1)}, f32[24,128]{1,0:T(8,128)S(1)}, u32[]{:S(2)}, u32[]{:S(2)}) collective-permute-start(f32[24,128]{1,0:T(8,128)S(1)} %pad_maximum_fusion), channel_id=1, source_target_pairs={{0,4},{4,0},{1,5},{5,1},{2,6},{6,2},{3,7},{7,3},{8,12},{12,8},{9,1... | collective-permute-start | bytes 36872 | tf_op jit(solution)/shard_map/ppermute | solution.py:254
  21.6 0.0 copy-done
  21.6 0.1 pad_add_fusion.place_ref
  21.7 0.7 collective-permute-done
  22.5 0.8 maximum_select_fusion.2
  23.2 1.1 collective-permute-start.1
  24.3 3.2 %collective-permute-done.1 = f32[2,8,128]{2,1,0:T(8,128)S(1)} collective-permute-done((f32[2,8,128]{2,1,0:T(8,128)S(1)}, f32[2,8,128]{2,1,0:T(8,128)S(1)}, u32[]{:S(2)}, u32[]{:S(2)}) %collective-permute-start.1) | collective-permute-done | bytes 8224 | tf_op jit(solution)/shard_map/ppermute | solution.py:254
  27.5 3.3 %all-to-all-done = bf16[256,2,128]{2,1,0:T(2,128)(2,1)S(1)} async-done(((bf16[256,2,128]{2,1,0:T(2,128)(2,1)}), bf16[256,2,128]{2,1,0:T(2,128)(2,1)S(1)}, u32[]{:S(2)}, u32[]{:S(2)}) %all-to-all-start) | async-done | bytes 131104 | tf_op jit(solution)/shard_map/all_to_all | solution.py:250
  30.9 2.2 %build_kernel.1 = (f32[2048,2048]{1,0:T(8,128)S(1)}, bf16[2048,256]{1,0:T(8,128)(2,1)S(1)}, bf16[256,2048]{1,0:T(8,128)(2,1)S(1)}, f32[16,128]{1,0:T(8,128)S(1)}, f32[16,128]{1,0:T(8,128)S(1)}, /*index=5*/s32[1,1]{1,0:T(1,128)}) custom-call(bf16[256,256]{1,0:T(8,128)(2,1)S(1)} %bitcast.19, bf16[32,2048]{1,0:T(8,128)(2,1)S(1)} %constant_dynamic-slice_fusion.site_ref), custom_call_target="tpu_custom_call" | custom-call | tf_op jit(solution)/shard_map/build_kernel/pallas_call | solution.py:61
  33.1 13.1 %first_row_kernel.1 = (f32[8,2,16,128]{3,2,1,0:T(8,128)S(1)}, f32[2,16,128]{2,1,0:T(8,128)S(1)}) custom-call(s32[1,1]{1,0:T(1,128)} %get-tuple-element.32.safe_ref, f32[2,16,128]{2,1,0:T(8,128)S(1)} %maximum_select_fusion.pots_ref, f32[16,128]{1,0:T(8,128)S(1)} %get-tuple-element.37.site_norm_ref, f32[2048,2048]{1,0:T(8,128)S(1)} %get-tuple-element.38.gibbs_ref, ...), custom_call_target="tpu_custom_call" | custom-call | tf_op jit(solution)/shard_map/first_row_kernel/pallas_call | solution.py:61
  46.2 8.4 %all_to_all.30.got_ref = f32[8,2,16,128]{3,2,1,0:T(8,128)S(1)} all-to-all(f32[8,2,16,128]{3,2,1,0:T(8,128)S(1)} %get-tuple-element.41), channel_id=1, replica_groups=mesh['z'=8,'y'=4,'core'=2,'xh'=2,'xl'=2] {'xh','xl','core'}, dimensions={0} | all-to-all | bytes 262144 | tf_op jit(solution)/shard_map/all_to_all | solution.py:250
  54.6 0.0 copy-done.1
  54.6 16.7 %column_kernel.2 = (f32[32,16,128]{2,1,0:T(8,128)S(1)}, f32[2,16,128]{2,1,0:T(8,128)S(1)}, f32[8,128]{1,0:T(8,128)}) custom-call(s32[1,1]{1,0:T(1,128)} %get-tuple-element.32.safe_ref, s32[3]{0:T(128)S(1)} %pad_add_fusion.place_ref, f32[1,64]{1,0:T(1,128)S(1)} %bitcast.20, f32[2,16,128]{2,1,0:T(8,128)S(1)} %maximum_select_fusion.1.shares_ref, ...), custom_call_target="tpu_custom_call" | custom-call | tf_op jit(solution)/shard_map/column_kernel/pallas_call | solution.py:61
  71.3 18.4 %all_to_all.31.terms_ref = f32[32,16,128]{2,1,0:T(8,128)S(1)} all-to-all(f32[32,16,128]{2,1,0:T(8,128)S(1)} %get-tuple-element.44), channel_id=1, replica_groups=mesh['z'=8,'y'=4,'core'=2,'xh'=2,'xl'=2] {'z','y'}, dimensions={0} | all-to-all | bytes 524288 | tf_op jit(solution)/shard_map/all_to_all | solution.py:250
  89.6 13.1 %next_row_kernel.1 = (f32[8,2,16,128]{3,2,1,0:T(8,128)S(1)}, f32[2,16,128]{2,1,0:T(8,128)S(1)}) custom-call(s32[1,1]{1,0:T(1,128)} %get-tuple-element.32.safe_ref, f32[32,16,128]{2,1,0:T(8,128)S(1)} %all_to_all.31.terms_ref, f32[2,16,128]{2,1,0:T(8,128)S(1)} %get-tuple-element.45.column_ref, f32[2048,2048]{1,0:T(8,128)S(1)} %get-tuple-element.38.gibbs_ref, ...), custom_call_target="tpu_custom_call" | custom-call | tf_op jit(solution)/shard_map/next_row_kernel/pallas_call | solution.py:61
  102.7 10.1 %all_to_all.32.got_ref = f32[8,2,16,128]{3,2,1,0:T(8,128)S(1)} all-to-all(f32[8,2,16,128]{3,2,1,0:T(8,128)S(1)} %get-tuple-element.46), channel_id=1, replica_groups=mesh['z'=8,'y'=4,'core'=2,'xh'=2,'xl'=2] {'xh','xl','core'}, dimensions={0} | all-to-all | bytes 262144 | tf_op jit(solution)/shard_map/all_to_all | solution.py:250
  112.8 16.7 %column_kernel.3 = (f32[32,16,128]{2,1,0:T(8,128)S(1)}, f32[2,16,128]{2,1,0:T(8,128)S(1)}, f32[8,128]{1,0:T(8,128)}) custom-call(s32[1,1]{1,0:T(1,128)} %get-tuple-element.32.safe_ref, s32[3]{0:T(128)S(1)} %pad_add_fusion.place_ref, f32[1,64]{1,0:T(1,128)S(1)} %bitcast.21, f32[2,16,128]{2,1,0:T(8,128)S(1)} %maximum_select_fusion.1.shares_ref, ...), custom_call_target="tpu_custom_call" | custom-call | tf_op jit(solution)/shard_map/column_kernel/pallas_call | solution.py:61
  129.5 14.8 %all_to_all.33.terms_ref = f32[32,16,128]{2,1,0:T(8,128)S(1)} all-to-all(f32[32,16,128]{2,1,0:T(8,128)S(1)} %get-tuple-element.49), channel_id=1, replica_groups=mesh['z'=8,'y'=4,'core'=2,'xh'=2,'xl'=2] {'z','y'}, dimensions={0} | all-to-all | bytes 524288 | tf_op jit(solution)/shard_map/all_to_all | solution.py:250
  144.3 9.6 %all_to_all.34 = f32[4,32,128]{2,1,0:T(8,128)S(1)} all-to-all(f32[4,32,128]{2,1,0:T(8,128)S(1)} %last_kernel.1), channel_id=1, replica_groups=mesh['z'=8,'y'=4,'core'=2,'xh'=2,'xl'=2] {'xh','core'}, dimensions={0} | all-to-all | bytes 131072 | tf_op jit(solution)/shard_map/all_to_all | solution.py:250
  153.9 0.6 fusion
  (8 shorter events, 0.1 us)
Async XLA Ops:
  0.6 21.0 %copy-start = (bf16[32,8192]{1,0:T(8,128)(2,1)S(1)}, bf16[32,8192]{1,0:T(8,128)(2,1)}, u32[]{:S(2)}) copy-start(bf16[32,8192]{1,0:T(8,128)(2,1)} %param.8) | copy-start | bytes 1572868
  0.6 53.9 %copy-start.1 = (f32[64]{0:T(128)S(1)}, f32[64]{0:T(128)}, u32[]{:S(2)}) copy-start(f32[64]{0:T(128)} %param.9) | copy-start | bytes 772
  2.3 28.5 %all-to-all-start = ((bf16[256,2,128]{2,1,0:T(2,128)(2,1)}), bf16[256,2,128]{2,1,0:T(2,128)(2,1)S(1)}, u32[]{:S(2)}, u32[]{:S(2)}) async-start(bf16[256,2,128]{2,1,0:T(2,128)(2,1)} %pack_kernel.1), calls=%async_computation | async-start | bytes 262144 | tf_op jit(solution)/shard_map/all_to_all | solution.py:250
  19.5 3.0 %collective-permute-start = (f32[24,128]{1,0:T(8,128)S(1)}, f32[24,128]{1,0:T(8,128)S(1)}, u32[]{:S(2)}, u32[]{:S(2)}) collective-permute-start(f32[24,128]{1,0:T(8,128)S(1)} %pad_maximum_fusion), channel_id=1, source_target_pairs={{0,4},{4,0},{1,5},{5,1},{2,6},{6,2},{3,7},{7,3},{8,12},{12,8},{9,1... | collective-permute-start | bytes 36872 | tf_op jit(solution)/shard_map/ppermute | solution.py:254
  23.2 4.3 %collective-permute-start.1 = (f32[2,8,128]{2,1,0:T(8,128)S(1)}, f32[2,8,128]{2,1,0:T(8,128)S(1)}, u32[]{:S(2)}, u32[]{:S(2)}) collective-permute-start(f32[2,8,128]{2,1,0:T(8,128)S(1)} %maximum_select_fusion.2), channel_id=1, source_target_pairs={{0,2},{2,0},{1,3},{3,1},{4,6},{6,4},{5,7},{7,5},{8,10},{10,8},{9,1... | collective-permute-start | bytes 24584 | tf_op jit(solution)/shard_map/ppermute | solution.py:254

commit v4 on v3

v4 whole, which is shorter than its diff:
```python
import math

import jax
import jax.numpy as jnp
from jax import lax
from jax.experimental import pallas as pl
from jax.experimental.pallas import tpu as pltpu
from jax.sharding import Mesh
from jax.sharding import PartitionSpec as P

ITERS = 2
EPS = 0.25
SCEN = ("z", "y", "core")
CELL_ORDER = ("xh", "z", "y", "core", "xl")
ROW_GROUP = ("xh", "xl", "core")
BARY_GROUP = ("z", "y")
HOME_GROUP = ("xh", "core")
SWAP_GROUP = ("core", "xh")
CORE, FAR, CROSS = 2, 1, 3
F32 = jnp.float32
BF16 = jnp.bfloat16
SAFE_NORMS = 14400.0
LANE = 128
VMEM = pl.BlockSpec(memory_space=pltpu.VMEM)
SMEM = pl.BlockSpec(memory_space=pltpu.SMEM)


def diagonal():
    shape = (LANE, LANE)
    return lax.broadcasted_iota(jnp.int32, shape, 0) == lax.broadcasted_iota(jnp.int32, shape, 1)


def to_row(column):
    return jnp.sum(jnp.where(diagonal(), column, 0.0), axis=0, keepdims=True)


def to_column(row):
    return jnp.sum(jnp.where(diagonal(), row, 0.0), axis=1, keepdims=True)


def block_at(i, size):
    return pl.ds(pl.multiple_of(i * size, size), size)


def unrolled_loop(steps, by, body):
    def several(i, _):
        for u in range(by):
            body(i * by + u)
        return 0

    lax.fori_loop(0, steps // by, several, 0)


def call(kernel, outs, *args, scratch=(), limit=16, apart=()):
    def spec(a):
        if any(a is one for one in apart):
            return pl.BlockSpec(memory_space=pltpu.HBM)
        return SMEM if a.dtype == jnp.int32 else VMEM

    outs = tuple(jax.ShapeDtypeStruct(*o) for o in outs)
    return pl.pallas_call(
        kernel,
        out_shape=outs,
        in_specs=[spec(a) for a in args],
        out_specs=tuple(spec(o) for o in outs),
        scratch_shapes=[pltpu.VMEM(s, F32) if isinstance(s, tuple) else s for s in scratch],
        compiler_params=pltpu.CompilerParams(vmem_limit_bytes=limit << 20),
    )(*args)


def pack_kernel(feat_ref, out_ref):
    per_row, depth = feat_ref.shape
    width = depth * per_row
    spread = lax.broadcasted_iota(jnp.int32, (depth, width), 1) // per_row == lax.broadcasted_iota(
        jnp.int32, (depth, width), 0
    )
    wide = jnp.dot(feat_ref[...], jnp.where(spread, 1.0, 0.0).astype(BF16), preferred_element_type=F32)
    own = lax.broadcasted_iota(jnp.int32, (per_row, width), 1) % per_row == lax.broadcasted_iota(
        jnp.int32, (per_row, width), 0
    )
    line = jnp.sum(jnp.where(own, wide, 0.0), axis=0, keepdims=True)
    lines = jnp.concatenate([line[:, h * LANE : (h + 1) * LANE] for h in range(width // LANE)], axis=0)
    out_ref[...] = jnp.broadcast_to(lines.astype(BF16)[None], out_ref.shape)


def prep_kernel(
    place_ref, site_ref, pot_ref, core_pot_ref, demand_ref, core_demand_ref, far_demand_ref, cross_demand_ref,
    weight_ref, sites_ref, site_norm_ref, site_top_ref, level_ref, part_ref, log_share_ref, mix_ref,
    quarter_ref, share_ref, weights_ref, sems,
):
    n_sites = site_ref.shape[1]
    core, far = place_ref[1], place_ref[2]
    here = pl.ds(pl.multiple_of((2 * far + core) * n_sites, n_sites), n_sites)
    copies = [
        pltpu.make_async_copy(source, target, sems.at[k])
        for k, (source, target) in enumerate(
            ((pot_ref.at[:, here], quarter_ref), (demand_ref, share_ref), (weight_ref, weights_ref))
        )
    ]
    for copy in copies:
        copy.start()
    width = sites_ref.shape[0]
    depth, n_sites = site_ref.shape
    site = site_ref[...]
    wide = site.astype(F32)
    site_norm = jnp.sum(wide * wide, axis=0, keepdims=True)
    site_top_ref[...] = jnp.broadcast_to(jnp.max(site_norm, axis=1, keepdims=True), site_top_ref.shape)
    for b in range(n_sites // LANE):
        site_norm_ref[b : b + 1, :] = site_norm[:, b * LANE : (b + 1) * LANE] / (depth * EPS)
    spread = (
        lax.broadcasted_iota(jnp.int32, (width, depth), 0) // (width // depth)
        == lax.broadcasted_iota(jnp.int32, (width, depth), 1)
    )
    sites_ref[...] = jnp.dot(
        jnp.where(spread, 1.0, 0.0).astype(BF16), site, preferred_element_type=F32
    ).astype(BF16)
    for copy in copies:
        copy.wait()

    def by_core(own, other):
        return jnp.where(core == 0, own, other), jnp.where(core == 0, other, own)

    for s, line in enumerate(by_core(quarter_ref[...], core_pot_ref[:, here])):
        for b in range(n_sites // LANE):
            level_ref[s, b : b + 1, :] = line[:, b * LANE : (b + 1) * LANE]
    level = level_ref[...] * (1.0 / EPS) - site_norm_ref[...][None]
    level_ref[...] = level
    part_ref[...] = jnp.exp(level - overall(jnp.max, level))
    near = by_core(share_ref[...], core_demand_ref[...])
    away = by_core(far_demand_ref[...], cross_demand_ref[...])
    half = log_share_ref.shape[1] // 2
    for s in range(2):
        first = jnp.where(far == 0, near[s], away[s])
        second = jnp.where(far == 0, away[s], near[s])
        for b in range(half):
            log_share_ref[s, b : b + 1, :] = first[:, b * LANE : (b + 1) * LANE]
            log_share_ref[s, half + b : half + b + 1, :] = second[:, b * LANE : (b + 1) * LANE]
    demand = log_share_ref[...]
    log_share_ref[...] = jnp.log(demand) - jnp.log(overall(jnp.sum, demand))
    weight = weights_ref[...]
    which = lax.broadcasted_iota(jnp.int32, weight.shape, 1)
    total = jnp.sum(weight, axis=1, keepdims=True)
    for s in range(2):
        own = jnp.sum(jnp.where(which == 2 * place_ref[0] + s, weight, 0.0), axis=1, keepdims=True)
        mix_ref[s] = jnp.broadcast_to(own / total, mix_ref.shape[1:])


def overall(reduce, value):
    return reduce(reduce(value, axis=2, keepdims=True), axis=1, keepdims=True)


def cell_rows(i, feat, size, per_row):
    width = feat.shape[1]
    rows = lax.broadcasted_iota(jnp.int32, (size, width), 0)
    lanes = lax.broadcasted_iota(jnp.int32, (size, width), 1)
    pick = jnp.where(rows // per_row + i * (size // per_row) == lanes, 1.0, 0.0).astype(BF16)
    block = jnp.dot(pick, feat, preferred_element_type=F32)
    return jnp.where(rows % per_row == lanes % per_row, block, 0.0).astype(BF16)


def build_kernel(
    feat_ref, sites_ref, site_top_ref, level_ref, part_ref,
    gibbs_ref, cells_ref, cell_norm_ref, safe_ref, send_ref, out_ref, sum_ref,
):
    n_cells, width = cells_ref.shape
    n_sites = sites_ref.shape[1]
    n_lines = feat_ref.shape[0]
    per_row = n_cells // n_lines
    depth = width // per_row
    rows_blk, cols_blk = 512, 512
    feat = feat_ref[...]
    wide = feat.astype(F32)
    square = wide * wide
    high = square.astype(BF16)
    low = (square - high.astype(F32)).astype(BF16)
    same = lax.broadcasted_iota(jnp.int32, (width, LANE), 0) % per_row == lax.broadcasted_iota(
        jnp.int32, (width, LANE), 1
    ) % per_row
    fold = jnp.where(same, 1.0, 0.0).astype(BF16)
    norm = jnp.dot(high, fold, preferred_element_type=F32) + jnp.dot(low, fold, preferred_element_type=F32)
    group = LANE // per_row
    own = lax.broadcasted_iota(jnp.int32, (n_lines, LANE), 0) % group == lax.broadcasted_iota(
        jnp.int32, (n_lines, LANE), 1
    ) // per_row
    cell_norm_ref[...] = jnp.sum(
        jnp.where(own, norm, 0.0).reshape(n_cells // LANE, group, LANE), axis=1
    ) / (depth * EPS)
    safe = jnp.max(norm) * jnp.max(site_top_ref[...]) <= SAFE_NORMS
    safe_ref[0, 0] = jnp.where(safe, 1, 0)

    @pl.when(safe)
    def _():
        scale = 2.0 / (depth * EPS) * math.log2(math.e)

        def block(i):
            at = block_at(i, rows_blk)
            rows = cell_rows(i, feat_ref[...], rows_blk, per_row)
            for j in range(n_sites // cols_blk):
                inner = jnp.dot(
                    rows, sites_ref[:, j * cols_blk : (j + 1) * cols_blk], preferred_element_type=F32
                )
                values = jnp.exp2(inner * scale)
                gibbs_ref[at, j * cols_blk : (j + 1) * cols_blk] = values
                for s in range(2):
                    terms = [
                        values[:, b * LANE : (b + 1) * LANE]
                        * part_ref[s, j * (cols_blk // LANE) + b : j * (cols_blk // LANE) + b + 1, :]
                        for b in range(cols_blk // LANE)
                    ]
                    added = (terms[0] + terms[1]) + (terms[2] + terms[3])
                    if j == 0:
                        sum_ref[s, at, :] = added
                    else:
                        sum_ref[s, at, :] += added

        unrolled_loop(n_cells // rows_blk, 1, block)

        def fold_block(i):
            at = block_at(i, LANE)
            for s in range(2):
                out_ref[s, pl.ds(i, 1), :] = to_row(jnp.sum(sum_ref[s, at, :], axis=1, keepdims=True))

        unrolled_loop(n_cells // LANE, 8, fold_block)
        out_ref[...] = overall(jnp.max, level_ref[...]) + jnp.log(out_ref[...])

    @pl.when(jnp.logical_not(safe))
    def _():
        for i in range(n_cells // rows_blk):
            cells_ref[i * rows_blk : (i + 1) * rows_blk, :] = cell_rows(i, feat_ref[...], rows_blk, per_row)
        log_domain(level_ref[...], cells_ref, sites_ref, out_ref, True)

    send_ref[...] = jnp.broadcast_to(out_ref[...][None], send_ref.shape)


def log_domain(level, cells_ref, sites_ref, out_ref, over_sites):
    n_scen, blocks_in, _ = level.shape
    scale = 2.0 / ((cells_ref.shape[1] // 8) * EPS)

    def block(i, _):
        at = block_at(i, LANE)
        if over_sites:
            inner = jnp.dot(cells_ref[at, :], sites_ref[...], preferred_element_type=F32)
        else:
            inner = lax.dot_general(
                sites_ref[:, at], cells_ref[...], (((0,), (1,)), ((), ())), preferred_element_type=F32
            )
        for s in range(n_scen):
            score = inner * scale + jnp.concatenate([level[s, b : b + 1, :] for b in range(blocks_in)], axis=1)
            top = jnp.max(score, axis=1, keepdims=True)
            total = jnp.sum(jnp.exp(score - top), axis=1, keepdims=True)
            out_ref[s, pl.ds(i, 1), :] = to_row(top + jnp.log(total))
        return 0

    lax.fori_loop(0, out_ref.shape[1], block, 0)


def log_sums(safe, level, gibbs_ref, cells_ref, sites_ref, out_ref, part_ref, sum_ref, over_sites):
    n_scen, blocks_in, _ = level.shape
    blocks_out = out_ref.shape[1]

    @pl.when(safe)
    def _():
        top = overall(jnp.max, level)
        part_ref[...] = jnp.exp(level - top)
        if over_sites:

            def cell_block(i):
                at = block_at(i, LANE)
                sums = [jnp.zeros((LANE, LANE), F32) for _ in range(n_scen)]
                for b in range(blocks_in):
                    tile = gibbs_ref[at, b * LANE : (b + 1) * LANE]
                    for s in range(n_scen):
                        sums[s] += tile * part_ref[s, b : b + 1, :]
                for s in range(n_scen):
                    out_ref[s, pl.ds(i, 1), :] = to_row(jnp.sum(sums[s], axis=1, keepdims=True))

            unrolled_loop(blocks_out, 8, cell_block)
        else:
            sum_ref[...] = jnp.zeros_like(sum_ref)

            def cell_block(i):
                at = block_at(i, LANE)
                columns = [
                    jnp.broadcast_to(to_column(part_ref[s, pl.ds(i, 1), :]), (LANE, LANE)) for s in range(n_scen)
                ]
                for b in range(blocks_out):
                    tile = gibbs_ref[at, b * LANE : (b + 1) * LANE]
                    for s in range(n_scen):
                        sum_ref[s, b] += jnp.sum((tile * columns[s]).reshape(LANE // 8, 8, LANE), axis=0)

            unrolled_loop(blocks_in, 8, cell_block)
            out_ref[...] = jnp.sum(sum_ref[...], axis=2)
        out_ref[...] = top + jnp.log(out_ref[...])

    @pl.when(jnp.logical_not(safe))
    def _():
        log_domain(level, cells_ref, sites_ref, out_ref, over_sites)


def next_row_kernel(
    safe_ref, terms_ref, column_ref, gibbs_ref, cells_ref, sites_ref, send_ref, level_ref, out_ref, part_ref
):
    level = jnp.sum(terms_ref[...], axis=0)[None] - column_ref[...]
    level_ref[...] = level
    log_sums(safe_ref[0, 0] == 1, level, gibbs_ref, cells_ref, sites_ref, out_ref, part_ref, None, True)
    send_ref[...] = jnp.broadcast_to(out_ref[...][None], send_ref.shape)


def column_kernel(
    safe_ref, place_ref, mix_ref, log_share_ref, got_ref, cell_norm_ref, level_ref, gibbs_ref, cells_ref, sites_ref,
    send_ref, column_ref, row_pot_ref, part_ref, sum_ref,
):
    half = row_pot_ref.shape[0]
    got = got_ref[...]
    top = jnp.max(got, axis=0)
    row = top + jnp.log(jnp.sum(jnp.exp(got - top[None]), axis=0))
    down = log_share_ref[...] - row
    own = jnp.where(place_ref[1] == 0, down[0], down[1])
    norm = cell_norm_ref[...]
    first = place_ref[2] == 0
    row_pot_ref[...] = EPS * (jnp.where(first, own[:half], own[half:]) + jnp.where(first, norm[:half], norm[half:]))
    log_sums(safe_ref[0, 0] == 1, down, gibbs_ref, cells_ref, sites_ref, column_ref, part_ref, sum_ref, False)
    term = mix_ref[0] * (level_ref[0] + column_ref[0]) + mix_ref[1] * (level_ref[1] + column_ref[1])
    send_ref[...] = jnp.broadcast_to(term[None], send_ref.shape)


def last_kernel(place_ref, terms_ref, column_ref, site_norm_ref, own_ref, other_ref):
    n_blocks = site_norm_ref.shape[0]
    log_bary = jnp.sum(terms_ref[...], axis=0)
    potential = EPS * (log_bary[None] - column_ref[...] + site_norm_ref[...][None])
    first = place_ref[1] == 0
    own_ref[:n_blocks, :] = jnp.where(first, potential[0], potential[1])
    other_ref[:n_blocks, :] = jnp.where(first, potential[1], potential[0])
    own_ref[n_blocks:, :] = log_bary
    other_ref[n_blocks:, :] = log_bary


def join_kernel(place_ref, own_ref, core_ref, far_ref, cross_ref, pot_ref, log_bary_ref):
    n_blocks = own_ref.shape[0] // 2
    here = 2 * place_ref[2] + place_ref[1]
    for flip, ref in enumerate((own_ref, core_ref, far_ref, cross_ref)):
        at = block_at(here ^ flip, n_blocks)
        pot_ref[at, :] = ref[:n_blocks, :]
        log_bary_ref[at, :] = ref[n_blocks:, :]


def exchange(value, axes):
    return lax.all_to_all(value, axes, split_axis=0, concat_axis=0, tiled=True)


def swapped(value, flip):
    return lax.ppermute(value, SWAP_GROUP, [(k, k ^ flip) for k in range(4)])


def on_device(demand, start_potential, cell_feat, site_feat, weights):
    n_home = lax.axis_size(HOME_GROUP)
    n_row = lax.axis_size(ROW_GROUP)
    n_bary = lax.axis_size(BARY_GROUP)
    n_sites = start_potential.shape[1] // n_home
    n_cells = demand.shape[1] * 2
    site_blocks, cell_blocks = n_sites // LANE, n_cells // LANE
    quarter = lax.axis_index(HOME_GROUP)
    place = jnp.stack([lax.axis_index(BARY_GROUP), lax.axis_index("core"), lax.axis_index("xh")]).astype(jnp.int32)

    width = cell_feat.size
    n_all = lax.axis_size(CELL_ORDER)
    (packed,) = call(pack_kernel, [((n_all, width // LANE, LANE), BF16)], cell_feat.T)
    packed, demand, start_potential = lax.optimization_barrier((packed, demand, start_potential))
    feat = exchange(packed, CELL_ORDER)
    feat = feat.reshape(n_all, width)
    core_pot = swapped(start_potential, CORE)
    core_demand = swapped(demand, CORE)
    far_demand = swapped(demand, FAR)
    cross_demand = swapped(demand, CROSS)
    own_sites = lax.dynamic_slice_in_dim(site_feat, quarter * n_sites, n_sites, 1)
    weight = weights.reshape(1, -1)
    on_cells, on_sites = (2, cell_blocks, LANE), (2, site_blocks, LANE)
    sites, site_norm, site_top, level, part, log_share, mix = call(
        prep_kernel,
        [
            ((width, n_sites), BF16),
            ((site_blocks, LANE), F32),
            ((8, LANE), F32),
            (on_sites, F32),
            (on_sites, F32),
            (on_cells, F32),
            ((2, 1, LANE), F32),
        ],
        place, own_sites, start_potential, core_pot, demand, core_demand, far_demand, cross_demand,
        weight,
        scratch=[(1, n_sites), demand.shape, weight.shape, pltpu.SemaphoreType.DMA((3,))],
        apart=(start_potential, demand, weight),
    )
    feat, sites, site_norm, site_top, level, part, log_share, mix, place = lax.optimization_barrier(
        (feat, sites, site_norm, site_top, level, part, log_share, mix, place)
    )
    row_outs = [((n_row, *on_cells), F32), (on_sites, F32)]
    row_scratch = [on_cells, on_sites]
    gibbs, cells, cell_norm, safe, send = call(
        build_kernel,
        [
            ((n_cells, n_sites), F32),
            ((n_cells, width), BF16),
            ((cell_blocks, LANE), F32),
            ((1, 1), jnp.int32),
            row_outs[0],
        ],
        feat, sites, site_top, level, part, scratch=[on_cells, (2, n_cells, LANE)], limit=24,
    )
    for repeat in range(ITERS):
        got = exchange(send, ROW_GROUP)
        send, column, row_pot = call(
            column_kernel,
            [((n_bary, site_blocks, LANE), F32), (on_sites, F32), ((cell_blocks // 2, LANE), F32)],
            safe, place, mix, log_share, got, cell_norm, level, gibbs, cells, sites,
            scratch=[on_cells, (2, site_blocks, 8, LANE)],
        )
        terms = exchange(send, BARY_GROUP)
        if repeat < ITERS - 1:
            send, level = call(
                next_row_kernel, row_outs, safe, terms, column, gibbs, cells, sites, scratch=row_scratch
            )
    message = ((2 * site_blocks, LANE), F32)
    own, other = call(last_kernel, [message] * 2, place, terms, column, site_norm)
    whole = ((n_home * site_blocks, LANE), F32)
    potential, log_bary = call(
        join_kernel, [whole] * 2, place, own, swapped(other, CORE), swapped(own, FAR), swapped(other, CROSS)
    )
    return row_pot.reshape(1, -1), potential.reshape(1, -1), log_bary.reshape(-1)


def solution(mesh):
    torus = Mesh(
        mesh.devices.reshape(8, 4, 2, mesh.shape["cell"], mesh.shape["site"]), ("z", "y", "core", "xh", "xl")
    )
    return jax.shard_map(
        on_device,
        mesh=torus,
        in_specs=(P(SCEN, "xh"), P(SCEN, "xl"), P(None, CELL_ORDER), P(None, "xl"), P()),
        out_specs=(P(SCEN, "xh"), P(SCEN, "xl"), P("xl")),
        check_vma=False,
    )
```

time: 155 us -> 152 us (0.981)
  blocking collectives: 61.2 us -> 47.8 us
  starting transfers between devices: 18.9 us -> 26.9 us
  other arithmetic: 2.32 us -> 0.08 us
  waiting for transfers between devices: 7.27 us -> 9.02 us
    all_to_all x5 -> x4, blocking collectives: 61.2 us -> 47.8 us  [exchange(): return lax.all_to_all(value, axes, split_axis=0, concat_axis=0, tiled=True)]
    ppermute x2 -> x7, starting transfers between devices: 3.25 us -> 14 us  [swapped(): return lax.ppermute(value, SWAP_GROUP, [(k, k ^ flip) for k in range(4)])]
    all_to_all x1, waiting for transfers between devices: 3.34 us -> 6.34 us  [exchange(): return lax.all_to_all(value, axes, split_axis=0, concat_axis=0, tiled=True)]
    all_to_all x1, starting transfers between devices: 15.6 us -> 13 us  [exchange(): return lax.all_to_all(value, axes, split_axis=0, concat_axis=0, tiled=True)]
    unnamed x6 -> x11, local copies, waits for them, and re-layouts: 0.85 us -> 2.86 us
    ppermute x2 -> x7, waiting for transfers between devices: 3.93 us -> 2.68 us  [swapped(): return lax.ppermute(value, SWAP_GROUP, [(k, k ^ flip) for k in range(4)])]
    pallas_call x7 -> x8, Pallas kernels: 62.6 us -> 63.7 us  [call(): pl.pallas_call(kernel, out_shape=outs, in_specs=[spec(a) for a in args],...]
  transfers between devices with their start and end apart: 3 -> 8, of which waited for: 3 -> 3; matrix products, arithmetic and copies ran while one was open for 2% -> 0% of each run, Pallas kernels for 0% -> 1%
where the time goes in v4:
time: 152 us; the launch traced here: 151 us
  Pallas kernels  63.7 us (42%)
  blocking collectives  47.8 us (31%)
  starting transfers between devices  26.9 us (18%)
  waiting for transfers between devices  9.02 us (6%)
  local copies, waits for them, and re-layouts  2.87 us (2%)
    pallas_call x8, Pallas kernels, call(): pl.pallas_call(kernel, out_shape=outs, in_specs=[spec(a) for a in args],...  63.7 us
    all_to_all x4, blocking collectives, exchange(): return lax.all_to_all(value, axes, split_axis=0, concat_axis=0, tiled=True)  47.8 us
    ppermute x7, starting transfers between devices, swapped(): return lax.ppermute(value, SWAP_GROUP, [(k, k ^ flip) for k in range(4)])  14 us
    all_to_all x1, starting transfers between devices, exchange(): return lax.all_to_all(value, axes, split_axis=0, concat_axis=0, tiled=True)  13 us
    all_to_all x1, waiting for transfers between devices, exchange(): return lax.all_to_all(value, axes, split_axis=0, concat_axis=0, tiled=True)  6.34 us
  transfers between devices with their start and end apart: 8, of which 3 were waited for; matrix products, arithmetic and copies ran while one was open for 0% of the time, Pallas kernels for 1%

profile of v4, /device:TPU:1, one launch (start us, length us, event | category | flops | bytes accessed | tf_op | source)
XLA Modules:
  0.0 151.1 jit_solution(7861524850976773062)
XLA Ops:
  0.6 0.0 copy-start
  0.6 0.0 copy-start.3
  0.7 0.7 copy-done.3
  1.4 0.8 shard_map.76
  2.2 4.1 %collective-permute-start.3 = (f32[1,1024]{1,0:T(1,128)}, f32[1,1024]{1,0:T(1,128)S(1)}, u32[]{:S(2)}, u32[]{:S(2)}) collective-permute-start(f32[1,1024]{1,0:T(1,128)} %demand_ref), channel_id=1, source_target_pairs={{0,6},{2,4},{4,2},{6,0},{1,7},{3,5},{5,3},{7,1},{8,14},{10,12},{12... | collective-permute-start | bytes 12296 | tf_op jit(solution)/shard_map/ppermute | solution.py:352
  6.4 1.9 %collective-permute-start.2 = (f32[1,1024]{1,0:T(1,128)}, f32[1,1024]{1,0:T(1,128)S(1)}, u32[]{:S(2)}, u32[]{:S(2)}) collective-permute-start(f32[1,1024]{1,0:T(1,128)} %demand_ref), channel_id=1, source_target_pairs={{0,2},{2,0},{4,6},{6,4},{1,3},{3,1},{5,7},{7,5},{8,10},{10,8},{12,... | collective-permute-start | bytes 12296 | tf_op jit(solution)/shard_map/ppermute | solution.py:352
  8.3 0.0 collective-permute-start.1
  8.3 13.0 %all-to-all-start = ((bf16[256,2,128]{2,1,0:T(2,128)(2,1)}), bf16[256,2,128]{2,1,0:T(2,128)(2,1)S(1)}, u32[]{:S(2)}, u32[]{:S(2)}) async-start(bf16[256,2,128]{2,1,0:T(2,128)(2,1)} %shard_map.76), calls=%async_computation | async-start | bytes 262144 | tf_op jit(solution)/shard_map/all_to_all | solution.py:348
  21.3 2.2 %collective-permute-start = (f32[1,8192]{1,0:T(1,128)}, f32[1,8192]{1,0:T(1,128)S(1)}, u32[]{:S(2)}, u32[]{:S(2)}) collective-permute-start(f32[1,8192]{1,0:T(1,128)} %pot_ref), channel_id=1, source_target_pairs={{0,4},{2,6},{4,0},{6,2},{1,5},{3,7},{5,1},{7,3},{8,12},{10,14},{12... | collective-permute-start | bytes 98312 | tf_op jit(solution)/shard_map/ppermute | solution.py:352
  23.5 0.0 copy-done
  23.5 0.1 pad_add_fusion.place_ref
  23.6 0.0 collective-permute-done.3.cross_demand_ref
  23.6 0.0 collective-permute-done.2.far_demand_ref
  23.6 0.0 collective-permute-done.1.core_demand_ref
  23.6 1.0 collective-permute-done.core_pot_ref
  24.6 0.0 copy-start.1
  24.6 0.8 copy-done.1
  25.3 0.0 copy-start.2
  25.3 0.7 copy-done.2
  26.0 0.0 copy-start.4
  26.0 0.7 copy-done.4
  26.7 1.1 shard_map.77
  27.8 6.3 %all-to-all-done = bf16[256,2,128]{2,1,0:T(2,128)(2,1)S(1)} async-done(((bf16[256,2,128]{2,1,0:T(2,128)(2,1)}), bf16[256,2,128]{2,1,0:T(2,128)(2,1)S(1)}, u32[]{:S(2)}, u32[]{:S(2)}) %all-to-all-start) | async-done | bytes 131104 | tf_op jit(solution)/shard_map/all_to_all | solution.py:348
  34.2 13.7 %shard_map.78 = (f32[2048,2048]{1,0:T(8,128)S(1)}, bf16[2048,256]{1,0:T(8,128)(2,1)S(1)}, f32[16,128]{1,0:T(8,128)S(1)}, s32[1,1]{1,0:T(1,128)}, f32[8,2,16,128]{3,2,1,0:T(8,128)S(1)}) custom-call(bf16[256,256]{1,0:T(8,128)(2,1)S(1)} %bitcast.12, bf16[256,2048]{1,0:T(8,128)(2,1)S(1)} %get-tuple-element.49.sites_ref, ...), custom_call_target="tpu_custom_call" | custom-call | tf_op jit(solution)/shard_map/pallas_call | solution.py:61
  47.8 8.4 %all_to_all.25.got_ref = f32[8,2,16,128]{3,2,1,0:T(8,128)S(1)} all-to-all(f32[8,2,16,128]{3,2,1,0:T(8,128)S(1)} %get-tuple-element.57), channel_id=1, replica_groups=mesh['z'=8,'y'=4,'core'=2,'xh'=2,'xl'=2] {'xh','xl','core'}, dimensions={0} | all-to-all | bytes 262144 | tf_op jit(solution)/shard_map/all_to_all | solution.py:348
  56.2 16.6 %shard_map.79 = (f32[32,16,128]{2,1,0:T(8,128)S(1)}, f32[2,16,128]{2,1,0:T(8,128)S(1)}, f32[8,128]{1,0:T(8,128)}) custom-call(s32[1,1]{1,0:T(1,128)} %get-tuple-element.53.safe_ref, s32[3]{0:T(128)S(1)} %pad_add_fusion.place_ref, f32[2,1,128]{2,1,0:T(1,128)S(1)} %get-tuple-element.55.mix_ref, f32[2,16,128]{2,1,0:T(8,128)S(1)} %get-tuple-element.56.log_share_ref, ...), custom_call_target="tpu_custom_call" | custom-call | tf_op jit(solution)/shard_map/pallas_call | solution.py:61
  72.8 14.5 %all_to_all.26.terms_ref = f32[32,16,128]{2,1,0:T(8,128)S(1)} all-to-all(f32[32,16,128]{2,1,0:T(8,128)S(1)} %get-tuple-element.61), channel_id=1, replica_groups=mesh['z'=8,'y'=4,'core'=2,'xh'=2,'xl'=2] {'z','y'}, dimensions={0} | all-to-all | bytes 524288 | tf_op jit(solution)/shard_map/all_to_all | solution.py:348
  87.4 13.1 %shard_map.80 = (f32[8,2,16,128]{3,2,1,0:T(8,128)S(1)}, f32[2,16,128]{2,1,0:T(8,128)S(1)}) custom-call(s32[1,1]{1,0:T(1,128)} %get-tuple-element.53.safe_ref, f32[32,16,128]{2,1,0:T(8,128)S(1)} %all_to_all.26.terms_ref, f32[2,16,128]{2,1,0:T(8,128)S(1)} %get-tuple-element.62.column_ref, f32[2048,2048]{1,0:T(8,128)S(1)} %get-tuple-element.59.gibbs_ref, ...), custom_call_target="tpu_custom_call" | custom-call | tf_op jit(solution)/shard_map/pallas_call | solution.py:61
  100.5 10.1 %all_to_all.27.got_ref = f32[8,2,16,128]{3,2,1,0:T(8,128)S(1)} all-to-all(f32[8,2,16,128]{3,2,1,0:T(8,128)S(1)} %get-tuple-element.63), channel_id=1, replica_groups=mesh['z'=8,'y'=4,'core'=2,'xh'=2,'xl'=2] {'xh','xl','core'}, dimensions={0} | all-to-all | bytes 262144 | tf_op jit(solution)/shard_map/all_to_all | solution.py:348
  110.5 16.6 %shard_map.81 = (f32[32,16,128]{2,1,0:T(8,128)S(1)}, f32[2,16,128]{2,1,0:T(8,128)S(1)}, f32[8,128]{1,0:T(8,128)}) custom-call(s32[1,1]{1,0:T(1,128)} %get-tuple-element.53.safe_ref, s32[3]{0:T(128)S(1)} %pad_add_fusion.place_ref, f32[2,1,128]{2,1,0:T(1,128)S(1)} %get-tuple-element.55.mix_ref, f32[2,16,128]{2,1,0:T(8,128)S(1)} %get-tuple-element.56.log_share_ref, ...), custom_call_target="tpu_custom_call" | custom-call | tf_op jit(solution)/shard_map/pallas_call | solution.py:61
  127.2 14.8 %all_to_all.28.terms_ref = f32[32,16,128]{2,1,0:T(8,128)S(1)} all-to-all(f32[32,16,128]{2,1,0:T(8,128)S(1)} %get-tuple-element.66), channel_id=1, replica_groups=mesh['z'=8,'y'=4,'core'=2,'xh'=2,'xl'=2] {'z','y'}, dimensions={0} | all-to-all | bytes 524288 | tf_op jit(solution)/shard_map/all_to_all | solution.py:348
  141.9 0.6 shard_map.82
  142.5 1.0 collective-permute-start.5
  143.5 4.7 %collective-permute-start.6 = (f32[32,128]{1,0:T(8,128)S(1)}, f32[32,128]{1,0:T(8,128)S(1)}, u32[]{:S(2)}, u32[]{:S(2)}) collective-permute-start(f32[32,128]{1,0:T(8,128)S(1)} %get-tuple-element.70), channel_id=1, source_target_pairs={{0,6},{2,4},{4,2},{6,0},{1,7},{3,5},{5,3},{7,1},{8,14},{10,12},{12... | collective-permute-start | bytes 49160 | tf_op jit(solution)/shard_map/ppermute | solution.py:352
  148.2 0.0 collective-permute-start.4
  148.2 0.0 collective-permute-done.5.far_ref
  148.2 1.7 %collective-permute-done.6.cross_ref = f32[32,128]{1,0:T(8,128)S(1)} collective-permute-done((f32[32,128]{1,0:T(8,128)S(1)}, f32[32,128]{1,0:T(8,128)S(1)}, u32[]{:S(2)}, u32[]{:S(2)}) %collective-permute-start.6) | collective-permute-done | bytes 16416 | tf_op jit(solution)/shard_map/ppermute | solution.py:352
  149.9 0.0 collective-permute-done.4.core_ref
  149.9 1.2 shard_map.83
  (2 shorter events, 0.0 us)
Async XLA Ops:
  0.6 22.9 %copy-start = (bf16[32,8192]{1,0:T(8,128)(2,1)S(1)}, bf16[32,8192]{1,0:T(8,128)(2,1)}, u32[]{:S(2)}) copy-start(bf16[32,8192]{1,0:T(8,128)(2,1)} %param.8) | copy-start | bytes 1572868
  0.6 0.7 copy-start.3
  2.2 21.4 %collective-permute-start.3 = (f32[1,1024]{1,0:T(1,128)}, f32[1,1024]{1,0:T(1,128)S(1)}, u32[]{:S(2)}, u32[]{:S(2)}) collective-permute-start(f32[1,1024]{1,0:T(1,128)} %demand_ref), channel_id=1, source_target_pairs={{0,6},{2,4},{4,2},{6,0},{1,7},{3,5},{5,3},{7,1},{8,14},{10,12},{12... | collective-permute-start | bytes 12296 | tf_op jit(solution)/shard_map/ppermute | solution.py:352
  6.4 17.2 %collective-permute-start.2 = (f32[1,1024]{1,0:T(1,128)}, f32[1,1024]{1,0:T(1,128)S(1)}, u32[]{:S(2)}, u32[]{:S(2)}) collective-permute-start(f32[1,1024]{1,0:T(1,128)} %demand_ref), channel_id=1, source_target_pairs={{0,2},{2,0},{4,6},{6,4},{1,3},{3,1},{5,7},{7,5},{8,10},{10,8},{12,... | collective-permute-start | bytes 12296 | tf_op jit(solution)/shard_map/ppermute | solution.py:352
  8.3 15.3 %collective-permute-start.1 = (f32[1,1024]{1,0:T(1,128)}, f32[1,1024]{1,0:T(1,128)S(1)}, u32[]{:S(2)}, u32[]{:S(2)}) collective-permute-start(f32[1,1024]{1,0:T(1,128)} %demand_ref), channel_id=1, source_target_pairs={{0,4},{2,6},{4,0},{6,2},{1,5},{3,7},{5,1},{7,3},{8,12},{10,14},{12... | collective-permute-start | bytes 12296 | tf_op jit(solution)/shard_map/ppermute | solution.py:352
  8.3 25.8 %all-to-all-start = ((bf16[256,2,128]{2,1,0:T(2,128)(2,1)}), bf16[256,2,128]{2,1,0:T(2,128)(2,1)S(1)}, u32[]{:S(2)}, u32[]{:S(2)}) async-start(bf16[256,2,128]{2,1,0:T(2,128)(2,1)} %shard_map.76), calls=%async_computation | async-start | bytes 262144 | tf_op jit(solution)/shard_map/all_to_all | solution.py:348
  21.3 3.3 %collective-permute-start = (f32[1,8192]{1,0:T(1,128)}, f32[1,8192]{1,0:T(1,128)S(1)}, u32[]{:S(2)}, u32[]{:S(2)}) collective-permute-start(f32[1,8192]{1,0:T(1,128)} %pot_ref), channel_id=1, source_target_pairs={{0,4},{2,6},{4,0},{6,2},{1,5},{3,7},{5,1},{7,3},{8,12},{10,14},{12... | collective-permute-start | bytes 98312 | tf_op jit(solution)/shard_map/ppermute | solution.py:352
  24.6 0.8 copy-start.1
  25.3 0.7 copy-start.2
  26.0 0.7 copy-start.4
  142.5 5.7 %collective-permute-start.5 = (f32[32,128]{1,0:T(8,128)S(1)}, f32[32,128]{1,0:T(8,128)S(1)}, u32[]{:S(2)}, u32[]{:S(2)}) collective-permute-start(f32[32,128]{1,0:T(8,128)S(1)} %get-tuple-element.69.own_ref), channel_id=1, source_target_pairs={{0,2},{2,0},{4,6},{6,4},{1,3},{3,1},{5,7},{7,5},{8,10},{10,8},{12,... | collective-permute-start | bytes 49160 | tf_op jit(solution)/shard_map/ppermute | solution.py:352
  143.5 6.4 %collective-permute-start.6 = (f32[32,128]{1,0:T(8,128)S(1)}, f32[32,128]{1,0:T(8,128)S(1)}, u32[]{:S(2)}, u32[]{:S(2)}) collective-permute-start(f32[32,128]{1,0:T(8,128)S(1)} %get-tuple-element.70), channel_id=1, source_target_pairs={{0,6},{2,4},{4,2},{6,0},{1,7},{3,5},{5,3},{7,1},{8,14},{10,12},{12... | collective-permute-start | bytes 49160 | tf_op jit(solution)/shard_map/ppermute | solution.py:352
  148.2 1.7 %collective-permute-start.4 = (f32[32,128]{1,0:T(8,128)S(1)}, f32[32,128]{1,0:T(8,128)S(1)}, u32[]{:S(2)}, u32[]{:S(2)}) collective-permute-start(f32[32,128]{1,0:T(8,128)S(1)} %get-tuple-element.70), channel_id=1, source_target_pairs={{0,4},{2,6},{4,0},{6,2},{1,5},{3,7},{5,1},{7,3},{8,12},{10,14},{12... | collective-permute-start | bytes 49160 | tf_op jit(solution)/shard_map/ppermute | solution.py:352

commit v5 on v4

--- a/solution.py
+++ b/solution.py
@@ -23,6 +23,7 @@
 LANE = 128
 VMEM = pl.BlockSpec(memory_space=pltpu.VMEM)
 SMEM = pl.BlockSpec(memory_space=pltpu.SMEM)
+HBM = pl.BlockSpec(memory_space=pltpu.HBM)
 
 
 def diagonal():
@@ -51,17 +52,19 @@
     lax.fori_loop(0, steps // by, several, 0)
 
 
+def in_hbm(value):
+    return pltpu.with_memory_space_constraint(value, pltpu.HBM)
+
+
 def call(kernel, outs, *args, scratch=(), limit=16, apart=()):
     def spec(a):
-        if any(a is one for one in apart):
-            return pl.BlockSpec(memory_space=pltpu.HBM)
         return SMEM if a.dtype == jnp.int32 else VMEM
 
     outs = tuple(jax.ShapeDtypeStruct(*o) for o in outs)
     return pl.pallas_call(
         kernel,
         out_shape=outs,
-        in_specs=[spec(a) for a in args],
+        in_specs=[HBM if k in apart else spec(a) for k, a in enumerate(args)],
         out_specs=tuple(spec(o) for o in outs),
         scratch_shapes=[pltpu.VMEM(s, F32) if isinstance(s, tuple) else s for s in scratch],
         compiler_params=pltpu.CompilerParams(vmem_limit_bytes=limit << 20),
@@ -84,23 +87,21 @@
 
 
 def prep_kernel(
-    place_ref, site_ref, pot_ref, core_pot_ref, demand_ref, core_demand_ref, far_demand_ref, cross_demand_ref,
-    weight_ref, sites_ref, site_norm_ref, site_top_ref, level_ref, part_ref, log_share_ref, mix_ref,
-    quarter_ref, share_ref, weights_ref, sems,
+    place_ref, site_ref, pot_ref, core_pot_ref, weight_ref, demand_ref,
+    sites_ref, site_norm_ref, site_top_ref, level_ref, part_ref, mix_ref, share_ref, spot_ref,
+    quarter_ref, weights_ref, line_ref, sems,
 ):
-    n_sites = site_ref.shape[1]
+    width = sites_ref.shape[0]
+    depth, n_sites = site_ref.shape
     core, far = place_ref[1], place_ref[2]
     here = pl.ds(pl.multiple_of((2 * far + core) * n_sites, n_sites), n_sites)
     copies = [
-        pltpu.make_async_copy(source, target, sems.at[k])
-        for k, (source, target) in enumerate(
-            ((pot_ref.at[:, here], quarter_ref), (demand_ref, share_ref), (weight_ref, weights_ref))
-        )
+        pltpu.make_async_copy(pot_ref.at[:, here], quarter_ref, sems.at[0]),
+        pltpu.make_async_copy(weight_ref, weights_ref, sems.at[1]),
+        pltpu.make_async_copy(demand_ref, line_ref, sems.at[2]),
     ]
     for copy in copies:
         copy.start()
-    width = sites_ref.shape[0]
-    depth, n_sites = site_ref.shape
     site = site_ref[...]
     wide = site.astype(F32)
     site_norm = jnp.sum(wide * wide, axis=0, keepdims=True)
@@ -116,33 +117,26 @@
     ).astype(BF16)
     for copy in copies:
         copy.wait()
-
-    def by_core(own, other):
-        return jnp.where(core == 0, own, other), jnp.where(core == 0, other, own)
-
-    for s, line in enumerate(by_core(quarter_ref[...], core_pot_ref[:, here])):
+    for s, line in enumerate(by_core(core, quarter_ref[...], core_pot_ref[:, here])):
         for b in range(n_sites // LANE):
             level_ref[s, b : b + 1, :] = line[:, b * LANE : (b + 1) * LANE]
     level = level_ref[...] * (1.0 / EPS) - site_norm_ref[...][None]
     level_ref[...] = level
     part_ref[...] = jnp.exp(level - overall(jnp.max, level))
-    near = by_core(share_ref[...], core_demand_ref[...])
-    away = by_core(far_demand_ref[...], cross_demand_ref[...])
-    half = log_share_ref.shape[1] // 2
-    for s in range(2):
-        first = jnp.where(far == 0, near[s], away[s])
-        second = jnp.where(far == 0, away[s], near[s])
-        for b in range(half):
-            log_share_ref[s, b : b + 1, :] = first[:, b * LANE : (b + 1) * LANE]
-            log_share_ref[s, half + b : half + b + 1, :] = second[:, b * LANE : (b + 1) * LANE]
-    demand = log_share_ref[...]
-    log_share_ref[...] = jnp.log(demand) - jnp.log(overall(jnp.sum, demand))
+    for k, bit in enumerate((core, far)):
+        spot_ref[k] = jnp.full(spot_ref.shape[1:], bit, jnp.int32).astype(F32)
+    for b in range(share_ref.shape[0]):
+        share_ref[b : b + 1, :] = line_ref[:, b * LANE : (b + 1) * LANE]
     weight = weights_ref[...]
     which = lax.broadcasted_iota(jnp.int32, weight.shape, 1)
     total = jnp.sum(weight, axis=1, keepdims=True)
     for s in range(2):
         own = jnp.sum(jnp.where(which == 2 * place_ref[0] + s, weight, 0.0), axis=1, keepdims=True)
         mix_ref[s] = jnp.broadcast_to(own / total, mix_ref.shape[1:])
+
+
+def by_core(core, own, other):
+    return jnp.where(core == 0, own, other), jnp.where(core == 0, other, own)
 
 
 def overall(reduce, value):
@@ -159,7 +153,7 @@
 
 
 def build_kernel(
-    feat_ref, sites_ref, site_top_ref, level_ref, part_ref,
+    feat_ref, sites_ref, site_top_ref, level_ref, part_ref, share_ref,
     gibbs_ref, cells_ref, cell_norm_ref, safe_ref, send_ref, out_ref, sum_ref,
 ):
     n_cells, width = cells_ref.shape
@@ -186,7 +180,7 @@
         jnp.where(own, norm, 0.0).reshape(n_cells // LANE, group, LANE), axis=1
     ) / (depth * EPS)
     safe = jnp.max(norm) * jnp.max(site_top_ref[...]) <= SAFE_NORMS
-    safe_ref[0, 0] = jnp.where(safe, 1, 0)
+    safe_ref[...] = jnp.full(safe_ref.shape, jnp.where(safe, 1.0, 0.0), F32)
 
     @pl.when(safe)
     def _():
@@ -229,7 +223,9 @@
             cells_ref[i * rows_blk : (i + 1) * rows_blk, :] = cell_rows(i, feat_ref[...], rows_blk, per_row)
         log_domain(level_ref[...], cells_ref, sites_ref, out_ref, True)
 
-    send_ref[...] = jnp.broadcast_to(out_ref[...][None], send_ref.shape)
+    flat = out_ref.shape[0] * out_ref.shape[1]
+    send_ref[:, :flat, :] = jnp.broadcast_to(out_ref[...].reshape(1, flat, LANE), (send_ref.shape[0], flat, LANE))
+    send_ref[:, flat:, :] = jnp.broadcast_to(share_ref[...][None], (send_ref.shape[0], *share_ref.shape))
 
 
 def log_domain(level, cells_ref, sites_ref, out_ref, over_sites):
@@ -302,46 +298,60 @@
 ):
     level = jnp.sum(terms_ref[...], axis=0)[None] - column_ref[...]
     level_ref[...] = level
-    log_sums(safe_ref[0, 0] == 1, level, gibbs_ref, cells_ref, sites_ref, out_ref, part_ref, None, True)
+    log_sums(jnp.max(safe_ref[...]) > 0.5, level, gibbs_ref, cells_ref, sites_ref, out_ref, part_ref, None, True)
     send_ref[...] = jnp.broadcast_to(out_ref[...][None], send_ref.shape)
 
 
-def column_kernel(
-    safe_ref, place_ref, mix_ref, log_share_ref, got_ref, cell_norm_ref, level_ref, gibbs_ref, cells_ref, sites_ref,
+def over_peers(got):
+    top = jnp.max(got, axis=0)
+    return top + jnp.log(jnp.sum(jnp.exp(got - top[None]), axis=0))
+
+
+def send_term(mix_ref, level_ref, column_ref, send_ref):
+    term = mix_ref[0] * (level_ref[0] + column_ref[0]) + mix_ref[1] * (level_ref[1] + column_ref[1])
+    send_ref[...] = jnp.broadcast_to(term[None], send_ref.shape)
+
+
+def first_column_kernel(
+    safe_ref, mix_ref, got_ref, level_ref, gibbs_ref, cells_ref, sites_ref,
+    send_ref, column_ref, log_share_ref, part_ref, sum_ref,
+):
+    on_cells = log_share_ref.shape
+    flat = on_cells[0] * on_cells[1]
+    near, away = 0, got_ref.shape[0] // 2
+    for s in range(2):
+        log_share_ref[s] = jnp.concatenate([got_ref[near + s, flat:, :], got_ref[away + s, flat:, :]], axis=0)
+    demand = log_share_ref[...]
+    log_share = jnp.log(demand) - jnp.log(overall(jnp.sum, demand))
+    log_share_ref[...] = log_share
+    down = log_share - over_peers(got_ref[:, :flat, :]).reshape(on_cells)
+    log_sums(jnp.max(safe_ref[...]) > 0.5, down, gibbs_ref, cells_ref, sites_ref, column_ref, part_ref, sum_ref, False)
+    send_term(mix_ref, level_ref, column_ref, send_ref)
+
+
+def next_column_kernel(
+    safe_ref, spot_ref, mix_ref, log_share_ref, got_ref, cell_norm_ref, level_ref, gibbs_ref, cells_ref, sites_ref,
     send_ref, column_ref, row_pot_ref, part_ref, sum_ref,
 ):
     half = row_pot_ref.shape[0]
-    got = got_ref[...]
-    top = jnp.max(got, axis=0)
-    row = top + jnp.log(jnp.sum(jnp.exp(got - top[None]), axis=0))
-    down = log_share_ref[...] - row
-    own = jnp.where(place_ref[1] == 0, down[0], down[1])
+    down = log_share_ref[...] - over_peers(got_ref[...])
+    own = jnp.where(spot_ref[0] == 0.0, down[0], down[1])
     norm = cell_norm_ref[...]
-    first = place_ref[2] == 0
+    first = spot_ref[1] == 0.0
     row_pot_ref[...] = EPS * (jnp.where(first, own[:half], own[half:]) + jnp.where(first, norm[:half], norm[half:]))
-    log_sums(safe_ref[0, 0] == 1, down, gibbs_ref, cells_ref, sites_ref, column_ref, part_ref, sum_ref, False)
-    term = mix_ref[0] * (level_ref[0] + column_ref[0]) + mix_ref[1] * (level_ref[1] + column_ref[1])
-    send_ref[...] = jnp.broadcast_to(term[None], send_ref.shape)
-
-
-def last_kernel(place_ref, terms_ref, column_ref, site_norm_ref, own_ref, other_ref):
+    log_sums(jnp.max(safe_ref[...]) > 0.5, down, gibbs_ref, cells_ref, sites_ref, column_ref, part_ref, sum_ref, False)
+    send_term(mix_ref, level_ref, column_ref, send_ref)
+
+
+def last_kernel(spot_ref, terms_ref, column_ref, site_norm_ref, own_ref, other_ref):
     n_blocks = site_norm_ref.shape[0]
     log_bary = jnp.sum(terms_ref[...], axis=0)
     potential = EPS * (log_bary[None] - column_ref[...] + site_norm_ref[...][None])
-    first = place_ref[1] == 0
+    first = spot_ref[0] == 0.0
     own_ref[:n_blocks, :] = jnp.where(first, potential[0], potential[1])
     other_ref[:n_blocks, :] = jnp.where(first, potential[1], potential[0])
     own_ref[n_blocks:, :] = log_bary
     other_ref[n_blocks:, :] = log_bary
-
-
-def join_kernel(place_ref, own_ref, core_ref, far_ref, cross_ref, pot_ref, log_bary_ref):
-    n_blocks = own_ref.shape[0] // 2
-    here = 2 * place_ref[2] + place_ref[1]
-    for flip, ref in enumerate((own_ref, core_ref, far_ref, cross_ref)):
-        at = block_at(here ^ flip, n_blocks)
-        pot_ref[at, :] = ref[:n_blocks, :]
-        log_bary_ref[at, :] = ref[n_blocks:, :]
 
 
 def exchange(value, axes):
@@ -369,13 +379,10 @@
     feat = exchange(packed, CELL_ORDER)
     feat = feat.reshape(n_all, width)
     core_pot = swapped(start_potential, CORE)
-    core_demand = swapped(demand, CORE)
-    far_demand = swapped(demand, FAR)
-    cross_demand = swapped(demand, CROSS)
     own_sites = lax.dynamic_slice_in_dim(site_feat, quarter * n_sites, n_sites, 1)
     weight = weights.reshape(1, -1)
     on_cells, on_sites = (2, cell_blocks, LANE), (2, site_blocks, LANE)
-    sites, site_norm, site_top, level, part, log_share, mix = call(
+    sites, site_norm, site_top, level, part, mix, share, spot = call(
         prep_kernel,
         [
             ((width, n_sites), BF16),
@@ -383,16 +390,16 @@
             ((8, LANE), F32),
             (on_sites, F32),
             (on_sites, F32),
-            (on_cells, F32),
+            ((2, 1, LANE), F32),
+            ((cell_blocks // 2, LANE), F32),
             ((2, 1, LANE), F32),
         ],
-        place, own_sites, start_potential, core_pot, demand, core_demand, far_demand, cross_demand,
-        weight,
-        scratch=[(1, n_sites), demand.shape, weight.shape, pltpu.SemaphoreType.DMA((3,))],
-        apart=(start_potential, demand, weight),
-    )
-    feat, sites, site_norm, site_top, level, part, log_share, mix, place = lax.optimization_barrier(
-        (feat, sites, site_norm, site_top, level, part, log_share, mix, place)
+        place, own_sites, in_hbm(start_potential), core_pot, in_hbm(weight), in_hbm(demand),
+        scratch=[(1, n_sites), weight.shape, demand.shape, pltpu.SemaphoreType.DMA((3,))],
+        apart=(2, 4, 5),
+    )
+    feat, sites, site_norm, site_top, level, part, mix, share, spot = lax.optimization_barrier(
+        (feat, sites, site_norm, site_top, level, part, mix, share, spot)
     )
     row_outs = [((n_row, *on_cells), F32), (on_sites, F32)]
     row_scratch = [on_cells, on_sites]
@@ -402,30 +409,37 @@
             ((n_cells, n_sites), F32),
             ((n_cells, width), BF16),
             ((cell_blocks, LANE), F32),
-            ((1, 1), jnp.int32),
-            row_outs[0],
+            ((8, LANE), F32),
+            ((n_row, 2 * cell_blocks + cell_blocks // 2, LANE), F32),
         ],
-        feat, sites, site_top, level, part, scratch=[on_cells, (2, n_cells, LANE)], limit=24,
+        feat, sites, site_top, level, part, share, scratch=[on_cells, (2, n_cells, LANE)], limit=24,
     )
     for repeat in range(ITERS):
         got = exchange(send, ROW_GROUP)
-        send, column, row_pot = call(
-            column_kernel,
-            [((n_bary, site_blocks, LANE), F32), (on_sites, F32), ((cell_blocks // 2, LANE), F32)],
-            safe, place, mix, log_share, got, cell_norm, level, gibbs, cells, sites,
-            scratch=[on_cells, (2, site_blocks, 8, LANE)],
-        )
+        column_outs = [((n_bary, site_blocks, LANE), F32), (on_sites, F32)]
+        column_scratch = [on_cells, (2, site_blocks, 8, LANE)]
+        if repeat == 0:
+            send, column, log_share = call(
+                first_column_kernel, [*column_outs, (on_cells, F32)],
+                safe, mix, got, level, gibbs, cells, sites, scratch=column_scratch,
+            )
+        else:
+            send, column, row_pot = call(
+                next_column_kernel, [*column_outs, ((cell_blocks // 2, LANE), F32)],
+                safe, spot, mix, log_share, got, cell_norm, level, gibbs, cells, sites, scratch=column_scratch,
+            )
         terms = exchange(send, BARY_GROUP)
         if repeat < ITERS - 1:
             send, level = call(
                 next_row_kernel, row_outs, safe, terms, column, gibbs, cells, sites, scratch=row_scratch
             )
     message = ((2 * site_blocks, LANE), F32)
-    own, other = call(last_kernel, [message] * 2, place, terms, column, site_norm)
-    whole = ((n_home * site_blocks, LANE), F32)
-    potential, log_bary = call(
-        join_kernel, [whole] * 2, place, own, swapped(other, CORE), swapped(own, FAR), swapped(other, CROSS)
-    )
+    own, other = call(last_kernel, [message] * 2, spot, terms, column, site_norm)
+    pieces = (own, swapped(other, CORE), swapped(own, FAR), swapped(other, CROSS))
+    here = lax.axis_index(HOME_GROUP)
+    ordered = [lax.select_n(here ^ k, *pieces) for k in range(n_home)]
+    potential = jnp.stack([piece[:site_blocks] for piece in ordered])
+    log_bary = jnp.stack([piece[site_blocks:] for piece in ordered])
     return row_pot.reshape(1, -1), potential.reshape(1, -1), log_bary.reshape(-1)
 
 

time: 152 us -> 145 us (0.954)
  starting transfers between devices: 26.9 us -> 21.5 us
  Pallas kernels: 63.7 us -> 58.8 us
  waiting for transfers between devices: 9.02 us -> 13.5 us
  local copies, waits for them, and re-layouts: 2.87 us -> 0.79 us
    ppermute x7 -> x4, starting transfers between devices: 14 us -> 8.96 us  [swapped(): return lax.ppermute(value, SWAP_GROUP, [(k, k ^ flip) for k in range(4)])]
    pallas_call x8 -> x7, Pallas kernels: 63.7 us -> 58.8 us  [call(): pl.pallas_call(kernel, out_shape=outs, in_specs=[HBM if k in apart else s...]
    all_to_all x1, waiting for transfers between devices: 6.34 us -> 11.1 us  [exchange(): return lax.all_to_all(value, axes, split_axis=0, concat_axis=0, tiled=True)]
    unnamed x11 -> x5, local copies, waits for them, and re-layouts: 2.86 us -> 0.76 us
  transfers between devices with their start and end apart: 8 -> 5, of which waited for: 3 -> 3; matrix products, arithmetic and copies ran while one was open for 0% -> 0% of each run, Pallas kernels for 1% -> 1%
where the time goes in v5:
time: 145 us
  Pallas kernels  58.8 us (41%)
  blocking collectives  48 us (33%)
  starting transfers between devices  21.5 us (15%)
  waiting for transfers between devices  13.5 us (9%)
    pallas_call x7, Pallas kernels, call(): pl.pallas_call(kernel, out_shape=outs, in_specs=[HBM if k in apart else s...  58.8 us
    all_to_all x4, blocking collectives, exchange(): return lax.all_to_all(value, axes, split_axis=0, concat_axis=0, tiled=True)  48 us
    all_to_all x1, starting transfers between devices, exchange(): return lax.all_to_all(value, axes, split_axis=0, concat_axis=0, tiled=True)  12.6 us
    all_to_all x1, waiting for transfers between devices, exchange(): return lax.all_to_all(value, axes, split_axis=0, concat_axis=0, tiled=True)  11.1 us
    ppermute x4, starting transfers between devices, swapped(): return lax.ppermute(value, SWAP_GROUP, [(k, k ^ flip) for k in range(4)])  8.96 us
  transfers between devices with their start and end apart: 5, of which 3 were waited for; matrix products, arithmetic and copies ran while one was open for 0% of the time, Pallas kernels for 1%

profile of v5, /device:TPU:1, one launch (start us, length us, event | category | flops | bytes accessed | tf_op | source)
XLA Modules:
  0.0 144.7 jit_solution(17336747861552501374)
XLA Ops:
  0.6 0.0 copy-start
  0.6 0.0 copy-start.1
  0.7 0.7 copy-done.1
  1.4 0.9 shard_map.76
  2.2 3.2 %collective-permute-start = (f32[1,8192]{1,0:T(1,128)}, f32[1,8192]{1,0:T(1,128)S(1)}, u32[]{:S(2)}, u32[]{:S(2)}) collective-permute-start(f32[1,8192]{1,0:T(1,128)} %pot_ref), channel_id=1, source_target_pairs={{0,4},{2,6},{4,0},{6,2},{1,5},{3,7},{5,1},{7,3},{8,12},{10,14},{12... | collective-permute-start | bytes 98312 | tf_op jit(solution)/shard_map/ppermute | solution.py:362
  5.4 12.6 %all-to-all-start = ((bf16[256,2,128]{2,1,0:T(2,128)(2,1)}), bf16[256,2,128]{2,1,0:T(2,128)(2,1)S(1)}, u32[]{:S(2)}, u32[]{:S(2)}) async-start(bf16[256,2,128]{2,1,0:T(2,128)(2,1)} %shard_map.76), calls=%async_computation | async-start | bytes 262144 | tf_op jit(solution)/shard_map/all_to_all | solution.py:358
  18.0 0.0 copy-done
  18.1 0.1 pad_add_fusion.place_ref
  18.1 0.0 collective-permute-done.core_pot_ref
  18.1 1.7 %shard_map.77 = (bf16[256,2048]{1,0:T(8,128)(2,1)S(1)}, f32[16,128]{1,0:T(8,128)S(1)}, f32[8,128]{1,0:T(8,128)S(1)}, f32[2,16,128]{2,1,0:T(8,128)S(1)}, f32[2,16...) custom-call(s32[3]{0:T(128)S(1)} %pad_add_fusion.place_ref, ...), custom_call_target="tpu_custom_call" | custom-call | tf_op jit(solution)/shard_map/pallas_call | solution.py:64
  19.8 11.1 %all-to-all-done = bf16[256,2,128]{2,1,0:T(2,128)(2,1)S(1)} async-done(((bf16[256,2,128]{2,1,0:T(2,128)(2,1)}), bf16[256,2,128]{2,1,0:T(2,128)(2,1)S(1)}, u32[]{:S(2)}, u32[]{:S(2)}) %all-to-all-start) | async-done | bytes 131104 | tf_op jit(solution)/shard_map/all_to_all | solution.py:358
  30.9 13.1 %shard_map.78 = (f32[2048,2048]{1,0:T(8,128)S(1)}, bf16[2048,256]{1,0:T(8,128)(2,1)S(1)}, f32[16,128]{1,0:T(8,128)S(1)}, f32[8,128]{1,0:T(8,128)S(1)}, f32[8,40,128]{2,1,0:T(8,128)S(1)}) custom-call(bf16[256,256]{1,0:T(8,128)(2,1)S(1)} %bitcast.28, bf16[256,2048]{1,0:T(8,128)(2,1)S(1)} %get-tuple-element.50.sites_ref, ...), custom_call_target="tpu_custom_call" | custom-call | tf_op jit(solution)/shard_map/pallas_call | solution.py:64
  44.1 8.7 %all_to_all.25.got_ref = f32[8,40,128]{2,1,0:T(8,128)S(1)} all-to-all(f32[8,40,128]{2,1,0:T(8,128)S(1)} %get-tuple-element.58), channel_id=1, replica_groups=mesh['z'=8,'y'=4,'core'=2,'xh'=2,'xl'=2] {'xh','xl','core'}, dimensions={0} | all-to-all | bytes 327680 | tf_op jit(solution)/shard_map/all_to_all | solution.py:358
  52.8 14.9 %shard_map.79 = (f32[32,16,128]{2,1,0:T(8,128)S(1)}, f32[2,16,128]{2,1,0:T(8,128)S(1)}, f32[2,16,128]{2,1,0:T(8,128)S(1)}) custom-call(f32[8,128]{1,0:T(8,128)S(1)} %get-tuple-element.55.safe_ref, f32[2,1,128]{2,1,0:T(1,128)S(1)} %get-tuple-element.57.mix_ref, f32[8,40,128]{2,1,0:T(8,128)S(1)} %all_to_all.25.got_ref, ...), custom_call_target="tpu_custom_call" | custom-call | tf_op jit(solution)/shard_map/pallas_call | solution.py:64
  67.7 14.3 %all_to_all.26.terms_ref = f32[32,16,128]{2,1,0:T(8,128)S(1)} all-to-all(f32[32,16,128]{2,1,0:T(8,128)S(1)} %get-tuple-element.62), channel_id=1, replica_groups=mesh['z'=8,'y'=4,'core'=2,'xh'=2,'xl'=2] {'z','y'}, dimensions={0} | all-to-all | bytes 524288 | tf_op jit(solution)/shard_map/all_to_all | solution.py:358
  82.0 12.5 %shard_map.80 = (f32[8,2,16,128]{3,2,1,0:T(8,128)S(1)}, f32[2,16,128]{2,1,0:T(8,128)S(1)}) custom-call(f32[8,128]{1,0:T(8,128)S(1)} %get-tuple-element.55.safe_ref, f32[32,16,128]{2,1,0:T(8,128)S(1)} %all_to_all.26.terms_ref, f32[2,16,128]{2,1,0:T(8,128)S(1)} %get-tuple-element.63.column_ref, f32[2048,2048]{1,0:T(8,128)S(1)} %get-tuple-element.59.gibbs_ref, ...), custom_call_target="tpu_custom_call" | custom-call | tf_op jit(solution)/shard_map/pallas_call | solution.py:64
  94.6 10.2 %all_to_all.27.got_ref = f32[8,2,16,128]{3,2,1,0:T(8,128)S(1)} all-to-all(f32[8,2,16,128]{3,2,1,0:T(8,128)S(1)} %get-tuple-element.64), channel_id=1, replica_groups=mesh['z'=8,'y'=4,'core'=2,'xh'=2,'xl'=2] {'xh','xl','core'}, dimensions={0} | all-to-all | bytes 262144 | tf_op jit(solution)/shard_map/all_to_all | solution.py:358
  104.7 15.7 %shard_map.81 = (f32[32,16,128]{2,1,0:T(8,128)S(1)}, f32[2,16,128]{2,1,0:T(8,128)S(1)}, f32[8,128]{1,0:T(8,128)}) custom-call(f32[8,128]{1,0:T(8,128)S(1)} %get-tuple-element.55.safe_ref, f32[2,1,128]{2,1,0:T(1,128)S(1)} %get-tuple-element.56.spot_ref, f32[2,1,128]{2,1,0:T(1,128)S(1)} %get-tuple-element.57.mix_ref, ...), custom_call_target="tpu_custom_call" | custom-call | tf_op jit(solution)/shard_map/pallas_call | solution.py:64
  120.4 14.8 %all_to_all.28.terms_ref = f32[32,16,128]{2,1,0:T(8,128)S(1)} all-to-all(f32[32,16,128]{2,1,0:T(8,128)S(1)} %get-tuple-element.68), channel_id=1, replica_groups=mesh['z'=8,'y'=4,'core'=2,'xh'=2,'xl'=2] {'z','y'}, dimensions={0} | all-to-all | bytes 524288 | tf_op jit(solution)/shard_map/all_to_all | solution.py:358
  135.3 2.5 %collective-permute-start.1 = (f32[32,128]{1,0:T(8,128)S(1)}, f32[32,128]{1,0:T(8,128)S(1)}, u32[]{:S(2)}, u32[]{:S(2)}) collective-permute-start(f32[32,128]{1,0:T(8,128)S(1)} %get-tuple-element.72), channel_id=1, source_target_pairs={{0,4},{2,6},{4,0},{6,2},{1,5},{3,7},{5,1},{7,3},{8,12},{10,14},{12... | collective-permute-start | bytes 49160 | tf_op jit(solution)/shard_map/ppermute | solution.py:362
  137.8 0.9 collective-permute-start.2
  138.7 2.3 %collective-permute-start.3 = (f32[32,128]{1,0:T(8,128)S(1)}, f32[32,128]{1,0:T(8,128)S(1)}, u32[]{:S(2)}, u32[]{:S(2)}) collective-permute-start(f32[32,128]{1,0:T(8,128)S(1)} %get-tuple-element.72), channel_id=1, source_target_pairs={{0,6},{2,4},{4,2},{6,0},{1,7},{3,5},{5,3},{7,1},{8,14},{10,12},{12... | collective-permute-start | bytes 49160 | tf_op jit(solution)/shard_map/ppermute | solution.py:362
  141.0 0.0 collective-permute-done.1
  141.0 0.9 collective-permute-done.2
  141.9 1.5 %collective-permute-done.3 = f32[32,128]{1,0:T(8,128)S(1)} collective-permute-done((f32[32,128]{1,0:T(8,128)S(1)}, f32[32,128]{1,0:T(8,128)S(1)}, u32[]{:S(2)}, u32[]{:S(2)}) %collective-permute-start.3) | collective-permute-done | bytes 16416 | tf_op jit(solution)/shard_map/ppermute | solution.py:362
  143.4 0.6 pad_maximum_fusion.1
  144.1 0.6 pad_maximum_fusion
  (6 shorter events, 0.1 us)
Async XLA Ops:
  0.6 17.4 %copy-start = (bf16[32,8192]{1,0:T(8,128)(2,1)S(1)}, bf16[32,8192]{1,0:T(8,128)(2,1)}, u32[]{:S(2)}) copy-start(bf16[32,8192]{1,0:T(8,128)(2,1)} %param.8) | copy-start | bytes 1572868
  0.6 0.7 copy-start.1
  2.2 15.9 %collective-permute-start = (f32[1,8192]{1,0:T(1,128)}, f32[1,8192]{1,0:T(1,128)S(1)}, u32[]{:S(2)}, u32[]{:S(2)}) collective-permute-start(f32[1,8192]{1,0:T(1,128)} %pot_ref), channel_id=1, source_target_pairs={{0,4},{2,6},{4,0},{6,2},{1,5},{3,7},{5,1},{7,3},{8,12},{10,14},{12... | collective-permute-start | bytes 98312 | tf_op jit(solution)/shard_map/ppermute | solution.py:362
  5.4 25.5 %all-to-all-start = ((bf16[256,2,128]{2,1,0:T(2,128)(2,1)}), bf16[256,2,128]{2,1,0:T(2,128)(2,1)S(1)}, u32[]{:S(2)}, u32[]{:S(2)}) async-start(bf16[256,2,128]{2,1,0:T(2,128)(2,1)} %shard_map.76), calls=%async_computation | async-start | bytes 262144 | tf_op jit(solution)/shard_map/all_to_all | solution.py:358
  135.3 5.8 %collective-permute-start.1 = (f32[32,128]{1,0:T(8,128)S(1)}, f32[32,128]{1,0:T(8,128)S(1)}, u32[]{:S(2)}, u32[]{:S(2)}) collective-permute-start(f32[32,128]{1,0:T(8,128)S(1)} %get-tuple-element.72), channel_id=1, source_target_pairs={{0,4},{2,6},{4,0},{6,2},{1,5},{3,7},{5,1},{7,3},{8,12},{10,14},{12... | collective-permute-start | bytes 49160 | tf_op jit(solution)/shard_map/ppermute | solution.py:362
  137.8 4.1 %collective-permute-start.2 = (f32[32,128]{1,0:T(8,128)S(1)}, f32[32,128]{1,0:T(8,128)S(1)}, u32[]{:S(2)}, u32[]{:S(2)}) collective-permute-start(f32[32,128]{1,0:T(8,128)S(1)} %get-tuple-element.71), channel_id=1, source_target_pairs={{0,2},{2,0},{4,6},{6,4},{1,3},{3,1},{5,7},{7,5},{8,10},{10,8},{12,... | collective-permute-start | bytes 49160 | tf_op jit(solution)/shard_map/ppermute | solution.py:362
  138.7 4.7 %collective-permute-start.3 = (f32[32,128]{1,0:T(8,128)S(1)}, f32[32,128]{1,0:T(8,128)S(1)}, u32[]{:S(2)}, u32[]{:S(2)}) collective-permute-start(f32[32,128]{1,0:T(8,128)S(1)} %get-tuple-element.72), channel_id=1, source_target_pairs={{0,6},{2,4},{4,2},{6,0},{1,7},{3,5},{5,3},{7,1},{8,14},{10,12},{12... | collective-permute-start | bytes 49160 | tf_op jit(solution)/shard_map/ppermute | solution.py:362

commit v6 on v5

--- a/solution.py
+++ b/solution.py
@@ -338,7 +338,7 @@
     own = jnp.where(spot_ref[0] == 0.0, down[0], down[1])
     norm = cell_norm_ref[...]
     first = spot_ref[1] == 0.0
-    row_pot_ref[...] = EPS * (jnp.where(first, own[:half], own[half:]) + jnp.where(first, norm[:half], norm[half:]))
+    row_pot_ref[...] = jnp.where(first, own[:half], own[half:]) + jnp.where(first, norm[:half], norm[half:])
     log_sums(jnp.max(safe_ref[...]) > 0.5, down, gibbs_ref, cells_ref, sites_ref, column_ref, part_ref, sum_ref, False)
     send_term(mix_ref, level_ref, column_ref, send_ref)
 
@@ -435,12 +435,11 @@
             )
     message = ((2 * site_blocks, LANE), F32)
     own, other = call(last_kernel, [message] * 2, spot, terms, column, site_norm)
+    own, other, here, row_pot = lax.optimization_barrier((own, other, quarter, row_pot))
     pieces = (own, swapped(other, CORE), swapped(own, FAR), swapped(other, CROSS))
-    here = lax.axis_index(HOME_GROUP)
-    ordered = [lax.select_n(here ^ k, *pieces) for k in range(n_home)]
-    potential = jnp.stack([piece[:site_blocks] for piece in ordered])
-    log_bary = jnp.stack([piece[site_blocks:] for piece in ordered])
-    return row_pot.reshape(1, -1), potential.reshape(1, -1), log_bary.reshape(-1)
+    ordered = lax.optimization_barrier(jnp.stack([lax.select_n(here ^ k, *pieces) for k in range(n_home)]))
+    potential, log_bary = ordered[:, :site_blocks], ordered[:, site_blocks:]
+    return EPS * row_pot.reshape(1, -1), potential.reshape(1, -1), log_bary.reshape(-1)
 
 
 def solution(mesh):

time: 145 us -> 143 us (0.986)
  waiting for transfers between devices: 13.5 us -> 10.4 us
  starting transfers between devices: 21.5 us -> 23.3 us
    all_to_all x1, waiting for transfers between devices: 11.1 us -> 7.92 us  [exchange(): return lax.all_to_all(value, axes, split_axis=0, concat_axis=0, tiled=True)]
    all_to_all x1, starting transfers between devices: 12.6 us -> 15.6 us  [exchange(): return lax.all_to_all(value, axes, split_axis=0, concat_axis=0, tiled=True)]
where the time goes in v6:
time: 143 us
  Pallas kernels  58.3 us (41%)
  blocking collectives  48 us (34%)
  starting transfers between devices  23.3 us (16%)
  waiting for transfers between devices  10.4 us (7%)
    pallas_call x7, Pallas kernels, call(): pl.pallas_call(kernel, out_shape=outs, in_specs=[HBM if k in apart else s...  58.3 us
    all_to_all x4, blocking collectives, exchange(): return lax.all_to_all(value, axes, split_axis=0, concat_axis=0, tiled=True)  48 us
    all_to_all x1, starting transfers between devices, exchange(): return lax.all_to_all(value, axes, split_axis=0, concat_axis=0, tiled=True)  15.6 us
    all_to_all x1, waiting for transfers between devices, exchange(): return lax.all_to_all(value, axes, split_axis=0, concat_axis=0, tiled=True)  7.92 us
    ppermute x4, starting transfers between devices, swapped(): return lax.ppermute(value, SWAP_GROUP, [(k, k ^ flip) for k in range(4)])  7.62 us
  transfers between devices with their start and end apart: 5, of which 3 were waited for; matrix products, arithmetic and copies ran while one was open for 0% of the time, Pallas kernels for 1%

profile of v6, /device:TPU:1, one launch (start us, length us, event | category | flops | bytes accessed | tf_op | source)
XLA Modules:
  0.0 142.7 jit_solution(13529485801304530049)
XLA Ops:
  0.6 0.0 copy-start
  0.6 0.0 copy-start.1
  0.7 0.7 copy-done.1
  1.4 0.9 shard_map.76
  2.2 15.6 %all-to-all-start = ((bf16[256,2,128]{2,1,0:T(2,128)(2,1)}), bf16[256,2,128]{2,1,0:T(2,128)(2,1)S(1)}, u32[]{:S(2)}, u32[]{:S(2)}) async-start(bf16[256,2,128]{2,1,0:T(2,128)(2,1)} %shard_map.76), calls=%async_computation | async-start | bytes 262144 | tf_op jit(solution)/shard_map/all_to_all | solution.py:358
  17.9 2.2 %collective-permute-start = (f32[1,8192]{1,0:T(1,128)}, f32[1,8192]{1,0:T(1,128)S(1)}, u32[]{:S(2)}, u32[]{:S(2)}) collective-permute-start(f32[1,8192]{1,0:T(1,128)} %pot_ref), channel_id=1, source_target_pairs={{0,4},{2,6},{4,0},{6,2},{1,5},{3,7},{5,1},{7,3},{8,12},{10,14},{12... | collective-permute-start | bytes 98312 | tf_op jit(solution)/shard_map/ppermute | solution.py:362
  20.1 0.0 copy-done
  20.1 0.1 pad_add_fusion.place_ref
  20.2 1.0 collective-permute-done.core_pot_ref
  21.2 1.6 %shard_map.77 = (bf16[256,2048]{1,0:T(8,128)(2,1)S(1)}, f32[16,128]{1,0:T(8,128)S(1)}, f32[8,128]{1,0:T(8,128)S(1)}, f32[2,16,128]{2,1,0:T(8,128)S(1)}, f32[2,16...) custom-call(s32[3]{0:T(128)S(1)} %pad_add_fusion.place_ref, ...), custom_call_target="tpu_custom_call" | custom-call | tf_op jit(solution)/shard_map/pallas_call | solution.py:64
  22.9 7.9 %all-to-all-done = bf16[256,2,128]{2,1,0:T(2,128)(2,1)S(1)} async-done(((bf16[256,2,128]{2,1,0:T(2,128)(2,1)}), bf16[256,2,128]{2,1,0:T(2,128)(2,1)S(1)}, u32[]{:S(2)}, u32[]{:S(2)}) %all-to-all-start) | async-done | bytes 131104 | tf_op jit(solution)/shard_map/all_to_all | solution.py:358
  30.8 13.1 %shard_map.78 = (f32[2048,2048]{1,0:T(8,128)S(1)}, bf16[2048,256]{1,0:T(8,128)(2,1)S(1)}, f32[16,128]{1,0:T(8,128)S(1)}, f32[8,128]{1,0:T(8,128)S(1)}, f32[8,40,128]{2,1,0:T(8,128)S(1)}) custom-call(bf16[256,256]{1,0:T(8,128)(2,1)S(1)} %bitcast.20, bf16[256,2048]{1,0:T(8,128)(2,1)S(1)} %get-tuple-element.55.sites_ref, ...), custom_call_target="tpu_custom_call" | custom-call | tf_op jit(solution)/shard_map/pallas_call | solution.py:64
  44.0 8.7 %all_to_all.25.got_ref = f32[8,40,128]{2,1,0:T(8,128)S(1)} all-to-all(f32[8,40,128]{2,1,0:T(8,128)S(1)} %get-tuple-element.62), channel_id=1, replica_groups=mesh['z'=8,'y'=4,'core'=2,'xh'=2,'xl'=2] {'xh','xl','core'}, dimensions={0} | all-to-all | bytes 327680 | tf_op jit(solution)/shard_map/all_to_all | solution.py:358
  52.7 14.9 %shard_map.79 = (f32[32,16,128]{2,1,0:T(8,128)S(1)}, f32[2,16,128]{2,1,0:T(8,128)S(1)}, f32[2,16,128]{2,1,0:T(8,128)S(1)}) custom-call(f32[8,128]{1,0:T(8,128)S(1)} %get-tuple-element.60.safe_ref, f32[2,1,128]{2,1,0:T(1,128)S(1)} %get-tuple-element.61.mix_ref, f32[8,40,128]{2,1,0:T(8,128)S(1)} %all_to_all.25.got_ref, ...), custom_call_target="tpu_custom_call" | custom-call | tf_op jit(solution)/shard_map/pallas_call | solution.py:64
  67.6 14.3 %all_to_all.26.terms_ref = f32[32,16,128]{2,1,0:T(8,128)S(1)} all-to-all(f32[32,16,128]{2,1,0:T(8,128)S(1)} %get-tuple-element.66), channel_id=1, replica_groups=mesh['z'=8,'y'=4,'core'=2,'xh'=2,'xl'=2] {'z','y'}, dimensions={0} | all-to-all | bytes 524288 | tf_op jit(solution)/shard_map/all_to_all | solution.py:358
  81.9 12.5 %shard_map.80 = (f32[8,2,16,128]{3,2,1,0:T(8,128)S(1)}, f32[2,16,128]{2,1,0:T(8,128)S(1)}) custom-call(f32[8,128]{1,0:T(8,128)S(1)} %get-tuple-element.60.safe_ref, f32[32,16,128]{2,1,0:T(8,128)S(1)} %all_to_all.26.terms_ref, f32[2,16,128]{2,1,0:T(8,128)S(1)} %get-tuple-element.67.column_ref, f32[2048,2048]{1,0:T(8,128)S(1)} %get-tuple-element.63.gibbs_ref, ...), custom_call_target="tpu_custom_call" | custom-call | tf_op jit(solution)/shard_map/pallas_call | solution.py:64
  94.5 10.2 %all_to_all.27.got_ref = f32[8,2,16,128]{3,2,1,0:T(8,128)S(1)} all-to-all(f32[8,2,16,128]{3,2,1,0:T(8,128)S(1)} %get-tuple-element.68), channel_id=1, replica_groups=mesh['z'=8,'y'=4,'core'=2,'xh'=2,'xl'=2] {'xh','xl','core'}, dimensions={0} | all-to-all | bytes 262144 | tf_op jit(solution)/shard_map/all_to_all | solution.py:358
  104.6 15.1 %shard_map.81 = (f32[32,16,128]{2,1,0:T(8,128)S(1)}, f32[2,16,128]{2,1,0:T(8,128)S(1)}, f32[8,128]{1,0:T(8,128)S(1)}) custom-call(f32[8,128]{1,0:T(8,128)S(1)} %get-tuple-element.60.safe_ref, f32[2,1,128]{2,1,0:T(1,128)S(1)} %get-tuple-element.53.spot_ref, f32[2,1,128]{2,1,0:T(1,128)S(1)} %get-tuple-element.61.mix_ref, ...), custom_call_target="tpu_custom_call" | custom-call | tf_op jit(solution)/shard_map/pallas_call | solution.py:64
  119.8 14.8 %all_to_all.28.terms_ref = f32[32,16,128]{2,1,0:T(8,128)S(1)} all-to-all(f32[32,16,128]{2,1,0:T(8,128)S(1)} %get-tuple-element.71), channel_id=1, replica_groups=mesh['z'=8,'y'=4,'core'=2,'xh'=2,'xl'=2] {'z','y'}, dimensions={0} | all-to-all | bytes 524288 | tf_op jit(solution)/shard_map/all_to_all | solution.py:358
  134.6 3.4 %collective-permute-start.3 = (f32[32,128]{1,0:T(8,128)S(1)}, f32[32,128]{1,0:T(8,128)S(1)}, u32[]{:S(2)}, u32[]{:S(2)}) collective-permute-start(f32[32,128]{1,0:T(8,128)S(1)} %get-tuple-element.80), channel_id=1, source_target_pairs={{0,6},{2,4},{4,2},{6,0},{1,7},{3,5},{5,3},{7,1},{8,14},{10,12},{12... | collective-permute-start | bytes 49160 | tf_op jit(solution)/shard_map/ppermute | solution.py:362
  138.0 0.0 collective-permute-start.1
  138.0 2.0 %collective-permute-start.2 = (f32[32,128]{1,0:T(8,128)S(1)}, f32[32,128]{1,0:T(8,128)S(1)}, u32[]{:S(2)}, u32[]{:S(2)}) collective-permute-start(f32[32,128]{1,0:T(8,128)S(1)} %get-tuple-element.79), channel_id=1, source_target_pairs={{0,2},{2,0},{4,6},{6,4},{1,3},{3,1},{5,7},{7,5},{8,10},{10,8},{12,... | collective-permute-start | bytes 49160 | tf_op jit(solution)/shard_map/ppermute | solution.py:362
  140.0 0.6 broadcast_multiply_fusion
  140.6 1.5 %collective-permute-done.2 = f32[32,128]{1,0:T(8,128)S(1)} collective-permute-done((f32[32,128]{1,0:T(8,128)S(1)}, f32[32,128]{1,0:T(8,128)S(1)}, u32[]{:S(2)}, u32[]{:S(2)}) %collective-permute-start.2) | collective-permute-done | bytes 16416 | tf_op jit(solution)/shard_map/ppermute | solution.py:362
  142.1 0.0 collective-permute-done.3
  142.1 0.0 collective-permute-done.1
  142.1 0.6 fusion
  (5 shorter events, 0.1 us)
Async XLA Ops:
  0.6 19.5 %copy-start = (bf16[32,8192]{1,0:T(8,128)(2,1)S(1)}, bf16[32,8192]{1,0:T(8,128)(2,1)}, u32[]{:S(2)}) copy-start(bf16[32,8192]{1,0:T(8,128)(2,1)} %param.8) | copy-start | bytes 1572868
  0.6 0.7 copy-start.1
  2.2 28.5 %all-to-all-start = ((bf16[256,2,128]{2,1,0:T(2,128)(2,1)}), bf16[256,2,128]{2,1,0:T(2,128)(2,1)S(1)}, u32[]{:S(2)}, u32[]{:S(2)}) async-start(bf16[256,2,128]{2,1,0:T(2,128)(2,1)} %shard_map.76), calls=%async_computation | async-start | bytes 262144 | tf_op jit(solution)/shard_map/all_to_all | solution.py:358
  17.9 3.3 %collective-permute-start = (f32[1,8192]{1,0:T(1,128)}, f32[1,8192]{1,0:T(1,128)S(1)}, u32[]{:S(2)}, u32[]{:S(2)}) collective-permute-start(f32[1,8192]{1,0:T(1,128)} %pot_ref), channel_id=1, source_target_pairs={{0,4},{2,6},{4,0},{6,2},{1,5},{3,7},{5,1},{7,3},{8,12},{10,14},{12... | collective-permute-start | bytes 98312 | tf_op jit(solution)/shard_map/ppermute | solution.py:362
  134.6 7.5 %collective-permute-start.3 = (f32[32,128]{1,0:T(8,128)S(1)}, f32[32,128]{1,0:T(8,128)S(1)}, u32[]{:S(2)}, u32[]{:S(2)}) collective-permute-start(f32[32,128]{1,0:T(8,128)S(1)} %get-tuple-element.80), channel_id=1, source_target_pairs={{0,6},{2,4},{4,2},{6,0},{1,7},{3,5},{5,3},{7,1},{8,14},{10,12},{12... | collective-permute-start | bytes 49160 | tf_op jit(solution)/shard_map/ppermute | solution.py:362
  138.0 4.1 %collective-permute-start.1 = (f32[32,128]{1,0:T(8,128)S(1)}, f32[32,128]{1,0:T(8,128)S(1)}, u32[]{:S(2)}, u32[]{:S(2)}) collective-permute-start(f32[32,128]{1,0:T(8,128)S(1)} %get-tuple-element.80), channel_id=1, source_target_pairs={{0,4},{2,6},{4,0},{6,2},{1,5},{3,7},{5,1},{7,3},{8,12},{10,14},{12... | collective-permute-start | bytes 49160 | tf_op jit(solution)/shard_map/ppermute | solution.py:362
  138.0 4.1 %collective-permute-start.2 = (f32[32,128]{1,0:T(8,128)S(1)}, f32[32,128]{1,0:T(8,128)S(1)}, u32[]{:S(2)}, u32[]{:S(2)}) collective-permute-start(f32[32,128]{1,0:T(8,128)S(1)} %get-tuple-element.79), channel_id=1, source_target_pairs={{0,2},{2,0},{4,6},{6,4},{1,3},{3,1},{5,7},{7,5},{8,10},{10,8},{12,... | collective-permute-start | bytes 49160 | tf_op jit(solution)/shard_map/ppermute | solution.py:362

commit v7 on v6

--- a/solution.py
+++ b/solution.py
@@ -161,7 +161,7 @@
     n_lines = feat_ref.shape[0]
     per_row = n_cells // n_lines
     depth = width // per_row
-    rows_blk, cols_blk = 512, 512
+    rows_blk, cols_blk = 2048, 512
     feat = feat_ref[...]
     wide = feat.astype(F32)
     square = wide * wide
@@ -214,7 +214,7 @@
             for s in range(2):
                 out_ref[s, pl.ds(i, 1), :] = to_row(jnp.sum(sum_ref[s, at, :], axis=1, keepdims=True))
 
-        unrolled_loop(n_cells // LANE, 8, fold_block)
+        unrolled_loop(n_cells // LANE, 16, fold_block)
         out_ref[...] = overall(jnp.max, level_ref[...]) + jnp.log(out_ref[...])
 
     @pl.when(jnp.logical_not(safe))
@@ -270,7 +270,7 @@
                 for s in range(n_scen):
                     out_ref[s, pl.ds(i, 1), :] = to_row(jnp.sum(sums[s], axis=1, keepdims=True))
 
-            unrolled_loop(blocks_out, 8, cell_block)
+            unrolled_loop(blocks_out, 16, cell_block)
         else:
             sum_ref[...] = jnp.zeros_like(sum_ref)
 
@@ -284,7 +284,7 @@
                     for s in range(n_scen):
                         sum_ref[s, b] += jnp.sum((tile * columns[s]).reshape(LANE // 8, 8, LANE), axis=0)
 
-            unrolled_loop(blocks_in, 8, cell_block)
+            unrolled_loop(blocks_in, 16, cell_block)
             out_ref[...] = jnp.sum(sum_ref[...], axis=2)
         out_ref[...] = top + jnp.log(out_ref[...])
 

time: 143 us -> 143 us (level)
  no operation moved by 1% of the time
where the time goes in v7:
time: 143 us; the launch traced here: 142 us
  Pallas kernels  58.1 us (41%)
  blocking collectives  48 us (34%)
  starting transfers between devices  23.3 us (16%)
  waiting for transfers between devices  10.4 us (7%)
    pallas_call x7, Pallas kernels, call(): pl.pallas_call(kernel, out_shape=outs, in_specs=[HBM if k in apart else s...  58.1 us
    all_to_all x4, blocking collectives, exchange(): return lax.all_to_all(value, axes, split_axis=0, concat_axis=0, tiled=True)  48 us
    all_to_all x1, starting transfers between devices, exchange(): return lax.all_to_all(value, axes, split_axis=0, concat_axis=0, tiled=True)  15.6 us
    all_to_all x1, waiting for transfers between devices, exchange(): return lax.all_to_all(value, axes, split_axis=0, concat_axis=0, tiled=True)  7.92 us
    ppermute x4, starting transfers between devices, swapped(): return lax.ppermute(value, SWAP_GROUP, [(k, k ^ flip) for k in range(4)])  7.63 us
  transfers between devices with their start and end apart: 5, of which 3 were waited for; matrix products, arithmetic and copies ran while one was open for 0% of the time, Pallas kernels for 1%

profile of v7, /device:TPU:1, one launch (start us, length us, event | category | flops | bytes accessed | tf_op | source)
XLA Modules:
  0.0 142.5 jit_solution(2279222286531754743)
XLA Ops:
  0.6 0.0 copy-start
  0.6 0.0 copy-start.1
  0.7 0.7 copy-done.1
  1.4 0.9 shard_map.76
  2.2 15.6 %all-to-all-start = ((bf16[256,2,128]{2,1,0:T(2,128)(2,1)}), bf16[256,2,128]{2,1,0:T(2,128)(2,1)S(1)}, u32[]{:S(2)}, u32[]{:S(2)}) async-start(bf16[256,2,128]{2,1,0:T(2,128)(2,1)} %shard_map.76), calls=%async_computation | async-start | bytes 262144 | tf_op jit(solution)/shard_map/all_to_all | solution.py:358
  17.9 2.2 %collective-permute-start = (f32[1,8192]{1,0:T(1,128)}, f32[1,8192]{1,0:T(1,128)S(1)}, u32[]{:S(2)}, u32[]{:S(2)}) collective-permute-start(f32[1,8192]{1,0:T(1,128)} %pot_ref), channel_id=1, source_target_pairs={{0,4},{2,6},{4,0},{6,2},{1,5},{3,7},{5,1},{7,3},{8,12},{10,14},{12... | collective-permute-start | bytes 98312 | tf_op jit(solution)/shard_map/ppermute | solution.py:362
  20.1 0.0 copy-done
  20.1 0.1 pad_add_fusion.place_ref
  20.2 1.0 collective-permute-done.core_pot_ref
  21.2 1.6 %shard_map.77 = (bf16[256,2048]{1,0:T(8,128)(2,1)S(1)}, f32[16,128]{1,0:T(8,128)S(1)}, f32[8,128]{1,0:T(8,128)S(1)}, f32[2,16,128]{2,1,0:T(8,128)S(1)}, f32[2,16...) custom-call(s32[3]{0:T(128)S(1)} %pad_add_fusion.place_ref, ...), custom_call_target="tpu_custom_call" | custom-call | tf_op jit(solution)/shard_map/pallas_call | solution.py:64
  22.9 7.9 %all-to-all-done = bf16[256,2,128]{2,1,0:T(2,128)(2,1)S(1)} async-done(((bf16[256,2,128]{2,1,0:T(2,128)(2,1)}), bf16[256,2,128]{2,1,0:T(2,128)(2,1)S(1)}, u32[]{:S(2)}, u32[]{:S(2)}) %all-to-all-start) | async-done | bytes 131104 | tf_op jit(solution)/shard_map/all_to_all | solution.py:358
  30.8 13.1 %shard_map.78 = (f32[2048,2048]{1,0:T(8,128)S(1)}, bf16[2048,256]{1,0:T(8,128)(2,1)S(1)}, f32[16,128]{1,0:T(8,128)S(1)}, f32[8,128]{1,0:T(8,128)S(1)}, f32[8,40,128]{2,1,0:T(8,128)S(1)}) custom-call(bf16[256,256]{1,0:T(8,128)(2,1)S(1)} %bitcast.20, bf16[256,2048]{1,0:T(8,128)(2,1)S(1)} %get-tuple-element.55.sites_ref, ...), custom_call_target="tpu_custom_call" | custom-call | tf_op jit(solution)/shard_map/pallas_call | solution.py:64
  43.9 8.7 %all_to_all.25.got_ref = f32[8,40,128]{2,1,0:T(8,128)S(1)} all-to-all(f32[8,40,128]{2,1,0:T(8,128)S(1)} %get-tuple-element.62), channel_id=1, replica_groups=mesh['z'=8,'y'=4,'core'=2,'xh'=2,'xl'=2] {'xh','xl','core'}, dimensions={0} | all-to-all | bytes 327680 | tf_op jit(solution)/shard_map/all_to_all | solution.py:358
  52.6 14.9 %shard_map.79 = (f32[32,16,128]{2,1,0:T(8,128)S(1)}, f32[2,16,128]{2,1,0:T(8,128)S(1)}, f32[2,16,128]{2,1,0:T(8,128)S(1)}) custom-call(f32[8,128]{1,0:T(8,128)S(1)} %get-tuple-element.60.safe_ref, f32[2,1,128]{2,1,0:T(1,128)S(1)} %get-tuple-element.61.mix_ref, f32[8,40,128]{2,1,0:T(8,128)S(1)} %all_to_all.25.got_ref, ...), custom_call_target="tpu_custom_call" | custom-call | tf_op jit(solution)/shard_map/pallas_call | solution.py:64
  67.6 14.3 %all_to_all.26.terms_ref = f32[32,16,128]{2,1,0:T(8,128)S(1)} all-to-all(f32[32,16,128]{2,1,0:T(8,128)S(1)} %get-tuple-element.66), channel_id=1, replica_groups=mesh['z'=8,'y'=4,'core'=2,'xh'=2,'xl'=2] {'z','y'}, dimensions={0} | all-to-all | bytes 524288 | tf_op jit(solution)/shard_map/all_to_all | solution.py:358
  81.9 12.5 %shard_map.80 = (f32[8,2,16,128]{3,2,1,0:T(8,128)S(1)}, f32[2,16,128]{2,1,0:T(8,128)S(1)}) custom-call(f32[8,128]{1,0:T(8,128)S(1)} %get-tuple-element.60.safe_ref, f32[32,16,128]{2,1,0:T(8,128)S(1)} %all_to_all.26.terms_ref, f32[2,16,128]{2,1,0:T(8,128)S(1)} %get-tuple-element.67.column_ref, f32[2048,2048]{1,0:T(8,128)S(1)} %get-tuple-element.63.gibbs_ref, ...), custom_call_target="tpu_custom_call" | custom-call | tf_op jit(solution)/shard_map/pallas_call | solution.py:64
  94.4 10.2 %all_to_all.27.got_ref = f32[8,2,16,128]{3,2,1,0:T(8,128)S(1)} all-to-all(f32[8,2,16,128]{3,2,1,0:T(8,128)S(1)} %get-tuple-element.68), channel_id=1, replica_groups=mesh['z'=8,'y'=4,'core'=2,'xh'=2,'xl'=2] {'xh','xl','core'}, dimensions={0} | all-to-all | bytes 262144 | tf_op jit(solution)/shard_map/all_to_all | solution.py:358
  104.6 14.9 %shard_map.81 = (f32[32,16,128]{2,1,0:T(8,128)S(1)}, f32[2,16,128]{2,1,0:T(8,128)S(1)}, f32[8,128]{1,0:T(8,128)S(1)}) custom-call(f32[8,128]{1,0:T(8,128)S(1)} %get-tuple-element.60.safe_ref, f32[2,1,128]{2,1,0:T(1,128)S(1)} %get-tuple-element.53.spot_ref, f32[2,1,128]{2,1,0:T(1,128)S(1)} %get-tuple-element.61.mix_ref, ...), custom_call_target="tpu_custom_call" | custom-call | tf_op jit(solution)/shard_map/pallas_call | solution.py:64
  119.5 14.8 %all_to_all.28.terms_ref = f32[32,16,128]{2,1,0:T(8,128)S(1)} all-to-all(f32[32,16,128]{2,1,0:T(8,128)S(1)} %get-tuple-element.71), channel_id=1, replica_groups=mesh['z'=8,'y'=4,'core'=2,'xh'=2,'xl'=2] {'z','y'}, dimensions={0} | all-to-all | bytes 524288 | tf_op jit(solution)/shard_map/all_to_all | solution.py:358
  134.4 3.4 %collective-permute-start.3 = (f32[32,128]{1,0:T(8,128)S(1)}, f32[32,128]{1,0:T(8,128)S(1)}, u32[]{:S(2)}, u32[]{:S(2)}) collective-permute-start(f32[32,128]{1,0:T(8,128)S(1)} %get-tuple-element.80), channel_id=1, source_target_pairs={{0,6},{2,4},{4,2},{6,0},{1,7},{3,5},{5,3},{7,1},{8,14},{10,12},{12... | collective-permute-start | bytes 49160 | tf_op jit(solution)/shard_map/ppermute | solution.py:362
  137.7 0.0 collective-permute-start.1
  137.7 2.0 %collective-permute-start.2 = (f32[32,128]{1,0:T(8,128)S(1)}, f32[32,128]{1,0:T(8,128)S(1)}, u32[]{:S(2)}, u32[]{:S(2)}) collective-permute-start(f32[32,128]{1,0:T(8,128)S(1)} %get-tuple-element.79), channel_id=1, source_target_pairs={{0,2},{2,0},{4,6},{6,4},{1,3},{3,1},{5,7},{7,5},{8,10},{10,8},{12,... | collective-permute-start | bytes 49160 | tf_op jit(solution)/shard_map/ppermute | solution.py:362
  139.8 0.6 broadcast_multiply_fusion
  140.3 1.5 %collective-permute-done.2 = f32[32,128]{1,0:T(8,128)S(1)} collective-permute-done((f32[32,128]{1,0:T(8,128)S(1)}, f32[32,128]{1,0:T(8,128)S(1)}, u32[]{:S(2)}, u32[]{:S(2)}) %collective-permute-start.2) | collective-permute-done | bytes 16416 | tf_op jit(solution)/shard_map/ppermute | solution.py:362
  141.8 0.0 collective-permute-done.3
  141.8 0.0 collective-permute-done.1
  141.9 0.6 fusion
  (5 shorter events, 0.1 us)
Async XLA Ops:
  0.6 19.5 %copy-start = (bf16[32,8192]{1,0:T(8,128)(2,1)S(1)}, bf16[32,8192]{1,0:T(8,128)(2,1)}, u32[]{:S(2)}) copy-start(bf16[32,8192]{1,0:T(8,128)(2,1)} %param.8) | copy-start | bytes 1572868
  0.6 0.7 copy-start.1
  2.2 28.5 %all-to-all-start = ((bf16[256,2,128]{2,1,0:T(2,128)(2,1)}), bf16[256,2,128]{2,1,0:T(2,128)(2,1)S(1)}, u32[]{:S(2)}, u32[]{:S(2)}) async-start(bf16[256,2,128]{2,1,0:T(2,128)(2,1)} %shard_map.76), calls=%async_computation | async-start | bytes 262144 | tf_op jit(solution)/shard_map/all_to_all | solution.py:358
  17.9 3.3 %collective-permute-start = (f32[1,8192]{1,0:T(1,128)}, f32[1,8192]{1,0:T(1,128)S(1)}, u32[]{:S(2)}, u32[]{:S(2)}) collective-permute-start(f32[1,8192]{1,0:T(1,128)} %pot_ref), channel_id=1, source_target_pairs={{0,4},{2,6},{4,0},{6,2},{1,5},{3,7},{5,1},{7,3},{8,12},{10,14},{12... | collective-permute-start | bytes 98312 | tf_op jit(solution)/shard_map/ppermute | solution.py:362
  134.4 7.5 %collective-permute-start.3 = (f32[32,128]{1,0:T(8,128)S(1)}, f32[32,128]{1,0:T(8,128)S(1)}, u32[]{:S(2)}, u32[]{:S(2)}) collective-permute-start(f32[32,128]{1,0:T(8,128)S(1)} %get-tuple-element.80), channel_id=1, source_target_pairs={{0,6},{2,4},{4,2},{6,0},{1,7},{3,5},{5,3},{7,1},{8,14},{10,12},{12... | collective-permute-start | bytes 49160 | tf_op jit(solution)/shard_map/ppermute | solution.py:362
  137.7 4.1 %collective-permute-start.1 = (f32[32,128]{1,0:T(8,128)S(1)}, f32[32,128]{1,0:T(8,128)S(1)}, u32[]{:S(2)}, u32[]{:S(2)}) collective-permute-start(f32[32,128]{1,0:T(8,128)S(1)} %get-tuple-element.80), channel_id=1, source_target_pairs={{0,4},{2,6},{4,0},{6,2},{1,5},{3,7},{5,1},{7,3},{8,12},{10,14},{12... | collective-permute-start | bytes 49160 | tf_op jit(solution)/shard_map/ppermute | solution.py:362
  137.7 4.1 %collective-permute-start.2 = (f32[32,128]{1,0:T(8,128)S(1)}, f32[32,128]{1,0:T(8,128)S(1)}, u32[]{:S(2)}, u32[]{:S(2)}) collective-permute-start(f32[32,128]{1,0:T(8,128)S(1)} %get-tuple-element.79), channel_id=1, source_target_pairs={{0,2},{2,0},{4,6},{6,4},{1,3},{3,1},{5,7},{7,5},{8,10},{10,8},{12,... | collective-permute-start | bytes 49160 | tf_op jit(solution)/shard_map/ppermute | solution.py:362
